TPU v7x, 32 devices: a whole 2x2x4 slice. The times are simulated.
32 devices in a mesh: slab: 8 (over z, x), yz: 4 (over y, core).
Axes of the slice: x: 2, y: 2, z: 4, core: 2. Of those that a mesh axis runs over, the one named last changes fastest.
Arguments:
- embeddings: bfloat16 [512, 25, 128], P(('slab', 'yz')), may hold values from -6 to 6
- neighbours: int32 [16384], P(('slab', 'yz')), may hold values from 0 to 127
- valid: int32 [16384], P(('slab', 'yz')), may hold values 0 or 1
- azimuth: float32 [16384], P(('slab', 'yz')), may hold values from -3.140625 to 3.140625
- polar: float32 [16384], P(('slab', 'yz')), may hold values from 0 to 3.14159
- distance: float32 [16384], P(('slab', 'yz')), may hold values from 0.9 to 5
- send_low: int32 [256], P(('slab', 'yz')), may hold values from 0 to 15
- send_high: int32 [256], P(('slab', 'yz')), may hold values from 0 to 15
- w_zero: bfloat16 [2, 640, 640], replicated, may hold values from -0.25 to 0.25
- w_one_re: bfloat16 [2, 512, 512], replicated, may hold values from -0.25 to 0.25
- w_one_im: bfloat16 [2, 512, 512], replicated, may hold values from -0.25 to 0.25
- w_two_re: bfloat16 [2, 384, 384], replicated, may hold values from -0.3125 to 0.3125
- w_two_im: bfloat16 [2, 384, 384], replicated, may hold values from -0.3125 to 0.3125
- radial_weight: float32 [2, 8, 128], replicated, may hold values from -2 to 2
- readout: float32 [128], replicated, may hold values from -0.5 to 0.5
Outputs:
- updated: bfloat16 [512, 25, 128], P(('slab', 'yz'))
- forces: float32 [3, 512], P(None, ('slab', 'yz'))
All inputs are finite; a program needn't handle non-finite values. No bound on the sum of `valid` on one device may be relied on, other than what follows from the above.
Results may differ from a plain program's by a relative error of at most 0.0043.
Values may be sent and summed in bfloat16 or wider, within the bound.
No kernel may reach another device: no remote copies, remote signals or barrier semaphores. Data moves between devices by JAX's collectives and lax.ppermute only.
A program may use at most 64 MiB of HBM per device.

v0:
```python
import math

import jax
import jax.numpy as jnp
from jax import lax
from jax.sharding import PartitionSpec as P

NEIGHB = 32
LAYERS = 2


HIGHEST = lax.Precision.HIGHEST


def from_behind(block, axis, distance):
    devices = range(lax.axis_size(axis))
    route = [((i - distance) % len(devices), i) for i in devices]
    return lax.ppermute(block, axis, route)


def slot_index(degree, azimuth_order):
    return degree * degree + degree + azimuth_order


def radial_scale(distance, radial_weight):
    centers = 1.0 + 0.5 * jnp.arange(8, dtype=jnp.float32)
    basis_values = jnp.exp(-jnp.square((distance[:, None] - centers[None, :]) / 0.5))
    return jax.nn.silu(jnp.dot(basis_values, radial_weight, precision=HIGHEST))


def slot_groups(degrees):
    zero_slots = [slot_index(degree, 0) for degree in range(degrees)]
    groups = [zero_slots]
    for azimuth_order in (1, 2):
        groups.append(
            [slot_index(degree, azimuth_order) for degree in range(azimuth_order, degrees)]
        )
        groups.append(
            [slot_index(degree, -azimuth_order) for degree in range(azimuth_order, degrees)]
        )
    return groups


def grouped_rows(rows, degrees):
    order = [coeff_slot for group in slot_groups(degrees) for coeff_slot in group]
    return jnp.concatenate([rows[:, coeff_slot] for coeff_slot in order], axis=1)


def convolve(
    features,
    degrees,
    channel_count,
    azimuth,
    distance,
    valid,
    w_zero,
    w_one_re,
    w_one_im,
    w_two_re,
    w_two_im,
    radial_weight,
):
    edge_count = features.shape[0]
    atom_count = edge_count // NEIGHB
    radial = radial_scale(distance, radial_weight) * valid.astype(jnp.float32)[:, None]
    radial_rows = radial[:, None, :]
    groups = slot_groups(degrees)
    bounds = []
    offset = 0
    for group in groups:
        bounds.append((offset, offset + len(group) * channel_count))
        offset += len(group) * channel_count
    results = [None] * (degrees * degrees)
    zero_in = features[:, bounds[0][0] : bounds[0][1]]
    zero_out = (
        jnp.dot(zero_in, w_zero, preferred_element_type=jnp.float32).reshape(
            edge_count, degrees, channel_count
        )
        * radial_rows
    )
    zero_sum = zero_out.reshape(atom_count, NEIGHB, degrees, channel_count).sum(axis=1)
    for position, coeff_slot in enumerate(groups[0]):
        results[coeff_slot] = zero_sum[:, position]
    for index_pair, azimuth_order, real_part, imag_part in (
        (1, 1, w_one_re, w_one_im),
        (3, 2, w_two_re, w_two_im),
    ):
        plus_slots = groups[index_pair]
        minus_slots = groups[index_pair + 1]
        plus_part = features[:, bounds[index_pair][0] : bounds[index_pair][1]].astype(jnp.float32)
        minus_part = features[:, bounds[index_pair + 1][0] : bounds[index_pair + 1][1]].astype(
            jnp.float32
        )
        cosine = jnp.cos(azimuth_order * azimuth)[:, None]
        sine = jnp.sin(azimuth_order * azimuth)[:, None]
        turned_plus = (cosine * plus_part + sine * minus_part).astype(jnp.bfloat16)
        turned_minus = (cosine * minus_part - sine * plus_part).astype(jnp.bfloat16)
        count = len(plus_slots)
        out_plus = (
            jnp.dot(turned_plus, real_part, preferred_element_type=jnp.float32)
            - jnp.dot(turned_minus, imag_part, preferred_element_type=jnp.float32)
        ).reshape(edge_count, count, channel_count) * radial_rows
        out_minus = (
            jnp.dot(turned_plus, imag_part, preferred_element_type=jnp.float32)
            + jnp.dot(turned_minus, real_part, preferred_element_type=jnp.float32)
        ).reshape(edge_count, count, channel_count) * radial_rows
        cos_rows = cosine[:, :, None]
        sin_rows = sine[:, :, None]
        back_plus = (
            (cos_rows * out_plus - sin_rows * out_minus)
            .reshape(atom_count, NEIGHB, count, channel_count)
            .sum(axis=1)
        )
        back_minus = (
            (sin_rows * out_plus + cos_rows * out_minus)
            .reshape(atom_count, NEIGHB, count, channel_count)
            .sum(axis=1)
        )
        for position, coeff_slot in enumerate(plus_slots):
            results[coeff_slot] = back_plus[:, position]
        for position, coeff_slot in enumerate(minus_slots):
            results[coeff_slot] = back_minus[:, position]
    blank = jnp.zeros((atom_count, channel_count), jnp.float32)
    summed = jnp.stack(
        [blank if entry_value is None else entry_value for entry_value in results], axis=1
    )
    return (summed, zero_out[:, 0])


def body(
    embeddings,
    neighbours,
    valid,
    azimuth,
    polar,
    distance,
    send_low,
    send_high,
    w_zero,
    w_one_re,
    w_one_im,
    w_two_re,
    w_two_im,
    radial_weight,
    readout,
):
    atom_rows = embeddings.shape[0]
    coeffs = embeddings.shape[1]
    channel_count = embeddings.shape[2]
    degrees = math.isqrt(coeffs)
    ghost_rows = send_low.shape[0]
    slab_devices = lax.axis_size("yz")
    table_rows = slab_devices * (atom_rows + 2 * ghost_rows)
    current = embeddings
    scalar_out = None
    for layer_index in range(LAYERS):
        outgoing = current
        low_piece = outgoing[send_low]
        high_piece = outgoing[send_high]
        below_one = from_behind(high_piece, "slab", 1)
        above_one = from_behind(low_piece, "slab", -1)
        own_rows, below_rows, above_rows = (
            lax.all_gather(outgoing, "yz", axis=0, tiled=True),
            lax.all_gather(below_one, "yz", axis=0, tiled=True),
            lax.all_gather(above_one, "yz", axis=0, tiled=True),
        )
        table = jnp.concatenate([own_rows, below_rows, above_rows], axis=0)
        table = grouped_rows(table, degrees)
        summed, scalar_out = convolve(
            table[neighbours],
            degrees,
            channel_count,
            azimuth,
            distance,
            valid,
            w_zero[layer_index],
            w_one_re[layer_index],
            w_one_im[layer_index],
            w_two_re[layer_index],
            w_two_im[layer_index],
            radial_weight[layer_index],
        )
        current = (current.astype(jnp.float32) + 0.18 * summed).astype(jnp.bfloat16)
    strength = 0.125 * jnp.dot(scalar_out, readout, precision=HIGHEST)
    direction = jnp.stack(
        [jnp.sin(polar) * jnp.cos(azimuth), jnp.sin(polar) * jnp.sin(azimuth), jnp.cos(polar)],
        axis=0,
    )
    pull = direction * strength[None, :]
    own_force = pull.reshape(3, -1, NEIGHB).sum(axis=-1)
    onehot = (neighbours[:, None] == jnp.arange(table_rows, dtype=jnp.int32)[None, :]).astype(
        jnp.float32
    )
    table_force = -jnp.dot(pull, onehot, precision=HIGHEST)
    own_count = slab_devices * atom_rows
    ghost_count = slab_devices * ghost_rows
    below_force = table_force[:, own_count : own_count + ghost_count]
    above_force = table_force[:, own_count + ghost_count :]
    below_back = from_behind(below_force, "slab", -1)
    above_back = from_behind(above_force, "slab", 1)
    own_sum, high_sum, low_sum = (
        lax.psum_scatter(table_force[:, :own_count], "yz", scatter_dimension=1, tiled=True),
        lax.psum_scatter(below_back, "yz", scatter_dimension=1, tiled=True),
        lax.psum_scatter(above_back, "yz", scatter_dimension=1, tiled=True),
    )
    atom_ids = jnp.arange(atom_rows, dtype=jnp.int32)
    high_hot = (send_high[:, None] == atom_ids[None, :]).astype(jnp.float32)
    low_hot = (send_low[:, None] == atom_ids[None, :]).astype(jnp.float32)
    forces = (
        own_force
        + own_sum
        + jnp.dot(high_sum, high_hot, precision=HIGHEST)
        + jnp.dot(low_sum, low_hot, precision=HIGHEST)
    )
    return (current, forces)


def solution(mesh):
    in_specs = (
        P(("slab", "yz"), None, None),
        P(("slab", "yz")),
        P(("slab", "yz")),
        P(("slab", "yz")),
        P(("slab", "yz")),
        P(("slab", "yz")),
        P(("slab", "yz")),
        P(("slab", "yz")),
        P(),
        P(),
        P(),
        P(),
        P(),
        P(),
        P(),
    )
    out_specs = (P(("slab", "yz"), None, None), P(None, ("slab", "yz")))
    return jax.shard_map(body, mesh=mesh, in_specs=in_specs, out_specs=out_specs, check_vma=False)
```

profile of v0, /device:TPU:0, one launch (start us, length us, event | category | flops | bytes accessed | tf_op | source)
XLA Modules:
  0.0 160.3 jit_solution(2242063938275191311)
XLA Ops:
  8.6 1.7 %gather_fusion = bf16[8,25,128]{2,0,1:T(8,128)(2,1)S(1)} fusion(bf16[16,25,128]{2,0,1:T(8,128)(2,1)} %param.15, s32[1024]{0:T(1024)S(1)} %get-tuple-element.111), kind=kCustom, calls=%fused_computation | custom fusion | bytes 102432 | tf_op jit(solution)/shard_map/gather | solution.py:159
  10.4 3.0 %collective-permute-start = (bf16[8,25,128]{2,0,1:T(8,128)(2,1)S(1)}, bf16[8,25,128]{2,0,1:T(8,128)(2,1)}, u32[]{:S(2)}, u32[]{:S(2)}) collective-permute-start(bf16[8,25,128]{2,0,1:T(8,128)(2,1)S(1)} %gather_fusion), channel_id=1, source_target_pairs={{28,0},{0,4},{4,8},{8,12},{12,16},{16,20},{20,24},{24,28},{29,1},{... | collective-permute-start | bytes 153608 | tf_op jit(solution)/shard_map/ppermute | solution.py:18
  13.4 1.6 %gather_fusion.1 = bf16[8,25,128]{2,0,1:T(8,128)(2,1)S(1)} fusion(bf16[16,25,128]{2,0,1:T(8,128)(2,1)} %param.15, s32[1024]{0:T(1024)S(1)} %get-tuple-element.110), kind=kCustom, calls=%fused_computation.1 | custom fusion | bytes 102432 | tf_op jit(solution)/shard_map/gather | solution.py:158
  15.0 3.1 %collective-permute-start.1 = (bf16[8,25,128]{2,0,1:T(8,128)(2,1)S(1)}, bf16[8,25,128]{2,0,1:T(8,128)(2,1)S(1)}, u32[]{:S(2)}, u32[]{:S(2)}) collective-permute-start(bf16[8,25,128]{2,0,1:T(8,128)(2,1)S(1)} %gather_fusion.1), channel_id=1, source_target_pairs={{4,0},{8,4},{12,8},{16,12},{20,16},{24,20},{28,24},{0,28},{5,1},{9... | collective-permute-start | bytes 153608 | tf_op jit(solution)/shard_map/ppermute | solution.py:18
  18.1 6.9 %all_gather.18 = bf16[64,25,128]{2,0,1:T(8,128)(2,1)S(1)} all-gather(bf16[16,25,128]{2,0,1:T(8,128)(2,1)} %param.15), channel_id=1, replica_groups=mesh['slab'=8,'yz'=4] {'yz'}, dimensions={0}, use_global_device_ids=true | all-gather | bytes 512000 | tf_op jit(solution)/shard_map/all_gather | solution.py:163
  25.7 2.1 %multiply_multiply_fusion.1 = f32[512,128]{1,0:T(8,128)} fusion(f32[512]{0:T(512)S(1)} %convert_element_type.68, f32[8]{0:T(128)S(1)} %multiply_add_fusion, f32[512]{0:T(512)} %param.20, f32[2,8,128]{2,1,0:T(8,128)} %param.28), kind=kOutput, calls=%fused_computation.103 | convolution fusion | flops 6635520 | bytes 270368 | tf_op jit(solution)/shard_map/dot_general | solution.py:28
  36.8 5.9 %all_gather.19 = bf16[32,25,128]{2,0,1:T(8,128)(2,1)S(1)} all-gather(bf16[8,25,128]{2,0,1:T(8,128)(2,1)} %collective-permute-done), channel_id=1, replica_groups=mesh['slab'=8,'yz'=4] {'yz'}, dimensions={0}, use_global_device_ids=true | all-gather | bytes 256000 | tf_op jit(solution)/shard_map/all_gather | solution.py:164
  42.7 5.8 %all_gather.20 = bf16[32,25,128]{2,0,1:T(8,128)(2,1)S(1)} all-gather(bf16[8,25,128]{2,0,1:T(8,128)(2,1)S(1)} %collective-permute-done.1), channel_id=1, replica_groups=mesh['slab'=8,'yz'=4] {'yz'}, dimensions={0}, use_global_device_ids=true | all-gather | bytes 256000 | tf_op jit(solution)/shard_map/all_gather | solution.py:165
  48.9 2.6 %gather_fusion.2 = bf16[512,2432]{1,0:T(8,128)(2,1)S(1)} fusion(bf16[128,2432]{1,0:T(8,128)(2,1)S(1)} %constant_dynamic-update-slice_fusion.3, s32[1024]{0:T(1024)S(1)} %pad_clamp_fusion), kind=kCustom, calls=%fused_computation.2 | custom fusion | bytes 4982784 | tf_op jit(solution)/shard_map/gather | solution.py:170
  56.2 1.7 %convolution_add_fusion.3 = f32[512,384]{1,0:T(8,128)S(1)} fusion(f32[512,384]{1,0:T(8,128)} %fusion.43, bf16[2,384,384]{2,1,0:T(8,128)(2,1)} %param.26, f32[512]{0:T(512)S(1)} %get-tuple-element.106, f32[512]{0:T(512)S(1)} %get-tuple-element.104, bf16[512,2432]{1,0:T(8,128)(2,1)S(1)} %gather_fusion.2), kind=kOutput, calls=%fused_computation.24 | convolution fusion | flops 152371200 | bytes 2658304 | tf_op jit(solution)/shard_map/dot_general | solution.py:105
  59.2 2.6 %subtract_reduce_fusion.2 = (f32[16,3,128]{2,1,0:T(4,128)S(1)}, f32[16,3,128]{2,1,0:T(4,128)S(1)}) fusion(f32[16,32,3,128]{3,2,1,0:T(4,128)} %reshape.135, f32[16,32,3,128]{3,2,1,0:T(4,128)} %reshape.134, f32[16,32]{1,0:T(8,128)S(1)} %mul.428, f32[16,32,128]{2,1,0:T(8,128)} %bitcast.261, f32[16,32]{1,0:T(8,128)S(1)} %mul.417), kind=kLoop, calls=%fused_computation.41 | loop fusion | flops 1953792 | bytes 1888256 | tf_op jit(solution)/shard_map/reduce_sum | solution.py:112
  65.6 2.5 %reshape.132 = f32[16,32,4,128]{3,2,1,0:T(4,128)} reshape(f32[512,512]{1,0:T(8,128)} %convolution_subtract_fusion.1) | data formatting | bytes 2097152 | tf_op jit(solution)/shard_map/reshape | solution.py:102
  68.1 3.0 %convolution_add_fusion.1 = f32[512,512]{1,0:T(8,128)} fusion(f32[512,512]{1,0:T(8,128)} %fusion.23, bf16[2,512,512]{2,1,0:T(8,128)(2,1)} %param.24, f32[512]{0:T(512)S(1)} %get-tuple-element.105, f32[512]{0:T(512)S(1)} %get-tuple-element.107, bf16[512,2432]{1,0:T(8,128)(2,1)S(1)} %gather_fusion.2), kind=kOutput, calls=%fused_computation.10 | convolution fusion | flops 270270464 | bytes 3674112 | tf_op jit(solution)/shard_map/dot_general | solution.py:105
  71.1 2.5 %reshape.133 = f32[16,32,4,128]{3,2,1,0:T(4,128)} reshape(f32[512,512]{1,0:T(8,128)} %convolution_add_fusion.1) | data formatting | bytes 2097152 | tf_op jit(solution)/shard_map/reshape | solution.py:106
  73.7 2.5 %subtract_reduce_fusion.3 = (f32[16,4,128]{2,1,0:T(4,128)S(1)}, f32[16,4,128]{2,1,0:T(4,128)S(1)}) fusion(f32[16,32,4,128]{3,2,1,0:T(4,128)} %reshape.133, f32[16,32,4,128]{3,2,1,0:T(4,128)} %reshape.132, f32[16,32]{1,0:T(8,128)S(1)} %mul.410, f32[16,32,128]{2,1,0:T(8,128)S(1)} %bitcast.262, f32[16,32]{1,0:T(8,128)S(1)} %mul.398), kind=kLoop, calls=%fused_computation.43 | loop fusion | flops 2605056 | bytes 2428928 | tf_op jit(solution)/shard_map/reduce_sum | solution.py:112
  79.0 6.7 %all_gather.21 = bf16[64,25,128]{2,0,1:T(8,128)(2,1)S(1)} all-gather(bf16[16,25,128]{2,0,1:T(8,128)(2,1)S(1)} %copy.311), channel_id=1, replica_groups=mesh['slab'=8,'yz'=4] {'yz'}, dimensions={0}, use_global_device_ids=true | all-gather | bytes 512000 | tf_op jit(solution)/shard_map/all_gather | solution.py:163
  86.4 4.8 %collective-permute-start.3 = (bf16[8,25,128]{2,1,0:T(8,128)(2,1)S(1)}, bf16[8,25,128]{2,1,0:T(8,128)(2,1)S(1)}, u32[]{:S(2)}, u32[]{:S(2)}) collective-permute-start(bf16[8,25,128]{2,1,0:T(8,128)(2,1)S(1)} %gather_fusion.4), channel_id=1, source_target_pairs={{4,0},{8,4},{12,8},{16,12},{20,16},{24,20},{28,24},{0,28},{5,1},{9... | collective-permute-start | bytes 153608 | tf_op jit(solution)/shard_map/ppermute | solution.py:18
  92.8 5.7 %all_gather.22 = bf16[32,25,128]{2,0,1:T(8,128)(2,1)S(1)} all-gather(bf16[8,25,128]{2,0,1:T(8,128)(2,1)S(1)} %copy.312), channel_id=1, replica_groups=mesh['slab'=8,'yz'=4] {'yz'}, dimensions={0}, use_global_device_ids=true | all-gather | bytes 256000 | tf_op jit(solution)/shard_map/all_gather | solution.py:164
  98.5 5.9 %all_gather.23 = bf16[32,25,128]{2,0,1:T(8,128)(2,1)S(1)} all-gather(bf16[8,25,128]{2,0,1:T(8,128)(2,1)S(1)} %copy.313), channel_id=1, replica_groups=mesh['slab'=8,'yz'=4] {'yz'}, dimensions={0}, use_global_device_ids=true | all-gather | bytes 256000 | tf_op jit(solution)/shard_map/all_gather | solution.py:165
  104.8 2.6 %gather_fusion.5 = bf16[512,2432]{1,0:T(8,128)(2,1)S(1)} fusion(bf16[128,2432]{1,0:T(8,128)(2,1)S(1)} %constant_dynamic-update-slice_fusion.25, s32[1024]{0:T(1024)S(1)} %copy-done.41), kind=kCustom, calls=%fused_computation.5 | custom fusion | bytes 4982784 | tf_op jit(solution)/shard_map/gather | solution.py:170
  112.0 1.6 fusion.17
  117.0 2.0 %collective-permute-start.5 = (f32[3,32]{1,0:T(4,128)}, f32[3,32]{1,0:T(4,128)}, u32[]{:S(2)}, u32[]{:S(2)}) collective-permute-start(f32[3,32]{1,0:T(4,128)} %get-tuple-element.99), channel_id=1, source_target_pairs={{28,0},{0,4},{4,8},{8,12},{12,16},{16,20},{20,24},{24,28},{29,1},{... | collective-permute-start | bytes 1160 | tf_op jit(solution)/shard_map/ppermute | solution.py:18
  119.8 2.3 %convolution_subtract_fusion.2 = f32[512,384]{1,0:T(8,128)} fusion(f32[512,384]{1,0:T(8,128)S(1)} %fusion.41, bf16[2,384,384]{2,1,0:T(8,128)(2,1)} %param.27, f32[512]{0:T(512)S(1)} %get-tuple-element.106, f32[512]{0:T(512)S(1)} %get-tuple-element.104, bf16[512,2432]{1,0:T(8,128)(2,1)S(1)} %gather_fusion.5), kind=kOutput, calls=%fused_computation.23 | convolution fusion | flops 152371200 | bytes 2658304 | tf_op jit(solution)/shard_map/dot_general | solution.py:101
  123.6 2.6 %convolution_add_fusion.2 = f32[512,384]{1,0:T(8,128)} fusion(f32[512,384]{1,0:T(8,128)} %fusion.37, bf16[2,384,384]{2,1,0:T(8,128)(2,1)} %param.26, f32[512]{0:T(512)} %copy-done.21, f32[512]{0:T(512)S(1)} %get-tuple-element.104, bf16[512,2432]{1,0:T(8,128)(2,1)S(1)} %gather_fusion.5), kind=kOutput, calls=%fused_computation.22 | convolution fusion | flops 152371200 | bytes 2658304 | tf_op jit(solution)/shard_map/dot_general | solution.py:105
  126.2 2.3 %reshape.140 = f32[16,32,3,128]{3,2,1,0:T(4,128)} reshape(f32[512,384]{1,0:T(8,128)} %convolution_add_fusion.2) | data formatting | bytes 1572864 | tf_op jit(solution)/shard_map/reshape | solution.py:106
  128.5 3.3 %subtract_reduce_fusion = (f32[16,3,128]{2,1,0:T(4,128)S(1)}, f32[16,3,128]{2,1,0:T(4,128)S(1)}) fusion(f32[16,32,3,128]{3,2,1,0:T(4,128)} %reshape.140, f32[16,32,3,128]{3,2,1,0:T(4,128)S(1)} %reshape.139, f32[16,32,128]{2,1,0:T(8,128)} %bitcast.259, f32[16,32]{1,0:T(8,128)} %copy-done.29, f32[16,32]{1,0:T(8,128)} %copy-done.28), kind=kLoop, calls=%fused_computation.37 | loop fusion | flops 1953792 | bytes 1888256 | tf_op jit(solution)/shard_map/reduce_sum | solution.py:112
  133.0 1.6 convolution_subtract_fusion
  134.5 1.6 reshape.137
  136.1 3.0 %convolution_add_fusion = f32[512,512]{1,0:T(8,128)} fusion(f32[512,512]{1,0:T(8,128)} %fusion.17, bf16[2,512,512]{2,1,0:T(8,128)(2,1)} %param.24, f32[512]{0:T(512)S(1)} %copy-done.23, f32[512]{0:T(512)} %copy-done.24, bf16[512,2432]{1,0:T(8,128)(2,1)S(1)} %gather_fusion.5), kind=kOutput, calls=%fused_computation.8 | convolution fusion | flops 270270464 | bytes 3674112 | tf_op jit(solution)/shard_map/dot_general | solution.py:105
  139.2 1.7 %reshape.138 = f32[16,32,4,128]{3,2,1,0:T(4,128)S(1)} reshape(f32[512,512]{1,0:T(8,128)} %convolution_add_fusion) | data formatting | bytes 2097152 | tf_op jit(solution)/shard_map/reshape | solution.py:106
  140.9 2.8 %subtract_reduce_fusion.1 = (f32[16,4,128]{2,1,0:T(4,128)S(1)}, f32[16,4,128]{2,1,0:T(4,128)S(1)}) fusion(f32[16,32,4,128]{3,2,1,0:T(4,128)S(1)} %reshape.138, f32[16,32,4,128]{3,2,1,0:T(4,128)S(1)} %reshape.137, f32[16,32,128]{2,1,0:T(8,128)} %bitcast.260, f32[16,32]{1,0:T(8,128)} %copy-done.27, f32[16,32]{1,0:T(8,128)} %copy-done.26), kind=kLoop, calls=%fused_computation.39 | loop fusion | flops 2605056 | bytes 2428928 | tf_op jit(solution)/shard_map/reduce_sum | solution.py:112
  145.2 6.5 %all-reduce.2 = (f32[3,32]{1,0:T(4,128)S(1)}, f32[3,32]{1,0:T(4,128)S(1)}) all-reduce(f32[3,32]{1,0:T(4,128)} %collective-permute-done.5, f32[3,32]{1,0:T(4,128)} %collective-permute-done.4), channel_id=4, replica_groups=mesh['slab'=8,'yz'=4] {'yz'}, use_global_device_ids=true, to_apply=%region_13.14.clone | all-reduce | flops 192 | bytes 1536
  (243 shorter events, 40.0 us)
Async XLA Ops:
  7.2 107.9 %copy-start = (f32[128]{0:T(128)S(1)}, f32[128]{0:T(128)}, u32[]{:S(2)}) copy-start(f32[128]{0:T(128)} %param.29) | copy-start | bytes 1540
  7.2 20.6 %copy-start.55 = (f32[512]{0:T(512)S(1)}, f32[512]{0:T(512)}, u32[]{:S(2)}) copy-start(f32[512]{0:T(512)} %param.20) | copy-start | bytes 6148
  7.2 20.6 %copy-start.54 = (f32[2,8,128]{2,1,0:T(8,128)S(1)}, f32[2,8,128]{2,1,0:T(8,128)}, u32[]{:S(2)}) copy-start(f32[2,8,128]{2,1,0:T(8,128)} %param.28) | copy-start | bytes 24580
  7.2 144.7 %reduce-scatter.6.cloned.1.call-start = ((), (), s32[]{:S(2)}) async-start(), calls=%async_computation.1 | async-start | bytes 40960
  8.6 21.5 %copy-start.48 = (s32[1024]{0:T(1024)}, s32[1024]{0:T(1024)S(1)}, u32[]{:S(2)}) copy-start(s32[1024]{0:T(1024)S(1)} %get-tuple-element.110) | copy-start | bytes 12292
  8.6 21.5 %copy-start.52 = (s32[512]{0:T(512)S(1)}, s32[512]{0:T(512)}, u32[]{:S(2)}) copy-start(s32[512]{0:T(512)} %param.16) | copy-start | bytes 6148
  8.6 21.5 %copy-start.50 = (f32[512]{0:T(512)S(1)}, f32[512]{0:T(512)}, u32[]{:S(2)}) copy-start(f32[512]{0:T(512)} %param.18) | copy-start | bytes 6148
  8.6 21.5 %copy-start.8 = (bf16[2,640,640]{2,1,0:T(8,128)(2,1)S(1)}, bf16[2,640,640]{2,1,0:T(8,128)(2,1)}, u32[]{:S(2)}) copy-start(bf16[2,640,640]{2,1,0:T(8,128)(2,1)} %param.23) | copy-start | bytes 4915204
  10.4 26.4 %collective-permute-start = (bf16[8,25,128]{2,0,1:T(8,128)(2,1)S(1)}, bf16[8,25,128]{2,0,1:T(8,128)(2,1)}, u32[]{:S(2)}, u32[]{:S(2)}) collective-permute-start(bf16[8,25,128]{2,0,1:T(8,128)(2,1)S(1)} %gather_fusion), channel_id=1, source_target_pairs={{28,0},{0,4},{4,8},{8,12},{12,16},{16,20},{20,24},{24,28},{29,1},{... | collective-permute-start | bytes 153608 | tf_op jit(solution)/shard_map/ppermute | solution.py:18
  15.0 27.7 %collective-permute-start.1 = (bf16[8,25,128]{2,0,1:T(8,128)(2,1)S(1)}, bf16[8,25,128]{2,0,1:T(8,128)(2,1)S(1)}, u32[]{:S(2)}, u32[]{:S(2)}) collective-permute-start(bf16[8,25,128]{2,0,1:T(8,128)(2,1)S(1)} %gather_fusion.1), channel_id=1, source_target_pairs={{4,0},{8,4},{12,8},{16,12},{20,16},{24,20},{28,24},{0,28},{5,1},{9... | collective-permute-start | bytes 153608 | tf_op jit(solution)/shard_map/ppermute | solution.py:18
  30.2 81.8 %copy-start.22 = (f32[512]{0:T(512)}, f32[512]{0:T(512)S(1)}, u32[]{:S(2)}) copy-start(f32[512]{0:T(512)S(1)} %get-tuple-element.105) | copy-start | bytes 6148
  30.2 81.8 %copy-start.24 = (f32[512]{0:T(512)}, f32[512]{0:T(512)S(1)}, u32[]{:S(2)}) copy-start(f32[512]{0:T(512)S(1)} %get-tuple-element.107) | copy-start | bytes 6148
  30.2 89.6 %copy-start.21 = (f32[512]{0:T(512)}, f32[512]{0:T(512)S(1)}, u32[]{:S(2)}) copy-start(f32[512]{0:T(512)S(1)} %get-tuple-element.106) | copy-start | bytes 6148
  30.4 12.2 %copy-start.9 = (bf16[128,25,128]{2,0,1:T(8,128)(2,1)S(1)}, bf16[128,25,128]{2,0,1:T(8,128)(2,1)}, u32[]{:S(2)}) copy-start(bf16[128,25,128]{2,0,1:T(8,128)(2,1)} %constant_dynamic-update-slice_fusion.2) | copy-start | bytes 2457604
  30.4 18.2 %copy-start.42 = (f32[512]{0:T(512)}, f32[512]{0:T(512)S(1)}, u32[]{:S(2)}) copy-start(f32[512]{0:T(512)S(1)} %get-tuple-element.103) | copy-start | bytes 6148
  30.4 18.2 %copy-start.44 = (f32[512]{0:T(512)}, f32[512]{0:T(512)S(1)}, u32[]{:S(2)}) copy-start(f32[512]{0:T(512)S(1)} %get-tuple-element.100) | copy-start | bytes 6148
  30.5 18.2 %copy-start.46 = (f32[512]{0:T(512)}, f32[512]{0:T(512)S(1)}, u32[]{:S(2)}) copy-start(f32[512]{0:T(512)S(1)} %get-tuple-element.101) | copy-start | bytes 6148
  30.5 18.4 %copy-start.40 = (s32[1024]{0:T(1024)}, s32[1024]{0:T(1024)S(1)}, u32[]{:S(2)}) copy-start(s32[1024]{0:T(1024)S(1)} %pad_clamp_fusion) | copy-start | bytes 12292
  30.6 43.1 %copy-start.26 = (f32[16,32]{1,0:T(8,128)}, f32[16,32]{1,0:T(8,128)S(1)}, u32[]{:S(2)}) copy-start(f32[16,32]{1,0:T(8,128)S(1)} %mul.398) | copy-start | bytes 6148
  30.6 43.0 %copy-start.27 = (f32[16,32]{1,0:T(8,128)}, f32[16,32]{1,0:T(8,128)S(1)}, u32[]{:S(2)}) copy-start(f32[16,32]{1,0:T(8,128)S(1)} %mul.410) | copy-start | bytes 6148
  30.7 28.5 %copy-start.28 = (f32[16,32]{1,0:T(8,128)}, f32[16,32]{1,0:T(8,128)S(1)}, u32[]{:S(2)}) copy-start(f32[16,32]{1,0:T(8,128)S(1)} %mul.417) | copy-start | bytes 6148
  30.8 28.4 %copy-start.29 = (f32[16,32]{1,0:T(8,128)}, f32[16,32]{1,0:T(8,128)S(1)}, u32[]{:S(2)}) copy-start(f32[16,32]{1,0:T(8,128)S(1)} %mul.428) | copy-start | bytes 6148
  68.1 5.5 %copy-start.10 = (f32[512,128]{1,0:T(8,128)S(1)}, f32[512,128]{1,0:T(8,128)}, u32[]{:S(2)}) copy-start(f32[512,128]{1,0:T(8,128)} %multiply_multiply_fusion.1) | copy-start | bytes 786436
  78.2 26.5 %copy-start.41 = (s32[1024]{0:T(1024)S(1)}, s32[1024]{0:T(1024)}, u32[]{:S(2)}) copy-start(s32[1024]{0:T(1024)} %copy-done.40) | copy-start | bytes 12292
  78.3 26.4 %copy-start.6 = (bf16[16,25,128]{2,1,0:T(8,128)(2,1)}, bf16[16,25,128]{2,1,0:T(8,128)(2,1)S(1)}, u32[]{:S(2)}) copy-start(bf16[16,25,128]{2,1,0:T(8,128)(2,1)S(1)} %add_convert_fusion.1) | copy-start | bytes 307204
  85.7 7.0 %collective-permute-start.2 = (bf16[8,25,128]{2,1,0:T(8,128)(2,1)S(1)}, bf16[8,25,128]{2,1,0:T(8,128)(2,1)S(1)}, u32[]{:S(2)}, u32[]{:S(2)}) collective-permute-start(bf16[8,25,128]{2,1,0:T(8,128)(2,1)S(1)} %gather_fusion.3), channel_id=1, source_target_pairs={{28,0},{0,4},{4,8},{8,12},{12,16},{16,20},{20,24},{24,28},{29,1},{... | collective-permute-start | bytes 153608 | tf_op jit(solution)/shard_map/ppermute | solution.py:18
  86.4 12.0 %collective-permute-start.3 = (bf16[8,25,128]{2,1,0:T(8,128)(2,1)S(1)}, bf16[8,25,128]{2,1,0:T(8,128)(2,1)S(1)}, u32[]{:S(2)}, u32[]{:S(2)}) collective-permute-start(bf16[8,25,128]{2,1,0:T(8,128)(2,1)S(1)} %gather_fusion.4), channel_id=1, source_target_pairs={{4,0},{8,4},{12,8},{16,12},{20,16},{24,20},{28,24},{0,28},{5,1},{9... | collective-permute-start | bytes 153608 | tf_op jit(solution)/shard_map/ppermute | solution.py:18
  117.0 28.2 %collective-permute-start.4 = (f32[3,32]{1,0:T(4,128)}, f32[3,32]{1,0:T(4,128)}, u32[]{:S(2)}, u32[]{:S(2)}) collective-permute-start(f32[3,32]{1,0:T(4,128)} %get-tuple-element.98), channel_id=1, source_target_pairs={{4,0},{8,4},{12,8},{16,12},{20,16},{24,20},{28,24},{0,28},{5,1},{9... | collective-permute-start | bytes 1160 | tf_op jit(solution)/shard_map/ppermute | solution.py:18
  117.0 28.2 %collective-permute-start.5 = (f32[3,32]{1,0:T(4,128)}, f32[3,32]{1,0:T(4,128)}, u32[]{:S(2)}, u32[]{:S(2)}) collective-permute-start(f32[3,32]{1,0:T(4,128)} %get-tuple-element.99), channel_id=1, source_target_pairs={{28,0},{0,4},{4,8},{8,12},{12,16},{16,20},{20,24},{24,28},{29,1},{... | collective-permute-start | bytes 1160 | tf_op jit(solution)/shard_map/ppermute | solution.py:18
  126.2 6.8 %copy-start.23 = (f32[512]{0:T(512)S(1)}, f32[512]{0:T(512)}, u32[]{:S(2)}) copy-start(f32[512]{0:T(512)} %copy-done.22) | copy-start | bytes 6148
  140.9 10.9 %copy-start.56 = (s32[8]{0:T(128)S(1)}, s32[8]{0:T(128)}, u32[]{:S(2)}) copy-start(s32[8]{0:T(128)} %param.21) | copy-start | bytes 100
  140.9 11.8 %copy-start.57 = (s32[8]{0:T(128)S(1)}, s32[8]{0:T(128)}, u32[]{:S(2)}) copy-start(s32[8]{0:T(128)} %param.22) | copy-start | bytes 100
  (34 other events, 133.5 us)
Sparse Core Ops, SparseCore 0:
  119.9 18.5 reduce-scatter.5
where the time goes:
time: 161 us; the launch traced here: 160 us
  blocking collectives  43.3 us (27%)
  local copies, waits for them, and re-layouts  38.6 us (24%)
  matrix products  34.1 us (21%)
  between operations  15.8 us (10%)
  other arithmetic  14 us (9%)
  starting transfers between devices  13 us (8%)
    all_gather x2, blocking collectives, body(): lax.all_gather(outgoing, 'yz', axis=0, tiled=True)  13.6 us
    ppermute x6, starting transfers between devices, from_behind(): return lax.ppermute(block, axis, route)  12.9 us
    all_gather x2, blocking collectives, body(): lax.all_gather(above_one, 'yz', axis=0, tiled=True)  11.7 us
    all_gather x2, blocking collectives, body(): lax.all_gather(below_one, 'yz', axis=0, tiled=True)  11.5 us
    reduce_sum x4, other arithmetic, convolve(): back_plus = (cos_rows * out_plus - sin_rows * out_minus).reshape(atom_cou...  11.3 us
    dot_general x4, matrix products, convolve(): jnp.dot(turned_minus, real_part, preferred_element_type=jnp.float32)  10.3 us
    reshape x4, local copies, waits for them, and re-layouts, convolve(): out_minus = (jnp.dot(turned_plus, imag_part, preferred_element_type=jnp.f...  7.79 us
    reshape x4, local copies, waits for them, and re-layouts, convolve(): out_plus = (jnp.dot(turned_plus, real_part, preferred_element_type=jnp.fl...  6.82 us
  transfers between devices with their start and end apart: 7, of which 1 were waited for; matrix products, arithmetic and copies ran while one was open for 24% of the time, Pallas kernels for 0%

commit v1 on v0

v1 whole, which is shorter than its diff:
```python
import functools
import math

import jax
import jax.numpy as jnp
from jax import lax
from jax.experimental import pallas as pl
from jax.experimental.pallas import tpu as pltpu
from jax.sharding import PartitionSpec as P

HIGHEST = lax.Precision.HIGHEST
BF16 = jnp.bfloat16
F32 = jnp.float32
ORDERS = (1, 2)
VMEM = pl.BlockSpec(memory_space=pltpu.VMEM)


def slot_index(degree, azimuth_order):
    return degree * degree + degree + azimuth_order


def slot_groups(degrees):
    groups = [[slot_index(degree, 0) for degree in range(degrees)]]
    for order in ORDERS:
        groups.append([slot_index(degree, order) for degree in range(order, degrees)])
        groups.append([slot_index(degree, -order) for degree in range(order, degrees)])
    return groups


def slot_order(degrees):
    return [slot for group in slot_groups(degrees) for slot in group]


def odd_slab():
    return lax.axis_index("slab") % 2 == 1


def dot(left, right, contract=((1,), (0,)), precision=None):
    return lax.dot_general(
        left, right, (contract, ((), ())), precision=precision, preferred_element_type=F32
    )


def lent_hot(low_ref, high_ref, atoms):
    odd = odd_slab()
    low, high = low_ref[...], high_ref[...]
    picks = jnp.concatenate([jnp.where(odd, low, high), jnp.where(odd, high, low)], axis=1)
    rows = lax.broadcasted_iota(jnp.int32, (atoms, picks.shape[1]), 0)
    return (rows == picks).astype(F32)


def lent_rows(hot, rows):
    return dot(hot.astype(BF16), rows, ((0,), (0,))).astype(BF16)


def pack_kernel(emb_ref, low_ref, high_ref, own_ref, pair_ref, other_ref, wide):
    atoms, coeffs, channels = emb_ref.shape
    ghosts = low_ref.shape[1]
    wide[...] = emb_ref[...].astype(F32)
    for place, slot in enumerate(slot_order(math.isqrt(coeffs))):
        own_ref[:, place * channels : (place + 1) * channels] = wide[:, slot, :].astype(BF16)
    lent = lent_rows(lent_hot(low_ref, high_ref, atoms), own_ref[...])
    pair_ref[...] = lent[:ghosts]
    other_ref[...] = lent[ghosts:]


def static_kernel(
    atoms, ghosts, slab_devices,
    nbr_ref, valid_ref, azi_ref, pol_ref, dist_ref, rw_ref,
    hot_ref, radial_ref, dirs_ref, pulls_ref,
):
    layers, centers = rw_ref.shape[0], rw_ref.shape[1]
    nbr = nbr_ref[...]
    edges = nbr.shape[1]
    own_count, ghost_count = slab_devices * atoms, slab_devices * ghosts
    block = atoms + 2 * ghosts
    me = lax.axis_index("yz")
    odd = odd_slab()
    is_own = nbr < own_count
    ghost = nbr - own_count
    below = ghost < ghost_count
    ghost = jnp.where(below, ghost, ghost - ghost_count)
    paired = jnp.where(odd, below.astype(jnp.int32), 1 - below.astype(jnp.int32))
    device = jnp.where(is_own, nbr // atoms, ghost // ghosts)
    inner = jnp.where(
        is_own, nbr % atoms, atoms + (1 - paired) * ghosts + ghost % ghosts
    )
    place = (device ^ me) * block + inner
    rows = lax.broadcasted_iota(jnp.int32, (slab_devices * block, edges), 0)
    hot = jnp.where((rows == place) & (valid_ref[...] != 0), 1.0, 0.0).astype(F32)
    hot_cols = jnp.transpose(hot).astype(BF16)
    hot_ref[...] = jnp.concatenate([hot_cols, hot_cols], axis=1)
    middle = 1.0 + 0.5 * lax.broadcasted_iota(jnp.int32, (centers, edges), 0).astype(F32)
    basis = jnp.exp(-jnp.square((dist_ref[...] - middle) / 0.5))
    for layer in range(layers):
        scale = dot(basis, rw_ref[layer], ((0,), (0,)), HIGHEST)
        radial = scale / (1.0 + jnp.exp(-scale))
        radial_ref[layer] = radial
    azimuth, polar = azi_ref[...], pol_ref[...]
    sin_polar = jnp.sin(polar)
    dirs = [sin_polar * jnp.cos(azimuth), sin_polar * jnp.sin(azimuth), jnp.cos(polar)]
    dirs_ref[...] = jnp.concatenate(dirs, axis=0)
    channels = rw_ref.shape[2]
    for axis, along in enumerate(dirs):
        pulls_ref[:, axis * channels : (axis + 1) * channels] = dot(
            hot * along, radial, precision=HIGHEST
        ).astype(BF16)


def layer_sums(layer, degrees, channels, tables, weights, hot_ref, radial_ref, scratch):
    joined, mixed = scratch
    groups = slot_groups(degrees)
    w_zero, w_one_re, w_one_im, w_two_re, w_two_im = (ref[layer] for ref in weights)
    width = joined.shape[1]
    start = 0
    for ref in tables:
        count = ref.shape[0]
        joined[start : start + count] = ref[:, :width].astype(F32)
        start += count
    rows = start

    def put(column, value):
        high = value.astype(BF16)
        low = (value - high.astype(F32)).astype(BF16)
        mixed[:rows, column : column + value.shape[1]] = high
        mixed[rows:, column : column + value.shape[1]] = low

    span = len(groups[0]) * channels
    zero = dot(joined[:, :span].astype(BF16), w_zero)
    put(0, zero)
    column = span
    for index, (real, imag) in enumerate(((w_one_re, w_one_im), (w_two_re, w_two_im))):
        span = len(groups[2 * index + 1]) * channels
        both = jnp.concatenate(
            [joined[:, column : column + span], joined[:, column + span : column + 2 * span]], axis=0
        ).astype(BF16)
        by_real = dot(both, real)
        by_imag = dot(both, imag)
        put(column, by_real[:rows] - by_imag[rows:])
        put(column + span, by_imag[:rows] + by_real[rows:])
        column += 2 * span
    radial = radial_ref[layer]
    edges = radial.shape[0]
    hot = hot_ref[...]
    atoms = tables[0].shape[0]
    sums = []
    first = None
    step = 2 * channels
    for begin in range(0, width, step):
        got = dot(hot, mixed[:, begin : min(begin + step, width)])
        for inner in range(0, got.shape[1], channels):
            message = got[:, inner : inner + channels] * radial
            if first is None:
                first = message
            sums.append(message.reshape(atoms, edges // atoms, channels).sum(axis=1))
    return sums, first, zero


def first_kernel(
    layer, last, degrees, channels, count,
    low_ref, high_ref, hot_ref, radial_ref, pulls_ref, *refs,
):
    tables, weights = refs[:count], refs[count : count + 5]
    own_ref, pair_ref, other_ref = refs[count + 5 : count + 8]
    scratch = refs[count + 8 :]
    sums, _, _ = layer_sums(
        layer, degrees, channels, tables, weights, hot_ref, radial_ref, scratch
    )
    atoms = tables[0].shape[0]
    ghosts = low_ref.shape[1]
    width = len(sums) * channels
    for place, total in enumerate(sums):
        cols = slice(place * channels, (place + 1) * channels)
        own_ref[:, cols] = (tables[0][:, cols].astype(F32) + 0.18 * total).astype(BF16)
    lent = lent_rows(lent_hot(low_ref, high_ref, atoms), own_ref[:, :width])
    pair_ref[:, :width] = lent[:ghosts]
    other_ref[:, :width] = lent[ghosts:]
    if last:
        block = atoms + 2 * ghosts
        part = pulls_ref.shape[1]
        for slot in range(pulls_ref.shape[0] // block):
            cols = slice(width + slot * part, width + (slot + 1) * part)
            at = slot * block
            own_ref[:, cols] = pulls_ref[at : at + atoms]
            pair_ref[:, cols] = pulls_ref[at + atoms : at + atoms + ghosts]
            other_ref[:, cols] = pulls_ref[at + atoms + ghosts : at + block]


def last_kernel(
    layer, degrees, channels, count,
    emb_ref, low_ref, high_ref, hot_ref, radial_ref, dirs_ref, readout_ref, *refs,
):
    tables, weights = refs[:count], refs[count : count + 5]
    out_ref, force_ref = refs[count + 5 : count + 7]
    joined, mixed, wide = refs[count + 7 :]
    sums, first, zero = layer_sums(
        layer, degrees, channels, tables, weights, hot_ref, radial_ref, (joined, mixed)
    )
    atoms = tables[0].shape[0]
    ghosts = low_ref.shape[1]
    wide[...] = emb_ref[...].astype(F32)
    for place, slot in enumerate(slot_order(degrees)):
        cols = slice(place * channels, (place + 1) * channels)
        wide[:, slot, :] = tables[0][:, cols].astype(F32) + 0.18 * sums[place]
    out_ref[...] = wide[...].astype(BF16)

    readout = 0.125 * readout_ref[...]
    strength = dot(readout, first, ((1,), (1,)), HIGHEST)
    pull = dirs_ref[...] * strength
    edges = pull.shape[1]
    edge = lax.broadcasted_iota(jnp.int32, (atoms, edges), 1)
    atom = lax.broadcasted_iota(jnp.int32, (atoms, edges), 0)
    owner = (edge // (edges // atoms) == atom).astype(F32)
    own_force = dot(pull, owner, ((1,), (1,)), HIGHEST)

    width = len(sums) * channels
    part = 3 * channels
    kinds = [0.0, 0.0, 0.0]
    for slot in range(count // 3):
        for kind in range(3):
            ref = tables[3 * slot + kind]
            kinds[kind] += ref[:, width + slot * part : width + (slot + 1) * part].astype(F32)
    lent = jnp.concatenate(kinds[1:], axis=0)
    pulls = kinds[0] + dot(lent_hot(low_ref, high_ref, atoms), lent, precision=HIGHEST)
    mine = zero[:atoms, :channels] * readout
    ones = jnp.ones((1, channels), F32)
    for axis in range(3):
        back = dot(
            ones, mine * pulls[:, axis * channels : (axis + 1) * channels], ((1,), (1,)), HIGHEST
        )
        force_ref[axis : axis + 1, :] = own_force[axis : axis + 1] - back


def exchange(own, pair, other, slabs, slab_devices):
    def toward(block, step):
        route = []
        for slab in range(slabs):
            to = slab + 1 if (slab % 2 == 0) == (step > 0) else slab - 1
            route.append((slab, to % slabs))
        return lax.ppermute(block, "slab", route)

    got_other = toward(other, -1)
    got_pair = toward(pair, 1)
    held = {0: (own, got_pair, got_other)}
    bit = slab_devices // 2
    while bit:
        route = [(q, q ^ bit) for q in range(slab_devices)]
        for slot in sorted(held):
            held[slot | bit] = tuple(lax.ppermute(block, "yz", route) for block in held[slot])
        bit //= 2
    return [block for slot in range(slab_devices) for block in held[slot]]


def body(
    embeddings, neighbours, valid, azimuth, polar, distance, send_low, send_high,
    w_zero, w_one_re, w_one_im, w_two_re, w_two_im, radial_weight, readout,
):
    atoms, coeffs, channels = embeddings.shape
    degrees = math.isqrt(coeffs)
    ghosts = send_low.shape[0]
    edges = neighbours.shape[0]
    layers = w_zero.shape[0]
    slabs, slab_devices = lax.axis_size("slab"), lax.axis_size("yz")
    rows = slab_devices * (atoms + 2 * ghosts)
    width = len(slot_order(degrees)) * channels
    low, high = send_low.reshape(1, -1), send_high.reshape(1, -1)
    shape = jax.ShapeDtypeStruct

    own, pair, other = pl.pallas_call(
        pack_kernel,
        out_shape=[
            shape((atoms, width), BF16), shape((ghosts, width), BF16), shape((ghosts, width), BF16)
        ],
        in_specs=[VMEM] * 3,
        out_specs=[VMEM] * 3,
        scratch_shapes=[pltpu.VMEM((atoms, coeffs, channels), F32)],
        name="pack",
    )(embeddings, low, high)

    row = lambda value: value.reshape(1, -1)
    hot, radial, dirs, pulls = pl.pallas_call(
        functools.partial(static_kernel, atoms, ghosts, slab_devices),
        out_shape=[
            shape((edges, 2 * rows), BF16), shape((layers, edges, channels), F32),
            shape((3, edges), F32), shape((rows, 3 * channels), BF16),
        ],
        in_specs=[VMEM] * 6,
        out_specs=[VMEM] * 4,
        name="geometry",
    )(row(neighbours), row(valid), row(azimuth), row(polar), row(distance), radial_weight)

    weights = (w_zero, w_one_re, w_one_im, w_two_re, w_two_im)
    scratch = [pltpu.VMEM((rows, width), F32), pltpu.VMEM((2 * rows, width), BF16)]
    for layer in range(layers):
        tables = exchange(own, pair, other, slabs, slab_devices)
        if layer < layers - 1:
            last = layer == layers - 2
            wide = width + (slab_devices * 3 * channels if last else 0)
            own, pair, other = pl.pallas_call(
                functools.partial(first_kernel, layer, last, degrees, channels, len(tables)),
                out_shape=[
                    shape((atoms, wide), BF16), shape((ghosts, wide), BF16),
                    shape((ghosts, wide), BF16),
                ],
                in_specs=[VMEM] * (5 + len(tables) + len(weights)),
                out_specs=[VMEM] * 3,
                scratch_shapes=scratch,
                name="layer",
            )(low, high, hot, radial, pulls, *tables, *weights)
        else:
            updated, forces = pl.pallas_call(
                functools.partial(last_kernel, layer, degrees, channels, len(tables)),
                out_shape=[shape((atoms, coeffs, channels), BF16), shape((3, atoms), F32)],
                in_specs=[VMEM] * (7 + len(tables) + len(weights)),
                out_specs=[VMEM] * 2,
                scratch_shapes=scratch + [pltpu.VMEM((atoms, coeffs, channels), F32)],
                name="last_layer",
            )(embeddings, low, high, hot, radial, dirs, readout.reshape(1, -1), *tables, *weights)
    return (updated, forces)


def solution(mesh):
    both = ("slab", "yz")
    in_specs = (P(both, None, None), *([P(both)] * 7), *([P()] * 7))
    out_specs = (P(both, None, None), P(None, both))
    return jax.shard_map(body, mesh=mesh, in_specs=in_specs, out_specs=out_specs, check_vma=False)
```

time: 161 us -> 49.9 us (0.31)
  blocking collectives: 43.3 us -> 0 us
  local copies, waits for them, and re-layouts: 38.6 us -> 4.37 us
  matrix products: 34.1 us -> 0 us
  Pallas kernels: 0 us -> 16 us
  between operations: 15.8 us -> 0.9 us
  other arithmetic: 14 us -> 0 us
  waiting for transfers between devices: 1.57 us -> 10.1 us
  starting transfers between devices: 13 us -> 18.3 us
    all_gather x6 -> x0, blocking collectives: 36.8 us -> none  [the longest x2 13.6 us: body(): lax.all_gather(outgoing, 'yz', axis=0, tiled=True)]
    dot_general x24 -> x0, matrix products: 34.1 us -> none  [the longest x4 10.3 us: convolve(): jnp.dot(turned_minus, real_part, preferred_element_type=jnp.float32)]
    pallas_call x0 -> x4, Pallas kernels: none -> 16 us  [the longest x1 5.88 us: body(): pl.pallas_call(functools.partial(last_kernel, layer, degrees, channels, l...]
    reshape x8 -> x0, local copies, waits for them, and re-layouts: 14.6 us -> none  [the longest x4 7.79 us: convolve(): out_minus = (jnp.dot(turned_plus, imag_part, preferred_element_type=jnp.f...]
    reduce_sum x5 -> x0, other arithmetic: 11.3 us -> none  [the longest x4 11.3 us: convolve(): back_plus = (cos_rows * out_plus - sin_rows * out_minus).reshape(atom_cou...]
    gather x6 -> x0, local copies, waits for them, and re-layouts: 9.93 us -> none  [the longest x2 5.22 us: body(): table[neighbours]]
    ppermute x6 -> x22, waiting for transfers between devices: 1.56 us -> 10.1 us  [the longest x18 6.29 us: exchange(): lax.ppermute(block, 'yz', route)]
    unnamed x1 -> x0, blocking collectives: 6.5 us -> none
  transfers between devices with their start and end apart: 7 -> 22, of which waited for: 1 -> 7; matrix products, arithmetic and copies ran while one was open for 24% -> 0% of each run, Pallas kernels for 0% -> 6%
where the time goes in v1:
time: 49.9 us; the launch traced here: 49.7 us
  starting transfers between devices  18.3 us (37%)
  Pallas kernels  16 us (32%)
  waiting for transfers between devices  10.1 us (20%)
  local copies, waits for them, and re-layouts  4.37 us (9%)
  between operations  0.9 us (2%)
    ppermute x18, starting transfers between devices, exchange(): lax.ppermute(block, 'yz', route)  9.67 us
    ppermute x4, starting transfers between devices, toward(): return lax.ppermute(block, 'slab', route)  8.64 us
    ppermute x18, waiting for transfers between devices, exchange(): lax.ppermute(block, 'yz', route)  6.29 us
    pallas_call x1, Pallas kernels, body(): pl.pallas_call(functools.partial(last_kernel, layer, degrees, channels, l...  5.88 us
    pallas_call x1, Pallas kernels, body(): pl.pallas_call(functools.partial(first_kernel, layer, last, degrees, chan...  5.17 us
    ppermute x4, waiting for transfers between devices, toward(): return lax.ppermute(block, 'slab', route)  3.84 us
    pallas_call x1, Pallas kernels, body(): pl.pallas_call(functools.partial(static_kernel, atoms, ghosts, slab_devic...  3.04 us
    unnamed x45, local copies, waits for them, and re-layouts  2.78 us
  transfers between devices with their start and end apart: 22, of which 7 were waited for; matrix products, arithmetic and copies ran while one was open for 0% of the time, Pallas kernels for 6%

profile of v1, /device:TPU:0, one launch (start us, length us, event | category | flops | bytes accessed | tf_op | source)
XLA Modules:
  0.0 49.7 jit_solution(11176982477191631861)
XLA Ops:
  0.6 1.6 %copy.18.emb_ref = bf16[16,25,128]{2,1,0:T(8,128)(2,1)} copy(bf16[16,25,128]{2,0,1:T(8,128)(2,1)} %param.15) | data formatting | bytes 204800 | tf_op args[0]
  2.2 1.9 %pack.1 = (bf16[16,2432]{1,0:T(8,128)(2,1)}, bf16[8,2432]{1,0:T(8,128)(2,1)}, bf16[8,2432]{1,0:T(8,128)(2,1)}) custom-call(bf16[16,25,128]{2,1,0:T(8,128)(2,1)} %copy.18.emb_ref, s32[1,8]{1,0:T(1,128)} %bitcast.8, s32[1,8]{1,0:T(1,128)} %bitcast.11), custom_call_target="tpu_custom_call" | custom-call | tf_op jit(solution)/shard_map/pack/pallas_call | solution.py:269
  4.1 3.0 %collective-permute-start.5 = (bf16[16,2432]{1,0:T(8,128)(2,1)}, bf16[16,2432]{1,0:T(8,128)(2,1)S(1)}, u32[]{:S(2)}, u32[]{:S(2)}) collective-permute-start(bf16[16,2432]{1,0:T(8,128)(2,1)} %get-tuple-element.16.refs_0_), channel_id=1, source_target_pairs={{0,2},{1,3},{2,0},{3,1},{4,6},{5,7},{6,4},{7,5},{8,10},{9,11},{10,... | collective-permute-start | bytes 233480 | tf_op jit(solution)/shard_map/ppermute | solution.py:249
  7.1 1.5 %collective-permute-start = (bf16[8,2432]{1,0:T(8,128)(2,1)}, bf16[8,2432]{1,0:T(8,128)(2,1)S(1)}, u32[]{:S(2)}, u32[]{:S(2)}) collective-permute-start(bf16[8,2432]{1,0:T(8,128)(2,1)} %get-tuple-element.17), channel_id=1, source_target_pairs={{0,4},{4,0},{8,12},{12,8},{16,20},{20,16},{24,28},{28,24},{1,5},{5... | collective-permute-start | bytes 116744 | tf_op jit(solution)/shard_map/ppermute | solution.py:240
  8.6 3.6 %collective-permute-start.1 = (bf16[8,2432]{1,0:T(8,128)(2,1)}, bf16[8,2432]{1,0:T(8,128)(2,1)S(1)}, u32[]{:S(2)}, u32[]{:S(2)}) collective-permute-start(bf16[8,2432]{1,0:T(8,128)(2,1)} %get-tuple-element.18), channel_id=1, source_target_pairs={{0,28},{4,8},{8,4},{12,16},{16,12},{20,24},{24,20},{28,0},{1,29},{... | collective-permute-start | bytes 116744 | tf_op jit(solution)/shard_map/ppermute | solution.py:240
  12.1 0.5 %collective-permute-start.6 = (bf16[8,2432]{1,0:T(8,128)(2,1)S(1)}, bf16[8,2432]{1,0:T(8,128)(2,1)S(1)}, u32[]{:S(2)}, u32[]{:S(2)}) collective-permute-start(bf16[8,2432]{1,0:T(8,128)(2,1)S(1)} %collective-permute-done.refs_1_), channel_id=1, source_target_pairs={{0,2},{1,3},{2,0},{3,1},{4,6},{5,7},{6,4},{7,5},{8,10},{9,11},{10,... | collective-permute-start | bytes 116744 | tf_op jit(solution)/shard_map/ppermute | solution.py:249
  12.7 0.5 %collective-permute-start.3 = (bf16[8,2432]{1,0:T(8,128)(2,1)S(1)}, bf16[8,2432]{1,0:T(8,128)(2,1)S(1)}, u32[]{:S(2)}, u32[]{:S(2)}) collective-permute-start(bf16[8,2432]{1,0:T(8,128)(2,1)S(1)} %collective-permute-done.refs_1_), channel_id=1, source_target_pairs={{0,1},{1,0},{2,3},{3,2},{4,5},{5,4},{6,7},{7,6},{8,9},{9,8},{10,11... | collective-permute-start | bytes 116744 | tf_op jit(solution)/shard_map/ppermute | solution.py:249
  13.2 2.3 %collective-permute-done.1.refs_2_ = bf16[8,2432]{1,0:T(8,128)(2,1)S(1)} collective-permute-done((bf16[8,2432]{1,0:T(8,128)(2,1)}, bf16[8,2432]{1,0:T(8,128)(2,1)S(1)}, u32[]{:S(2)}, u32[]{:S(2)}) %collective-permute-start.1) | collective-permute-done | bytes 38944 | tf_op jit(solution)/shard_map/ppermute | solution.py:240
  15.5 0.5 %collective-permute-start.7 = (bf16[8,2432]{1,0:T(8,128)(2,1)S(1)}, bf16[8,2432]{1,0:T(8,128)(2,1)S(1)}, u32[]{:S(2)}, u32[]{:S(2)}) collective-permute-start(bf16[8,2432]{1,0:T(8,128)(2,1)S(1)} %collective-permute-done.1.refs_2_), channel_id=1, source_target_pairs={{0,2},{1,3},{2,0},{3,1},{4,6},{5,7},{6,4},{7,5},{8,10},{9,11},{10,... | collective-permute-start | bytes 116744 | tf_op jit(solution)/shard_map/ppermute | solution.py:249
  16.0 0.2 collective-permute-done.6.refs_7_
  16.1 0.4 collective-permute-start.4
  16.5 0.2 collective-permute-start.9
  16.6 2.8 %collective-permute-done.7.refs_8_ = bf16[8,2432]{1,0:T(8,128)(2,1)S(1)} collective-permute-done((bf16[8,2432]{1,0:T(8,128)(2,1)S(1)}, bf16[8,2432]{1,0:T(8,128)(2,1)S(1)}, u32[]{:S(2)}, u32[]{:S(2)}) %collective-permute-start.7) | collective-permute-done | bytes 38944 | tf_op jit(solution)/shard_map/ppermute | solution.py:249
  19.4 3.0 %geometry.1 = (bf16[512,256]{1,0:T(8,128)(2,1)}, f32[2,512,128]{2,1,0:T(8,128)}, f32[3,512]{1,0:T(4,128)}, bf16[128,384]{1,0:T(8,128)(2,1)}) custom-call(s32[1,512]{1,0:T(1,128)} %bitcast.14, s32[1,512]{1,0:T(1,128)} %bitcast.15, f32[1,512]{1,0:T(1,128)} %bitcast.16, f32[1,512]{1,0:T(1,128)} %bitcast.17, f32[1,512]{1,0:T(1,128)} %bitcast.18, f32[2,8,128]{2,1,0:T(8,128)} %rw_ref.1), custom_call_target="tpu_custom_call" | custom-call | tf_op jit(solution)/shard_map/geometry/pallas_call | solution.py:281
  22.6 0.5 copy-done.19
  23.1 0.0 copy-done.4
  23.2 5.2 %layer.1 = (bf16[16,3968]{1,0:T(8,128)(2,1)}, bf16[8,3968]{1,0:T(8,128)(2,1)}, bf16[8,3968]{1,0:T(8,128)(2,1)}) custom-call(s32[1,8]{1,0:T(1,128)} %bitcast.9, s32[1,8]{1,0:T(1,128)} %bitcast.12, bf16[512,256]{1,0:T(8,128)(2,1)} %get-tuple-element.12.hot_ref, f32[2,512,128]{2,1,0:T(8,128)} %get-tuple-element.13.radial_ref, ...), custom_call_target="tpu_custom_call" | custom-call | tf_op jit(solution)/shard_map/layer/pallas_call | solution.py:299
  28.4 0.5 %collective-permute-start.16 = (bf16[16,3968]{1,0:T(8,128)(2,1)}, bf16[16,3968]{1,0:T(8,128)(2,1)S(1)}, u32[]{:S(2)}, u32[]{:S(2)}) collective-permute-start(bf16[16,3968]{1,0:T(8,128)(2,1)} %get-tuple-element.19.refs_0_), channel_id=1, source_target_pairs={{0,2},{1,3},{2,0},{3,1},{4,6},{5,7},{6,4},{7,5},{8,10},{9,11},{10,... | collective-permute-start | bytes 380936 | tf_op jit(solution)/shard_map/ppermute | solution.py:249
  28.9 3.6 %collective-permute-start.12 = (bf16[8,3968]{1,0:T(8,128)(2,1)}, bf16[8,3968]{1,0:T(8,128)(2,1)S(1)}, u32[]{:S(2)}, u32[]{:S(2)}) collective-permute-start(bf16[8,3968]{1,0:T(8,128)(2,1)} %get-tuple-element.21), channel_id=1, source_target_pairs={{0,28},{4,8},{8,4},{12,16},{16,12},{20,24},{24,20},{28,0},{1,29},{... | collective-permute-start | bytes 190472 | tf_op jit(solution)/shard_map/ppermute | solution.py:240
  32.5 0.9 %collective-permute-done.11.refs_1_ = bf16[8,3968]{1,0:T(8,128)(2,1)S(1)} collective-permute-done((bf16[8,3968]{1,0:T(8,128)(2,1)}, bf16[8,3968]{1,0:T(8,128)(2,1)S(1)}, u32[]{:S(2)}, u32[]{:S(2)}) %collective-permute-start.11) | collective-permute-done | bytes 63520 | tf_op jit(solution)/shard_map/ppermute | solution.py:240
  33.3 1.5 %collective-permute-start.17 = (bf16[8,3968]{1,0:T(8,128)(2,1)S(1)}, bf16[8,3968]{1,0:T(8,128)(2,1)S(1)}, u32[]{:S(2)}, u32[]{:S(2)}) collective-permute-start(bf16[8,3968]{1,0:T(8,128)(2,1)S(1)} %collective-permute-done.11.refs_1_), channel_id=1, source_target_pairs={{0,2},{1,3},{2,0},{3,1},{4,6},{5,7},{6,4},{7,5},{8,10},{9,11},{10,... | collective-permute-start | bytes 190472 | tf_op jit(solution)/shard_map/ppermute | solution.py:249
  34.9 0.5 %collective-permute-start.14 = (bf16[8,3968]{1,0:T(8,128)(2,1)S(1)}, bf16[8,3968]{1,0:T(8,128)(2,1)S(1)}, u32[]{:S(2)}, u32[]{:S(2)}) collective-permute-start(bf16[8,3968]{1,0:T(8,128)(2,1)S(1)} %collective-permute-done.11.refs_1_), channel_id=1, source_target_pairs={{0,1},{1,0},{2,3},{3,2},{4,5},{5,4},{6,7},{7,6},{8,9},{9,8},{10,11... | collective-permute-start | bytes 190472 | tf_op jit(solution)/shard_map/ppermute | solution.py:249
  35.4 0.7 %collective-permute-done.12.refs_2_ = bf16[8,3968]{1,0:T(8,128)(2,1)S(1)} collective-permute-done((bf16[8,3968]{1,0:T(8,128)(2,1)}, bf16[8,3968]{1,0:T(8,128)(2,1)S(1)}, u32[]{:S(2)}, u32[]{:S(2)}) %collective-permute-start.12) | collective-permute-done | bytes 63520 | tf_op jit(solution)/shard_map/ppermute | solution.py:240
  36.0 1.5 %collective-permute-start.18 = (bf16[8,3968]{1,0:T(8,128)(2,1)S(1)}, bf16[8,3968]{1,0:T(8,128)(2,1)S(1)}, u32[]{:S(2)}, u32[]{:S(2)}) collective-permute-start(bf16[8,3968]{1,0:T(8,128)(2,1)S(1)} %collective-permute-done.12.refs_2_), channel_id=1, source_target_pairs={{0,2},{1,3},{2,0},{3,1},{4,6},{5,7},{6,4},{7,5},{8,10},{9,11},{10,... | collective-permute-start | bytes 190472 | tf_op jit(solution)/shard_map/ppermute | solution.py:249
  37.6 0.5 collective-permute-start.15
  38.1 0.1 collective-permute-start.20
  38.2 2.1 %collective-permute-done.18.refs_8_ = bf16[8,3968]{1,0:T(8,128)(2,1)S(1)} collective-permute-done((bf16[8,3968]{1,0:T(8,128)(2,1)S(1)}, bf16[8,3968]{1,0:T(8,128)(2,1)S(1)}, u32[]{:S(2)}, u32[]{:S(2)}) %collective-permute-start.18) | collective-permute-done | bytes 63520 | tf_op jit(solution)/shard_map/ppermute | solution.py:249
  40.3 1.2 %collective-permute-done.21.refs_11_ = bf16[8,3968]{1,0:T(8,128)(2,1)S(1)} collective-permute-done((bf16[8,3968]{1,0:T(8,128)(2,1)S(1)}, bf16[8,3968]{1,0:T(8,128)(2,1)S(1)}, u32[]{:S(2)}, u32[]{:S(2)}) %collective-permute-start.21) | collective-permute-done | bytes 63520 | tf_op jit(solution)/shard_map/ppermute | solution.py:249
  41.6 0.5 %copy-done.13 = bf16[8,3968]{1,0:T(8,128)(2,1)} copy-done((bf16[8,3968]{1,0:T(8,128)(2,1)}, bf16[8,3968]{1,0:T(8,128)(2,1)S(1)}, u32[]{:S(2)}) %copy-start.13) | copy-done | bytes 63512
  42.1 0.1 copy-done.2
  42.2 5.9 %last_layer.1 = (bf16[16,25,128]{2,1,0:T(8,128)(2,1)}, f32[3,16]{1,0:T(4,128)}) custom-call(bf16[16,25,128]{2,1,0:T(8,128)(2,1)} %copy.18.emb_ref, s32[1,8]{1,0:T(1,128)} %bitcast.10, s32[1,8]{1,0:T(1,128)} %bitcast.13, bf16[512,256]{1,0:T(8,128)(2,1)} %get-tuple-element.12.hot_ref, f32[2,512,128]{2,1,0:T(8,128)} %get-tuple-element.13.radial_ref, ...), custom_call_target="tpu_custom_call" | custom-call | tf_op jit(solution)/shard_map/last_layer/pallas_call | solution.py:311
  48.1 1.6 %copy.19 = bf16[16,25,128]{2,0,1:T(8,128)(2,1)} copy(bf16[16,25,128]{2,1,0:T(8,128)(2,1)} %get-tuple-element.22) | data formatting | bytes 204800 | tf_op jit(solution)/shard_map/last_layer/pallas_call | solution.py:311
  (62 shorter events, 0.2 us)
Async XLA Ops:
  4.1 11.9 %collective-permute-start.5 = (bf16[16,2432]{1,0:T(8,128)(2,1)}, bf16[16,2432]{1,0:T(8,128)(2,1)S(1)}, u32[]{:S(2)}, u32[]{:S(2)}) collective-permute-start(bf16[16,2432]{1,0:T(8,128)(2,1)} %get-tuple-element.16.refs_0_), channel_id=1, source_target_pairs={{0,2},{1,3},{2,0},{3,1},{4,6},{5,7},{6,4},{7,5},{8,10},{9,11},{10,... | collective-permute-start | bytes 233480 | tf_op jit(solution)/shard_map/ppermute | solution.py:249
  7.1 5.1 %collective-permute-start = (bf16[8,2432]{1,0:T(8,128)(2,1)}, bf16[8,2432]{1,0:T(8,128)(2,1)S(1)}, u32[]{:S(2)}, u32[]{:S(2)}) collective-permute-start(bf16[8,2432]{1,0:T(8,128)(2,1)} %get-tuple-element.17), channel_id=1, source_target_pairs={{0,4},{4,0},{8,12},{12,8},{16,20},{20,16},{24,28},{28,24},{1,5},{5... | collective-permute-start | bytes 116744 | tf_op jit(solution)/shard_map/ppermute | solution.py:240
  8.6 6.9 %collective-permute-start.1 = (bf16[8,2432]{1,0:T(8,128)(2,1)}, bf16[8,2432]{1,0:T(8,128)(2,1)S(1)}, u32[]{:S(2)}, u32[]{:S(2)}) collective-permute-start(bf16[8,2432]{1,0:T(8,128)(2,1)} %get-tuple-element.18), channel_id=1, source_target_pairs={{0,28},{4,8},{8,4},{12,16},{16,12},{20,24},{24,20},{28,0},{1,29},{... | collective-permute-start | bytes 116744 | tf_op jit(solution)/shard_map/ppermute | solution.py:240
  12.1 10.4 %copy-start.14 = (bf16[8,2432]{1,0:T(8,128)(2,1)}, bf16[8,2432]{1,0:T(8,128)(2,1)S(1)}, u32[]{:S(2)}) copy-start(bf16[8,2432]{1,0:T(8,128)(2,1)S(1)} %collective-permute-done.refs_1_) | copy-start | bytes 116740
  12.1 4.0 %collective-permute-start.6 = (bf16[8,2432]{1,0:T(8,128)(2,1)S(1)}, bf16[8,2432]{1,0:T(8,128)(2,1)S(1)}, u32[]{:S(2)}, u32[]{:S(2)}) collective-permute-start(bf16[8,2432]{1,0:T(8,128)(2,1)S(1)} %collective-permute-done.refs_1_), channel_id=1, source_target_pairs={{0,2},{1,3},{2,0},{3,1},{4,6},{5,7},{6,4},{7,5},{8,10},{9,11},{10,... | collective-permute-start | bytes 116744 | tf_op jit(solution)/shard_map/ppermute | solution.py:249
  12.6 9.8 %collective-permute-start.2 = (bf16[16,2432]{1,0:T(8,128)(2,1)}, bf16[16,2432]{1,0:T(8,128)(2,1)S(1)}, u32[]{:S(2)}, u32[]{:S(2)}) collective-permute-start(bf16[16,2432]{1,0:T(8,128)(2,1)} %get-tuple-element.16.refs_0_), channel_id=1, source_target_pairs={{0,1},{1,0},{2,3},{3,2},{4,5},{5,4},{6,7},{7,6},{8,9},{9,8},{10,11... | collective-permute-start | bytes 233480 | tf_op jit(solution)/shard_map/ppermute | solution.py:249
  12.7 3.8 %collective-permute-start.3 = (bf16[8,2432]{1,0:T(8,128)(2,1)S(1)}, bf16[8,2432]{1,0:T(8,128)(2,1)S(1)}, u32[]{:S(2)}, u32[]{:S(2)}) collective-permute-start(bf16[8,2432]{1,0:T(8,128)(2,1)S(1)} %collective-permute-done.refs_1_), channel_id=1, source_target_pairs={{0,1},{1,0},{2,3},{3,2},{4,5},{5,4},{6,7},{7,6},{8,9},{9,8},{10,11... | collective-permute-start | bytes 116744 | tf_op jit(solution)/shard_map/ppermute | solution.py:249
  15.4 7.1 %copy-start.15 = (bf16[8,2432]{1,0:T(8,128)(2,1)}, bf16[8,2432]{1,0:T(8,128)(2,1)S(1)}, u32[]{:S(2)}) copy-start(bf16[8,2432]{1,0:T(8,128)(2,1)S(1)} %collective-permute-done.1.refs_2_) | copy-start | bytes 116740
  15.5 4.0 %collective-permute-start.7 = (bf16[8,2432]{1,0:T(8,128)(2,1)S(1)}, bf16[8,2432]{1,0:T(8,128)(2,1)S(1)}, u32[]{:S(2)}, u32[]{:S(2)}) collective-permute-start(bf16[8,2432]{1,0:T(8,128)(2,1)S(1)} %collective-permute-done.1.refs_2_), channel_id=1, source_target_pairs={{0,2},{1,3},{2,0},{3,1},{4,6},{5,7},{6,4},{7,5},{8,10},{9,11},{10,... | collective-permute-start | bytes 116744 | tf_op jit(solution)/shard_map/ppermute | solution.py:249
  16.0 6.6 %copy-start.3 = (bf16[16,2432]{1,0:T(8,128)(2,1)}, bf16[16,2432]{1,0:T(8,128)(2,1)S(1)}, u32[]{:S(2)}) copy-start(bf16[16,2432]{1,0:T(8,128)(2,1)S(1)} %collective-permute-done.5.refs_6_) | copy-start | bytes 233476
  16.0 6.6 %collective-permute-start.8 = (bf16[16,2432]{1,0:T(8,128)(2,1)S(1)}, bf16[16,2432]{1,0:T(8,128)(2,1)S(1)}, u32[]{:S(2)}, u32[]{:S(2)}) collective-permute-start(bf16[16,2432]{1,0:T(8,128)(2,1)S(1)} %collective-permute-done.5.refs_6_), channel_id=1, source_target_pairs={{0,1},{1,0},{2,3},{3,2},{4,5},{5,4},{6,7},{7,6},{8,9},{9,8},{10,11... | collective-permute-start | bytes 233480 | tf_op jit(solution)/shard_map/ppermute | solution.py:249
  16.1 6.5 %copy-start.16 = (bf16[8,2432]{1,0:T(8,128)(2,1)}, bf16[8,2432]{1,0:T(8,128)(2,1)S(1)}, u32[]{:S(2)}) copy-start(bf16[8,2432]{1,0:T(8,128)(2,1)S(1)} %collective-permute-done.6.refs_7_) | copy-start | bytes 116740
  16.1 6.4 %collective-permute-start.4 = (bf16[8,2432]{1,0:T(8,128)(2,1)S(1)}, bf16[8,2432]{1,0:T(8,128)(2,1)S(1)}, u32[]{:S(2)}, u32[]{:S(2)}) collective-permute-start(bf16[8,2432]{1,0:T(8,128)(2,1)S(1)} %collective-permute-done.1.refs_2_), channel_id=1, source_target_pairs={{0,1},{1,0},{2,3},{3,2},{4,5},{5,4},{6,7},{7,6},{8,9},{9,8},{10,11... | collective-permute-start | bytes 116744 | tf_op jit(solution)/shard_map/ppermute | solution.py:249
  16.5 6.1 %copy-start.17 = (bf16[8,2432]{1,0:T(8,128)(2,1)}, bf16[8,2432]{1,0:T(8,128)(2,1)S(1)}, u32[]{:S(2)}) copy-start(bf16[8,2432]{1,0:T(8,128)(2,1)S(1)} %collective-permute-done.3.refs_4_) | copy-start | bytes 116740
  16.5 6.0 %collective-permute-start.9 = (bf16[8,2432]{1,0:T(8,128)(2,1)S(1)}, bf16[8,2432]{1,0:T(8,128)(2,1)S(1)}, u32[]{:S(2)}, u32[]{:S(2)}) collective-permute-start(bf16[8,2432]{1,0:T(8,128)(2,1)S(1)} %collective-permute-done.6.refs_7_), channel_id=1, source_target_pairs={{0,1},{1,0},{2,3},{3,2},{4,5},{5,4},{6,7},{7,6},{8,9},{9,8},{10,11... | collective-permute-start | bytes 116744 | tf_op jit(solution)/shard_map/ppermute | solution.py:249
  19.4 3.1 %collective-permute-start.10 = (bf16[8,2432]{1,0:T(8,128)(2,1)S(1)}, bf16[8,2432]{1,0:T(8,128)(2,1)S(1)}, u32[]{:S(2)}, u32[]{:S(2)}) collective-permute-start(bf16[8,2432]{1,0:T(8,128)(2,1)S(1)} %collective-permute-done.7.refs_8_), channel_id=1, source_target_pairs={{0,1},{1,0},{2,3},{3,2},{4,5},{5,4},{6,7},{7,6},{8,9},{9,8},{10,11... | collective-permute-start | bytes 116744 | tf_op jit(solution)/shard_map/ppermute | solution.py:249
  28.4 9.2 %collective-permute-start.16 = (bf16[16,3968]{1,0:T(8,128)(2,1)}, bf16[16,3968]{1,0:T(8,128)(2,1)S(1)}, u32[]{:S(2)}, u32[]{:S(2)}) collective-permute-start(bf16[16,3968]{1,0:T(8,128)(2,1)} %get-tuple-element.19.refs_0_), channel_id=1, source_target_pairs={{0,2},{1,3},{2,0},{3,1},{4,6},{5,7},{6,4},{7,5},{8,10},{9,11},{10,... | collective-permute-start | bytes 380936 | tf_op jit(solution)/shard_map/ppermute | solution.py:249
  28.9 4.5 %collective-permute-start.11 = (bf16[8,3968]{1,0:T(8,128)(2,1)}, bf16[8,3968]{1,0:T(8,128)(2,1)S(1)}, u32[]{:S(2)}, u32[]{:S(2)}) collective-permute-start(bf16[8,3968]{1,0:T(8,128)(2,1)} %get-tuple-element.20), channel_id=1, source_target_pairs={{0,4},{4,0},{8,12},{12,8},{16,20},{20,16},{24,28},{28,24},{1,5},{5... | collective-permute-start | bytes 190472 | tf_op jit(solution)/shard_map/ppermute | solution.py:240
  28.9 7.2 %collective-permute-start.12 = (bf16[8,3968]{1,0:T(8,128)(2,1)}, bf16[8,3968]{1,0:T(8,128)(2,1)S(1)}, u32[]{:S(2)}, u32[]{:S(2)}) collective-permute-start(bf16[8,3968]{1,0:T(8,128)(2,1)} %get-tuple-element.21), channel_id=1, source_target_pairs={{0,28},{4,8},{8,4},{12,16},{16,12},{20,24},{24,20},{28,0},{1,29},{... | collective-permute-start | bytes 190472 | tf_op jit(solution)/shard_map/ppermute | solution.py:240
  33.3 8.2 %copy-start.6 = (bf16[8,3968]{1,0:T(8,128)(2,1)}, bf16[8,3968]{1,0:T(8,128)(2,1)S(1)}, u32[]{:S(2)}) copy-start(bf16[8,3968]{1,0:T(8,128)(2,1)S(1)} %collective-permute-done.11.refs_1_) | copy-start | bytes 190468
  33.3 4.2 %collective-permute-start.17 = (bf16[8,3968]{1,0:T(8,128)(2,1)S(1)}, bf16[8,3968]{1,0:T(8,128)(2,1)S(1)}, u32[]{:S(2)}, u32[]{:S(2)}) collective-permute-start(bf16[8,3968]{1,0:T(8,128)(2,1)S(1)} %collective-permute-done.11.refs_1_), channel_id=1, source_target_pairs={{0,2},{1,3},{2,0},{3,1},{4,6},{5,7},{6,4},{7,5},{8,10},{9,11},{10,... | collective-permute-start | bytes 190472 | tf_op jit(solution)/shard_map/ppermute | solution.py:249
  34.9 5.4 %collective-permute-start.13 = (bf16[16,3968]{1,0:T(8,128)(2,1)}, bf16[16,3968]{1,0:T(8,128)(2,1)S(1)}, u32[]{:S(2)}, u32[]{:S(2)}) collective-permute-start(bf16[16,3968]{1,0:T(8,128)(2,1)} %get-tuple-element.19.refs_0_), channel_id=1, source_target_pairs={{0,1},{1,0},{2,3},{3,2},{4,5},{5,4},{6,7},{7,6},{8,9},{9,8},{10,11... | collective-permute-start | bytes 380936 | tf_op jit(solution)/shard_map/ppermute | solution.py:249
  34.9 3.2 %collective-permute-start.14 = (bf16[8,3968]{1,0:T(8,128)(2,1)S(1)}, bf16[8,3968]{1,0:T(8,128)(2,1)S(1)}, u32[]{:S(2)}, u32[]{:S(2)}) collective-permute-start(bf16[8,3968]{1,0:T(8,128)(2,1)S(1)} %collective-permute-done.11.refs_1_), channel_id=1, source_target_pairs={{0,1},{1,0},{2,3},{3,2},{4,5},{5,4},{6,7},{7,6},{8,9},{9,8},{10,11... | collective-permute-start | bytes 190472 | tf_op jit(solution)/shard_map/ppermute | solution.py:249
  36.0 5.5 %copy-start.7 = (bf16[8,3968]{1,0:T(8,128)(2,1)}, bf16[8,3968]{1,0:T(8,128)(2,1)S(1)}, u32[]{:S(2)}) copy-start(bf16[8,3968]{1,0:T(8,128)(2,1)S(1)} %collective-permute-done.12.refs_2_) | copy-start | bytes 190468
  36.0 4.2 %collective-permute-start.18 = (bf16[8,3968]{1,0:T(8,128)(2,1)S(1)}, bf16[8,3968]{1,0:T(8,128)(2,1)S(1)}, u32[]{:S(2)}, u32[]{:S(2)}) collective-permute-start(bf16[8,3968]{1,0:T(8,128)(2,1)S(1)} %collective-permute-done.12.refs_2_), channel_id=1, source_target_pairs={{0,2},{1,3},{2,0},{3,1},{4,6},{5,7},{6,4},{7,5},{8,10},{9,11},{10,... | collective-permute-start | bytes 190472 | tf_op jit(solution)/shard_map/ppermute | solution.py:249
  37.6 4.0 %copy-start = (bf16[16,3968]{1,0:T(8,128)(2,1)}, bf16[16,3968]{1,0:T(8,128)(2,1)S(1)}, u32[]{:S(2)}) copy-start(bf16[16,3968]{1,0:T(8,128)(2,1)S(1)} %collective-permute-done.16.refs_6_) | copy-start | bytes 380932
  37.6 4.0 %collective-permute-start.19 = (bf16[16,3968]{1,0:T(8,128)(2,1)S(1)}, bf16[16,3968]{1,0:T(8,128)(2,1)S(1)}, u32[]{:S(2)}, u32[]{:S(2)}) collective-permute-start(bf16[16,3968]{1,0:T(8,128)(2,1)S(1)} %collective-permute-done.16.refs_6_), channel_id=1, source_target_pairs={{0,1},{1,0},{2,3},{3,2},{4,5},{5,4},{6,7},{7,6},{8,9},{9,8},{10,11... | collective-permute-start | bytes 380936 | tf_op jit(solution)/shard_map/ppermute | solution.py:249
  37.6 4.0 %copy-start.8 = (bf16[8,3968]{1,0:T(8,128)(2,1)}, bf16[8,3968]{1,0:T(8,128)(2,1)S(1)}, u32[]{:S(2)}) copy-start(bf16[8,3968]{1,0:T(8,128)(2,1)S(1)} %collective-permute-done.17.refs_7_) | copy-start | bytes 190468
  37.6 2.7 %collective-permute-start.15 = (bf16[8,3968]{1,0:T(8,128)(2,1)S(1)}, bf16[8,3968]{1,0:T(8,128)(2,1)S(1)}, u32[]{:S(2)}, u32[]{:S(2)}) collective-permute-start(bf16[8,3968]{1,0:T(8,128)(2,1)S(1)} %collective-permute-done.12.refs_2_), channel_id=1, source_target_pairs={{0,1},{1,0},{2,3},{3,2},{4,5},{5,4},{6,7},{7,6},{8,9},{9,8},{10,11... | collective-permute-start | bytes 190472 | tf_op jit(solution)/shard_map/ppermute | solution.py:249
  38.1 3.5 %copy-start.9 = (bf16[8,3968]{1,0:T(8,128)(2,1)}, bf16[8,3968]{1,0:T(8,128)(2,1)S(1)}, u32[]{:S(2)}) copy-start(bf16[8,3968]{1,0:T(8,128)(2,1)S(1)} %collective-permute-done.14.refs_4_) | copy-start | bytes 190468
  38.1 2.2 %collective-permute-start.20 = (bf16[8,3968]{1,0:T(8,128)(2,1)S(1)}, bf16[8,3968]{1,0:T(8,128)(2,1)S(1)}, u32[]{:S(2)}, u32[]{:S(2)}) collective-permute-start(bf16[8,3968]{1,0:T(8,128)(2,1)S(1)} %collective-permute-done.17.refs_7_), channel_id=1, source_target_pairs={{0,1},{1,0},{2,3},{3,2},{4,5},{5,4},{6,7},{7,6},{8,9},{9,8},{10,11... | collective-permute-start | bytes 190472 | tf_op jit(solution)/shard_map/ppermute | solution.py:249
  40.3 1.3 %collective-permute-start.21 = (bf16[8,3968]{1,0:T(8,128)(2,1)S(1)}, bf16[8,3968]{1,0:T(8,128)(2,1)S(1)}, u32[]{:S(2)}, u32[]{:S(2)}) collective-permute-start(bf16[8,3968]{1,0:T(8,128)(2,1)S(1)} %collective-permute-done.18.refs_8_), channel_id=1, source_target_pairs={{0,1},{1,0},{2,3},{3,2},{4,5},{5,4},{6,7},{7,6},{8,9},{9,8},{10,11... | collective-permute-start | bytes 190472 | tf_op jit(solution)/shard_map/ppermute | solution.py:249
  (12 other events, 12.8 us)

commit v2 on v1

--- a/solution.py
+++ b/solution.py
@@ -15,6 +15,14 @@
 VMEM = pl.BlockSpec(memory_space=pltpu.VMEM)
 
 
+def near(*arrays):
+    return [pltpu.with_memory_space_constraint(array, pltpu.VMEM) for array in arrays]
+
+
+def away(*arrays):
+    return [pltpu.with_memory_space_constraint(array, pltpu.HBM) for array in arrays]
+
+
 def slot_index(degree, azimuth_order):
     return degree * degree + degree + azimuth_order
 
@@ -31,6 +39,11 @@
     return [slot for group in slot_groups(degrees) for slot in group]
 
 
+def unused_slots(coeffs):
+    order = slot_order(math.isqrt(coeffs))
+    return [slot for slot in range(coeffs) if slot not in order]
+
+
 def odd_slab():
     return lax.axis_index("slab") % 2 == 1
 
@@ -53,22 +66,31 @@
     return dot(hot.astype(BF16), rows, ((0,), (0,))).astype(BF16)
 
 
-def pack_kernel(emb_ref, low_ref, high_ref, own_ref, pair_ref, other_ref, wide):
-    atoms, coeffs, channels = emb_ref.shape
+def pack_kernel(emb_ref, low_ref, high_ref, own_ref, pair_ref, other_ref, rest_ref, lent_ref):
+    coeffs, atoms, channels = emb_ref.shape
     ghosts = low_ref.shape[1]
-    wide[...] = emb_ref[...].astype(F32)
-    for place, slot in enumerate(slot_order(math.isqrt(coeffs))):
-        own_ref[:, place * channels : (place + 1) * channels] = wide[:, slot, :].astype(BF16)
-    lent = lent_rows(lent_hot(low_ref, high_ref, atoms), own_ref[...])
+    order = slot_order(math.isqrt(coeffs))
+    for place, slot in enumerate(order):
+        own_ref[:, place * channels : (place + 1) * channels] = emb_ref[slot]
+    for place, slot in enumerate(unused_slots(coeffs)):
+        rest_ref[place] = emb_ref[slot]
+    hot = lent_hot(low_ref, high_ref, atoms)
+    lent_ref[...] = hot
+    lent = lent_rows(hot, own_ref[...])
     pair_ref[...] = lent[:ghosts]
     other_ref[...] = lent[ghosts:]
 
 
-def static_kernel(
+def scale_kernel(
     atoms, ghosts, slab_devices,
-    nbr_ref, valid_ref, azi_ref, pol_ref, dist_ref, rw_ref,
-    hot_ref, radial_ref, dirs_ref, pulls_ref,
+    nbr_ref, valid_ref, dist_ref, rw_ref, readout_ref, *refs,
 ):
+    count = (len(refs) - 5) // 2
+    far, (hot_ref, radial_ref, flags_ref, vector_ref), held = refs[:count], refs[count : count + 4], refs[count + 4 : -1]
+    sems = refs[-1]
+    copies = [pltpu.make_async_copy(far[i], held[i], sems.at[i]) for i in range(count)]
+    for copy in copies:
+        copy.start()
     layers, centers = rw_ref.shape[0], rw_ref.shape[1]
     nbr = nbr_ref[...]
     edges = nbr.shape[1]
@@ -88,22 +110,29 @@
     place = (device ^ me) * block + inner
     rows = lax.broadcasted_iota(jnp.int32, (slab_devices * block, edges), 0)
     hot = jnp.where((rows == place) & (valid_ref[...] != 0), 1.0, 0.0).astype(F32)
+    flags_ref[...] = hot
     hot_cols = jnp.transpose(hot).astype(BF16)
     hot_ref[...] = jnp.concatenate([hot_cols, hot_cols], axis=1)
     middle = 1.0 + 0.5 * lax.broadcasted_iota(jnp.int32, (centers, edges), 0).astype(F32)
     basis = jnp.exp(-jnp.square((dist_ref[...] - middle) / 0.5))
     for layer in range(layers):
         scale = dot(basis, rw_ref[layer], ((0,), (0,)), HIGHEST)
-        radial = scale / (1.0 + jnp.exp(-scale))
-        radial_ref[layer] = radial
+        radial_ref[layer] = scale / (1.0 + jnp.exp(-scale))
+    vector_ref[...] = 0.125 * readout_ref[...]
+    for copy in copies:
+        copy.wait()
+
+
+def pull_kernel(azi_ref, pol_ref, radial_ref, flags_ref, dirs_ref, pulls_ref):
     azimuth, polar = azi_ref[...], pol_ref[...]
     sin_polar = jnp.sin(polar)
     dirs = [sin_polar * jnp.cos(azimuth), sin_polar * jnp.sin(azimuth), jnp.cos(polar)]
     dirs_ref[...] = jnp.concatenate(dirs, axis=0)
-    channels = rw_ref.shape[2]
+    radial = radial_ref[radial_ref.shape[0] - 1]
+    channels = radial.shape[1]
     for axis, along in enumerate(dirs):
         pulls_ref[:, axis * channels : (axis + 1) * channels] = dot(
-            hot * along, radial, precision=HIGHEST
+            flags_ref[...] * along, radial, precision=HIGHEST
         ).astype(BF16)
 
 
@@ -158,7 +187,7 @@
 
 def first_kernel(
     layer, last, degrees, channels, count,
-    low_ref, high_ref, hot_ref, radial_ref, pulls_ref, *refs,
+    lent_ref, hot_ref, radial_ref, pulls_ref, *refs,
 ):
     tables, weights = refs[:count], refs[count : count + 5]
     own_ref, pair_ref, other_ref = refs[count + 5 : count + 8]
@@ -167,12 +196,12 @@
         layer, degrees, channels, tables, weights, hot_ref, radial_ref, scratch
     )
     atoms = tables[0].shape[0]
-    ghosts = low_ref.shape[1]
+    ghosts = lent_ref.shape[1] // 2
     width = len(sums) * channels
     for place, total in enumerate(sums):
         cols = slice(place * channels, (place + 1) * channels)
         own_ref[:, cols] = (tables[0][:, cols].astype(F32) + 0.18 * total).astype(BF16)
-    lent = lent_rows(lent_hot(low_ref, high_ref, atoms), own_ref[:, :width])
+    lent = lent_rows(lent_ref[...], own_ref[:, :width])
     pair_ref[:, :width] = lent[:ghosts]
     other_ref[:, :width] = lent[ghosts:]
     if last:
@@ -188,23 +217,23 @@
 
 def last_kernel(
     layer, degrees, channels, count,
-    emb_ref, low_ref, high_ref, hot_ref, radial_ref, dirs_ref, readout_ref, *refs,
+    rest_ref, lent_ref, hot_ref, radial_ref, dirs_ref, readout_ref, *refs,
 ):
     tables, weights = refs[:count], refs[count : count + 5]
     out_ref, force_ref = refs[count + 5 : count + 7]
-    joined, mixed, wide = refs[count + 7 :]
+    scratch = refs[count + 7 :]
     sums, first, zero = layer_sums(
-        layer, degrees, channels, tables, weights, hot_ref, radial_ref, (joined, mixed)
+        layer, degrees, channels, tables, weights, hot_ref, radial_ref, scratch
     )
     atoms = tables[0].shape[0]
-    ghosts = low_ref.shape[1]
-    wide[...] = emb_ref[...].astype(F32)
-    for place, slot in enumerate(slot_order(degrees)):
+    order = slot_order(degrees)
+    for place, slot in enumerate(order):
         cols = slice(place * channels, (place + 1) * channels)
-        wide[:, slot, :] = tables[0][:, cols].astype(F32) + 0.18 * sums[place]
-    out_ref[...] = wide[...].astype(BF16)
-
-    readout = 0.125 * readout_ref[...]
+        out_ref[slot] = (tables[0][:, cols].astype(F32) + 0.18 * sums[place]).astype(BF16)
+    for place, slot in enumerate(unused_slots(degrees * degrees)):
+        out_ref[slot] = rest_ref[place]
+
+    readout = readout_ref[...]
     strength = dot(readout, first, ((1,), (1,)), HIGHEST)
     pull = dirs_ref[...] * strength
     edges = pull.shape[1]
@@ -221,7 +250,7 @@
             ref = tables[3 * slot + kind]
             kinds[kind] += ref[:, width + slot * part : width + (slot + 1) * part].astype(F32)
     lent = jnp.concatenate(kinds[1:], axis=0)
-    pulls = kinds[0] + dot(lent_hot(low_ref, high_ref, atoms), lent, precision=HIGHEST)
+    pulls = kinds[0] + dot(lent_ref[...], lent, precision=HIGHEST)
     mine = zero[:atoms, :channels] * readout
     ones = jnp.ones((1, channels), F32)
     for axis in range(3):
@@ -231,7 +260,7 @@
         force_ref[axis : axis + 1, :] = own_force[axis : axis + 1] - back
 
 
-def exchange(own, pair, other, slabs, slab_devices):
+def exchange(own, pair, other, slabs, slab_devices, between=()):
     def toward(block, step):
         route = []
         for slab in range(slabs):
@@ -241,6 +270,8 @@
 
     got_other = toward(other, -1)
     got_pair = toward(pair, 1)
+    if between:
+        got_pair, *between = lax.optimization_barrier((got_pair, *between))
     held = {0: (own, got_pair, got_other)}
     bit = slab_devices // 2
     while bit:
@@ -248,7 +279,7 @@
         for slot in sorted(held):
             held[slot | bit] = tuple(lax.ppermute(block, "yz", route) for block in held[slot])
         bit //= 2
-    return [block for slot in range(slab_devices) for block in held[slot]]
+    return [block for slot in range(slab_devices) for block in held[slot]], between
 
 
 def body(
@@ -264,59 +295,79 @@
     rows = slab_devices * (atoms + 2 * ghosts)
     width = len(slot_order(degrees)) * channels
     low, high = send_low.reshape(1, -1), send_high.reshape(1, -1)
-    shape = jax.ShapeDtypeStruct
-
-    own, pair, other = pl.pallas_call(
+    held, shape = pltpu.VMEM, jax.ShapeDtypeStruct
+    embeddings = embeddings.transpose(1, 0, 2)
+    params = pltpu.CompilerParams(vmem_limit_bytes=20 * 2**20)
+    row = lambda value: value.reshape(1, -1)
+    far = pl.BlockSpec(memory_space=pl.ANY)
+
+    own, pair, other, rest, lent = pl.pallas_call(
         pack_kernel,
         out_shape=[
-            shape((atoms, width), BF16), shape((ghosts, width), BF16), shape((ghosts, width), BF16)
+            held((atoms, width), BF16), held((ghosts, width), BF16), held((ghosts, width), BF16),
+            held((len(unused_slots(coeffs)), atoms, channels), BF16), held((atoms, 2 * ghosts), F32),
         ],
         in_specs=[VMEM] * 3,
-        out_specs=[VMEM] * 3,
-        scratch_shapes=[pltpu.VMEM((atoms, coeffs, channels), F32)],
+        out_specs=[VMEM] * 5,
+        compiler_params=params,
         name="pack",
-    )(embeddings, low, high)
-
-    row = lambda value: value.reshape(1, -1)
-    hot, radial, dirs, pulls = pl.pallas_call(
-        functools.partial(static_kernel, atoms, ghosts, slab_devices),
+    )(*away(embeddings, low, high))
+
+    weights = (w_zero, w_one_re, w_one_im, w_two_re, w_two_im)
+    hot, radial, flags, vector, *weights = pl.pallas_call(
+        functools.partial(scale_kernel, atoms, ghosts, slab_devices),
         out_shape=[
-            shape((edges, 2 * rows), BF16), shape((layers, edges, channels), F32),
-            shape((3, edges), F32), shape((rows, 3 * channels), BF16),
+            held((edges, 2 * rows), BF16), held((layers, edges, channels), F32),
+            held((rows, edges), F32), held((1, channels), F32),
+            *(held(array.shape, array.dtype) for array in weights),
         ],
-        in_specs=[VMEM] * 6,
-        out_specs=[VMEM] * 4,
-        name="geometry",
-    )(row(neighbours), row(valid), row(azimuth), row(polar), row(distance), radial_weight)
-
-    weights = (w_zero, w_one_re, w_one_im, w_two_re, w_two_im)
+        in_specs=[VMEM] * 5 + [far] * len(weights),
+        out_specs=[VMEM] * (4 + len(weights)),
+        scratch_shapes=[pltpu.SemaphoreType.DMA((len(weights),))],
+        compiler_params=params,
+        name="scales",
+    )(*away(*map(row, (neighbours, valid, distance)), radial_weight, row(readout), *weights))
+    dirs, pulls = pl.pallas_call(
+        pull_kernel,
+        out_shape=[held((3, edges), F32), held((rows, 3 * channels), BF16)],
+        in_specs=[VMEM] * 4,
+        out_specs=[VMEM] * 2,
+        compiler_params=params,
+        name="pulls",
+    )(*away(row(azimuth), row(polar)), *near(radial, flags))
+
     scratch = [pltpu.VMEM((rows, width), F32), pltpu.VMEM((2 * rows, width), BF16)]
+    between = (hot, radial)
     for layer in range(layers):
-        tables = exchange(own, pair, other, slabs, slab_devices)
+        tables, between = exchange(own, pair, other, slabs, slab_devices, between)
+        if layer == 0:
+            hot, radial = between
+            between = ()
         if layer < layers - 1:
             last = layer == layers - 2
             wide = width + (slab_devices * 3 * channels if last else 0)
             own, pair, other = pl.pallas_call(
                 functools.partial(first_kernel, layer, last, degrees, channels, len(tables)),
                 out_shape=[
-                    shape((atoms, wide), BF16), shape((ghosts, wide), BF16),
-                    shape((ghosts, wide), BF16),
+                    held((atoms, wide), BF16), held((ghosts, wide), BF16), held((ghosts, wide), BF16)
                 ],
-                in_specs=[VMEM] * (5 + len(tables) + len(weights)),
+                in_specs=[VMEM] * (4 + len(tables) + len(weights)),
                 out_specs=[VMEM] * 3,
                 scratch_shapes=scratch,
+                compiler_params=params,
                 name="layer",
-            )(low, high, hot, radial, pulls, *tables, *weights)
+            )(*near(lent, hot, radial, pulls, *tables, *weights))
         else:
             updated, forces = pl.pallas_call(
                 functools.partial(last_kernel, layer, degrees, channels, len(tables)),
-                out_shape=[shape((atoms, coeffs, channels), BF16), shape((3, atoms), F32)],
-                in_specs=[VMEM] * (7 + len(tables) + len(weights)),
+                out_shape=[shape((coeffs, atoms, channels), BF16), shape((3, atoms), F32)],
+                in_specs=[VMEM] * (6 + len(tables) + len(weights)),
                 out_specs=[VMEM] * 2,
-                scratch_shapes=scratch + [pltpu.VMEM((atoms, coeffs, channels), F32)],
+                scratch_shapes=scratch,
+                compiler_params=params,
                 name="last_layer",
-            )(embeddings, low, high, hot, radial, dirs, readout.reshape(1, -1), *tables, *weights)
-    return (updated, forces)
+            )(*near(rest, lent, hot, radial, dirs, vector, *tables, *weights))
+    return (updated.transpose(1, 0, 2), forces)
 
 
 def solution(mesh):

time: 49.9 us -> 39.7 us (0.80)
  Pallas kernels: 16 us -> 10.4 us
  local copies, waits for them, and re-layouts: 4.37 us -> 0 us
  starting transfers between devices: 18.3 us -> 17.4 us
  waiting for transfers between devices: 10.1 us -> 11 us
    pallas_call x1, Pallas kernels: 5.17 us -> 1.71 us  [body(): pl.pallas_call(functools.partial(first_kernel, layer, last, degrees, chan...]
    pallas_call x1, Pallas kernels: 5.88 us -> 2.7 us  [body(): pl.pallas_call(functools.partial(last_kernel, layer, degrees, channels, l...]
    unnamed x45 -> x0, local copies, waits for them, and re-layouts: 2.78 us -> none
    pallas_call x1 -> x0, local copies, waits for them, and re-layouts: 1.59 us -> none  [body(): pl.pallas_call(functools.partial(last_kernel, layer, degrees, channels, l...]
    pallas_call x2 -> x3, Pallas kernels: 4.92 us -> 6 us  [the longest x1 3.27 us: body(): pl.pallas_call(functools.partial(scale_kernel, atoms, ghosts, slab_device...]
    ppermute x4, starting transfers between devices: 8.64 us -> 7.63 us  [toward(): return lax.ppermute(block, 'slab', route)]
    ppermute x4, waiting for transfers between devices: 3.84 us -> 4.75 us  [toward(): return lax.ppermute(block, 'slab', route)]
  transfers between devices with their start and end apart: 22 -> 22, of which waited for: 7 -> 7; matrix products, arithmetic and copies ran while one was open for 0% -> 0% of each run, Pallas kernels for 6% -> 12%
where the time goes in v2:
time: 39.7 us; the launch traced here: 39.5 us
  starting transfers between devices  17.4 us (44%)
  waiting for transfers between devices  11 us (28%)
  Pallas kernels  10.4 us (26%)
  between operations  0.73 us (2%)
    ppermute x18, starting transfers between devices, exchange(): lax.ppermute(block, 'yz', route)  9.75 us
    ppermute x4, starting transfers between devices, toward(): return lax.ppermute(block, 'slab', route)  7.63 us
    ppermute x18, waiting for transfers between devices, exchange(): lax.ppermute(block, 'yz', route)  6.23 us
    ppermute x4, waiting for transfers between devices, toward(): return lax.ppermute(block, 'slab', route)  4.75 us
    pallas_call x1, Pallas kernels, body(): pl.pallas_call(functools.partial(scale_kernel, atoms, ghosts, slab_device...  3.27 us
    pallas_call x1, Pallas kernels, body(): pl.pallas_call(functools.partial(last_kernel, layer, degrees, channels, l...  2.7 us
    pallas_call x1, Pallas kernels, body(): pl.pallas_call(functools.partial(first_kernel, layer, last, degrees, chan...  1.71 us
    pallas_call x1, Pallas kernels, body(): pl.pallas_call(pull_kernel, out_shape=[held((3, edges), F32), held((rows,...  1.53 us
  transfers between devices with their start and end apart: 22, of which 7 were waited for; matrix products, arithmetic and copies ran while one was open for 0% of the time, Pallas kernels for 12%

profile of v2, /device:TPU:0, one launch (start us, length us, event | category | flops | bytes accessed | tf_op | source)
XLA Modules:
  0.0 39.5 jit_solution(11268220010642079729)
XLA Ops:
  0.6 1.2 %pack.1 = (bf16[16,2432]{1,0:T(8,128)(2,1)S(1)}, bf16[8,2432]{1,0:T(8,128)(2,1)S(1)}, bf16[8,2432]{1,0:T(8,128)(2,1)S(1)}, bf16[6,16,128]{2,1,0:T(8,128)(2,1)S(1)}, f32[16,16]{1,0:T(8,128)S(1)}) custom-call(bf16[25,16,128]{2,1,0:T(8,128)(2,1)} %bitcast.10, s32[1,8]{1,0:T(1,128)} %bitcast.16, s32[1,8]{1,0:T(1,128)} %bitcast.17), custom_call_target="tpu_custom_call" | custom-call | tf_op jit(solution)/shard_map/pack/pallas_call | solution.py:304
  1.8 3.1 %collective-permute-start.5 = (bf16[16,2432]{1,0:T(8,128)(2,1)S(1)}, bf16[16,2432]{1,0:T(8,128)(2,1)S(1)}, u32[]{:S(2)}, u32[]{:S(2)}) collective-permute-start(bf16[16,2432]{1,0:T(8,128)(2,1)S(1)} %get-tuple-element.37.refs_0_), channel_id=1, source_target_pairs={{0,2},{1,3},{2,0},{3,1},{4,6},{5,7},{6,4},{7,5},{8,10},{9,11},{10,... | collective-permute-start | bytes 233480 | tf_op jit(solution)/shard_map/ppermute | solution.py:280
  4.9 4.5 %collective-permute-start.1 = (bf16[8,2432]{1,0:T(8,128)(2,1)S(1)}, bf16[8,2432]{1,0:T(8,128)(2,1)S(1)}, u32[]{:S(2)}, u32[]{:S(2)}) collective-permute-start(bf16[8,2432]{1,0:T(8,128)(2,1)S(1)} %get-tuple-element.39), channel_id=1, source_target_pairs={{0,28},{4,8},{8,4},{12,16},{16,12},{20,24},{24,20},{28,0},{1,29},{... | collective-permute-start | bytes 116744 | tf_op jit(solution)/shard_map/ppermute | solution.py:269
  9.4 0.0 collective-permute-start
  9.4 0.0 collective-permute-start.2
  9.4 3.3 %scales.1 = (bf16[512,256]{1,0:T(8,128)(2,1)S(1)}, f32[2,512,128]{2,1,0:T(8,128)S(1)}, f32[128,512]{1,0:T(8,128)S(1)}, f32[1,128]{1,0:T(1,128)S(1)}, bf16[2,640,...) custom-call(s32[1,512]{1,0:T(1,128)} %bitcast.11, ...), custom_call_target="tpu_custom_call" | custom-call | tf_op jit(solution)/shard_map/scales/pallas_call | solution.py:317
  12.7 0.0 collective-permute-done.1.refs_2_
  12.7 0.6 %collective-permute-start.7 = (bf16[8,2432]{1,0:T(8,128)(2,1)S(1)}, bf16[8,2432]{1,0:T(8,128)(2,1)S(1)}, u32[]{:S(2)}, u32[]{:S(2)}) collective-permute-start(bf16[8,2432]{1,0:T(8,128)(2,1)S(1)} %collective-permute-done.1.refs_2_), channel_id=1, source_target_pairs={{0,2},{1,3},{2,0},{3,1},{4,6},{5,7},{6,4},{7,5},{8,10},{9,11},{10,... | collective-permute-start | bytes 116744 | tf_op jit(solution)/shard_map/ppermute | solution.py:280
  13.3 0.1 collective-permute-done.refs_1_
  13.4 0.1 collective-permute-start.4
  13.5 1.5 %collective-permute-start.6 = (bf16[8,2432]{1,0:T(8,128)(2,1)S(1)}, bf16[8,2432]{1,0:T(8,128)(2,1)S(1)}, u32[]{:S(2)}, u32[]{:S(2)}) collective-permute-start(bf16[8,2432]{1,0:T(8,128)(2,1)S(1)} %collective-permute-done.refs_1_), channel_id=1, source_target_pairs={{0,2},{1,3},{2,0},{3,1},{4,6},{5,7},{6,4},{7,5},{8,10},{9,11},{10,... | collective-permute-start | bytes 116744 | tf_op jit(solution)/shard_map/ppermute | solution.py:280
  15.0 0.0 collective-permute-done.5.refs_6_
  15.0 0.0 collective-permute-start.8
  15.0 2.0 %collective-permute-done.7.refs_8_ = bf16[8,2432]{1,0:T(8,128)(2,1)S(1)} collective-permute-done((bf16[8,2432]{1,0:T(8,128)(2,1)S(1)}, bf16[8,2432]{1,0:T(8,128)(2,1)S(1)}, u32[]{:S(2)}, u32[]{:S(2)}) %collective-permute-start.7) | collective-permute-done | bytes 38944 | tf_op jit(solution)/shard_map/ppermute | solution.py:280
  17.0 0.5 %collective-permute-start.10 = (bf16[8,2432]{1,0:T(8,128)(2,1)S(1)}, bf16[8,2432]{1,0:T(8,128)(2,1)S(1)}, u32[]{:S(2)}, u32[]{:S(2)}) collective-permute-start(bf16[8,2432]{1,0:T(8,128)(2,1)S(1)} %collective-permute-done.7.refs_8_), channel_id=1, source_target_pairs={{0,1},{1,0},{2,3},{3,2},{4,5},{5,4},{6,7},{7,6},{8,9},{9,8},{10,11... | collective-permute-start | bytes 116744 | tf_op jit(solution)/shard_map/ppermute | solution.py:280
  17.5 0.1 collective-permute-done.6.refs_7_
  17.6 0.0 collective-permute-start.9
  17.6 1.5 %pulls.1 = (f32[3,512]{1,0:T(4,128)S(1)}, bf16[128,384]{1,0:T(8,128)(2,1)S(1)}) custom-call(f32[1,512]{1,0:T(1,128)} %bitcast.14, f32[1,512]{1,0:T(1,128)} %bitcast.15, f32[2,512,128]{2,1,0:T(8,128)S(1)} %get-tuple-element.32.radial_ref, f32[128,512]{1,0:T(8,128)S(1)} %get-tuple-element.33.flags_ref), custom_call_target="tpu_custom_call" | custom-call | tf_op jit(solution)/shard_map/pulls/pallas_call | solution.py:330
  19.2 1.7 %layer.1 = (bf16[16,3968]{1,0:T(8,128)(2,1)S(1)}, bf16[8,3968]{1,0:T(8,128)(2,1)S(1)}, bf16[8,3968]{1,0:T(8,128)(2,1)S(1)}) custom-call(f32[16,16]{1,0:T(8,128)S(1)} %get-tuple-element.27.lent_ref, bf16[512,256]{1,0:T(8,128)(2,1)S(1)} %get-tuple-element.31.hot_ref, f32[2,512,128]{2,1,0:T(8,128)S(1)} %get-tuple-element.32.radial_ref, ...), custom_call_target="tpu_custom_call" | custom-call | tf_op jit(solution)/shard_map/layer/pallas_call | solution.py:349
  20.9 1.4 %collective-permute-start.16 = (bf16[16,3968]{1,0:T(8,128)(2,1)S(1)}, bf16[16,3968]{1,0:T(8,128)(2,1)S(1)}, u32[]{:S(2)}, u32[]{:S(2)}) collective-permute-start(bf16[16,3968]{1,0:T(8,128)(2,1)S(1)} %get-tuple-element.45.refs_0_), channel_id=1, source_target_pairs={{0,2},{1,3},{2,0},{3,1},{4,6},{5,7},{6,4},{7,5},{8,10},{9,11},{10,... | collective-permute-start | bytes 380936 | tf_op jit(solution)/shard_map/ppermute | solution.py:280
  22.3 2.0 %collective-permute-start.11 = (bf16[8,3968]{1,0:T(8,128)(2,1)S(1)}, bf16[8,3968]{1,0:T(8,128)(2,1)S(1)}, u32[]{:S(2)}, u32[]{:S(2)}) collective-permute-start(bf16[8,3968]{1,0:T(8,128)(2,1)S(1)} %get-tuple-element.46), channel_id=1, source_target_pairs={{0,4},{4,0},{8,12},{12,8},{16,20},{20,16},{24,28},{28,24},{1,5},{5... | collective-permute-start | bytes 190472 | tf_op jit(solution)/shard_map/ppermute | solution.py:269
  24.4 1.1 %collective-permute-start.12 = (bf16[8,3968]{1,0:T(8,128)(2,1)S(1)}, bf16[8,3968]{1,0:T(8,128)(2,1)S(1)}, u32[]{:S(2)}, u32[]{:S(2)}) collective-permute-start(bf16[8,3968]{1,0:T(8,128)(2,1)S(1)} %get-tuple-element.47), channel_id=1, source_target_pairs={{0,28},{4,8},{8,4},{12,16},{16,12},{20,24},{24,20},{28,0},{1,29},{... | collective-permute-start | bytes 190472 | tf_op jit(solution)/shard_map/ppermute | solution.py:269
  25.4 2.1 %collective-permute-done.11.refs_1_ = bf16[8,3968]{1,0:T(8,128)(2,1)S(1)} collective-permute-done((bf16[8,3968]{1,0:T(8,128)(2,1)S(1)}, bf16[8,3968]{1,0:T(8,128)(2,1)S(1)}, u32[]{:S(2)}, u32[]{:S(2)}) %collective-permute-start.11) | collective-permute-done | bytes 63520 | tf_op jit(solution)/shard_map/ppermute | solution.py:269
  27.5 0.7 %collective-permute-start.17 = (bf16[8,3968]{1,0:T(8,128)(2,1)S(1)}, bf16[8,3968]{1,0:T(8,128)(2,1)S(1)}, u32[]{:S(2)}, u32[]{:S(2)}) collective-permute-start(bf16[8,3968]{1,0:T(8,128)(2,1)S(1)} %collective-permute-done.11.refs_1_), channel_id=1, source_target_pairs={{0,2},{1,3},{2,0},{3,1},{4,6},{5,7},{6,4},{7,5},{8,10},{9,11},{10,... | collective-permute-start | bytes 190472 | tf_op jit(solution)/shard_map/ppermute | solution.py:280
  28.2 0.5 %collective-permute-start.14 = (bf16[8,3968]{1,0:T(8,128)(2,1)S(1)}, bf16[8,3968]{1,0:T(8,128)(2,1)S(1)}, u32[]{:S(2)}, u32[]{:S(2)}) collective-permute-start(bf16[8,3968]{1,0:T(8,128)(2,1)S(1)} %collective-permute-done.11.refs_1_), channel_id=1, source_target_pairs={{0,1},{1,0},{2,3},{3,2},{4,5},{5,4},{6,7},{7,6},{8,9},{9,8},{10,11... | collective-permute-start | bytes 190472 | tf_op jit(solution)/shard_map/ppermute | solution.py:280
  28.7 2.6 %collective-permute-done.12.refs_2_ = bf16[8,3968]{1,0:T(8,128)(2,1)S(1)} collective-permute-done((bf16[8,3968]{1,0:T(8,128)(2,1)S(1)}, bf16[8,3968]{1,0:T(8,128)(2,1)S(1)}, u32[]{:S(2)}, u32[]{:S(2)}) %collective-permute-start.12) | collective-permute-done | bytes 63520 | tf_op jit(solution)/shard_map/ppermute | solution.py:269
  31.3 0.7 %collective-permute-start.18 = (bf16[8,3968]{1,0:T(8,128)(2,1)S(1)}, bf16[8,3968]{1,0:T(8,128)(2,1)S(1)}, u32[]{:S(2)}, u32[]{:S(2)}) collective-permute-start(bf16[8,3968]{1,0:T(8,128)(2,1)S(1)} %collective-permute-done.12.refs_2_), channel_id=1, source_target_pairs={{0,2},{1,3},{2,0},{3,1},{4,6},{5,7},{6,4},{7,5},{8,10},{9,11},{10,... | collective-permute-start | bytes 190472 | tf_op jit(solution)/shard_map/ppermute | solution.py:280
  32.0 0.5 %collective-permute-start.15 = (bf16[8,3968]{1,0:T(8,128)(2,1)S(1)}, bf16[8,3968]{1,0:T(8,128)(2,1)S(1)}, u32[]{:S(2)}, u32[]{:S(2)}) collective-permute-start(bf16[8,3968]{1,0:T(8,128)(2,1)S(1)} %collective-permute-done.12.refs_2_), channel_id=1, source_target_pairs={{0,1},{1,0},{2,3},{3,2},{4,5},{5,4},{6,7},{7,6},{8,9},{9,8},{10,11... | collective-permute-start | bytes 190472 | tf_op jit(solution)/shard_map/ppermute | solution.py:280
  32.5 0.1 collective-permute-start.20
  32.6 2.9 %collective-permute-done.18.refs_8_ = bf16[8,3968]{1,0:T(8,128)(2,1)S(1)} collective-permute-done((bf16[8,3968]{1,0:T(8,128)(2,1)S(1)}, bf16[8,3968]{1,0:T(8,128)(2,1)S(1)}, u32[]{:S(2)}, u32[]{:S(2)}) %collective-permute-start.18) | collective-permute-done | bytes 63520 | tf_op jit(solution)/shard_map/ppermute | solution.py:280
  35.6 1.2 %collective-permute-done.21.refs_11_ = bf16[8,3968]{1,0:T(8,128)(2,1)S(1)} collective-permute-done((bf16[8,3968]{1,0:T(8,128)(2,1)S(1)}, bf16[8,3968]{1,0:T(8,128)(2,1)S(1)}, u32[]{:S(2)}, u32[]{:S(2)}) %collective-permute-start.21) | collective-permute-done | bytes 63520 | tf_op jit(solution)/shard_map/ppermute | solution.py:280
  36.8 2.7 %last_layer.1 = (bf16[25,16,128]{2,1,0:T(8,128)(2,1)}, f32[3,16]{1,0:T(4,128)}) custom-call(bf16[6,16,128]{2,1,0:T(8,128)(2,1)S(1)} %get-tuple-element.26.rest_ref, f32[16,16]{1,0:T(8,128)S(1)} %get-tuple-element.27.lent_ref, bf16[512,256]{1,0:T(8,128)(2,1)S(1)} %get-tuple-element.31.hot_ref, f32[2,512,128]{2,1,0:T(8,128)S(1)} %get-tuple-element.32.radial_ref, ...), custom_call_target="tpu_custom_call" | custom-call | tf_op jit(solution)/shard_map/last_layer/pallas_call | solution.py:361
  (17 shorter events, 0.0 us)
Async XLA Ops:
  1.8 13.2 %collective-permute-start.5 = (bf16[16,2432]{1,0:T(8,128)(2,1)S(1)}, bf16[16,2432]{1,0:T(8,128)(2,1)S(1)}, u32[]{:S(2)}, u32[]{:S(2)}) collective-permute-start(bf16[16,2432]{1,0:T(8,128)(2,1)S(1)} %get-tuple-element.37.refs_0_), channel_id=1, source_target_pairs={{0,2},{1,3},{2,0},{3,1},{4,6},{5,7},{6,4},{7,5},{8,10},{9,11},{10,... | collective-permute-start | bytes 233480 | tf_op jit(solution)/shard_map/ppermute | solution.py:280
  4.9 7.8 %collective-permute-start.1 = (bf16[8,2432]{1,0:T(8,128)(2,1)S(1)}, bf16[8,2432]{1,0:T(8,128)(2,1)S(1)}, u32[]{:S(2)}, u32[]{:S(2)}) collective-permute-start(bf16[8,2432]{1,0:T(8,128)(2,1)S(1)} %get-tuple-element.39), channel_id=1, source_target_pairs={{0,28},{4,8},{8,4},{12,16},{16,12},{20,24},{24,20},{28,0},{1,29},{... | collective-permute-start | bytes 116744 | tf_op jit(solution)/shard_map/ppermute | solution.py:269
  9.4 4.0 %collective-permute-start = (bf16[8,2432]{1,0:T(8,128)(2,1)S(1)}, bf16[8,2432]{1,0:T(8,128)(2,1)S(1)}, u32[]{:S(2)}, u32[]{:S(2)}) collective-permute-start(bf16[8,2432]{1,0:T(8,128)(2,1)S(1)} %get-tuple-element.28), channel_id=1, source_target_pairs={{0,4},{4,0},{8,12},{12,8},{16,20},{20,16},{24,28},{28,24},{1,5},{5... | collective-permute-start | bytes 116744 | tf_op jit(solution)/shard_map/ppermute | solution.py:269
  9.4 9.7 %collective-permute-start.2 = (bf16[16,2432]{1,0:T(8,128)(2,1)S(1)}, bf16[16,2432]{1,0:T(8,128)(2,1)S(1)}, u32[]{:S(2)}, u32[]{:S(2)}) collective-permute-start(bf16[16,2432]{1,0:T(8,128)(2,1)S(1)} %get-tuple-element.37.refs_0_), channel_id=1, source_target_pairs={{0,1},{1,0},{2,3},{3,2},{4,5},{5,4},{6,7},{7,6},{8,9},{9,8},{10,11... | collective-permute-start | bytes 233480 | tf_op jit(solution)/shard_map/ppermute | solution.py:280
  12.7 4.3 %collective-permute-start.7 = (bf16[8,2432]{1,0:T(8,128)(2,1)S(1)}, bf16[8,2432]{1,0:T(8,128)(2,1)S(1)}, u32[]{:S(2)}, u32[]{:S(2)}) collective-permute-start(bf16[8,2432]{1,0:T(8,128)(2,1)S(1)} %collective-permute-done.1.refs_2_), channel_id=1, source_target_pairs={{0,2},{1,3},{2,0},{3,1},{4,6},{5,7},{6,4},{7,5},{8,10},{9,11},{10,... | collective-permute-start | bytes 116744 | tf_op jit(solution)/shard_map/ppermute | solution.py:280
  13.4 3.6 %collective-permute-start.4 = (bf16[8,2432]{1,0:T(8,128)(2,1)S(1)}, bf16[8,2432]{1,0:T(8,128)(2,1)S(1)}, u32[]{:S(2)}, u32[]{:S(2)}) collective-permute-start(bf16[8,2432]{1,0:T(8,128)(2,1)S(1)} %collective-permute-done.1.refs_2_), channel_id=1, source_target_pairs={{0,1},{1,0},{2,3},{3,2},{4,5},{5,4},{6,7},{7,6},{8,9},{9,8},{10,11... | collective-permute-start | bytes 116744 | tf_op jit(solution)/shard_map/ppermute | solution.py:280
  13.5 4.1 %collective-permute-start.6 = (bf16[8,2432]{1,0:T(8,128)(2,1)S(1)}, bf16[8,2432]{1,0:T(8,128)(2,1)S(1)}, u32[]{:S(2)}, u32[]{:S(2)}) collective-permute-start(bf16[8,2432]{1,0:T(8,128)(2,1)S(1)} %collective-permute-done.refs_1_), channel_id=1, source_target_pairs={{0,2},{1,3},{2,0},{3,1},{4,6},{5,7},{6,4},{7,5},{8,10},{9,11},{10,... | collective-permute-start | bytes 116744 | tf_op jit(solution)/shard_map/ppermute | solution.py:280
  15.0 4.1 %collective-permute-start.8 = (bf16[16,2432]{1,0:T(8,128)(2,1)S(1)}, bf16[16,2432]{1,0:T(8,128)(2,1)S(1)}, u32[]{:S(2)}, u32[]{:S(2)}) collective-permute-start(bf16[16,2432]{1,0:T(8,128)(2,1)S(1)} %collective-permute-done.5.refs_6_), channel_id=1, source_target_pairs={{0,1},{1,0},{2,3},{3,2},{4,5},{5,4},{6,7},{7,6},{8,9},{9,8},{10,11... | collective-permute-start | bytes 233480 | tf_op jit(solution)/shard_map/ppermute | solution.py:280
  17.0 2.1 %collective-permute-start.3 = (bf16[8,2432]{1,0:T(8,128)(2,1)S(1)}, bf16[8,2432]{1,0:T(8,128)(2,1)S(1)}, u32[]{:S(2)}, u32[]{:S(2)}) collective-permute-start(bf16[8,2432]{1,0:T(8,128)(2,1)S(1)} %collective-permute-done.refs_1_), channel_id=1, source_target_pairs={{0,1},{1,0},{2,3},{3,2},{4,5},{5,4},{6,7},{7,6},{8,9},{9,8},{10,11... | collective-permute-start | bytes 116744 | tf_op jit(solution)/shard_map/ppermute | solution.py:280
  17.0 2.1 %collective-permute-start.10 = (bf16[8,2432]{1,0:T(8,128)(2,1)S(1)}, bf16[8,2432]{1,0:T(8,128)(2,1)S(1)}, u32[]{:S(2)}, u32[]{:S(2)}) collective-permute-start(bf16[8,2432]{1,0:T(8,128)(2,1)S(1)} %collective-permute-done.7.refs_8_), channel_id=1, source_target_pairs={{0,1},{1,0},{2,3},{3,2},{4,5},{5,4},{6,7},{7,6},{8,9},{9,8},{10,11... | collective-permute-start | bytes 116744 | tf_op jit(solution)/shard_map/ppermute | solution.py:280
  17.6 1.6 %collective-permute-start.9 = (bf16[8,2432]{1,0:T(8,128)(2,1)S(1)}, bf16[8,2432]{1,0:T(8,128)(2,1)S(1)}, u32[]{:S(2)}, u32[]{:S(2)}) collective-permute-start(bf16[8,2432]{1,0:T(8,128)(2,1)S(1)} %collective-permute-done.6.refs_7_), channel_id=1, source_target_pairs={{0,1},{1,0},{2,3},{3,2},{4,5},{5,4},{6,7},{7,6},{8,9},{9,8},{10,11... | collective-permute-start | bytes 116744 | tf_op jit(solution)/shard_map/ppermute | solution.py:280
  20.9 11.1 %collective-permute-start.16 = (bf16[16,3968]{1,0:T(8,128)(2,1)S(1)}, bf16[16,3968]{1,0:T(8,128)(2,1)S(1)}, u32[]{:S(2)}, u32[]{:S(2)}) collective-permute-start(bf16[16,3968]{1,0:T(8,128)(2,1)S(1)} %get-tuple-element.45.refs_0_), channel_id=1, source_target_pairs={{0,2},{1,3},{2,0},{3,1},{4,6},{5,7},{6,4},{7,5},{8,10},{9,11},{10,... | collective-permute-start | bytes 380936 | tf_op jit(solution)/shard_map/ppermute | solution.py:280
  22.3 5.2 %collective-permute-start.11 = (bf16[8,3968]{1,0:T(8,128)(2,1)S(1)}, bf16[8,3968]{1,0:T(8,128)(2,1)S(1)}, u32[]{:S(2)}, u32[]{:S(2)}) collective-permute-start(bf16[8,3968]{1,0:T(8,128)(2,1)S(1)} %get-tuple-element.46), channel_id=1, source_target_pairs={{0,4},{4,0},{8,12},{12,8},{16,20},{20,16},{24,28},{28,24},{1,5},{5... | collective-permute-start | bytes 190472 | tf_op jit(solution)/shard_map/ppermute | solution.py:269
  24.4 6.9 %collective-permute-start.12 = (bf16[8,3968]{1,0:T(8,128)(2,1)S(1)}, bf16[8,3968]{1,0:T(8,128)(2,1)S(1)}, u32[]{:S(2)}, u32[]{:S(2)}) collective-permute-start(bf16[8,3968]{1,0:T(8,128)(2,1)S(1)} %get-tuple-element.47), channel_id=1, source_target_pairs={{0,28},{4,8},{8,4},{12,16},{16,12},{20,24},{24,20},{28,0},{1,29},{... | collective-permute-start | bytes 190472 | tf_op jit(solution)/shard_map/ppermute | solution.py:269
  27.5 4.5 %collective-permute-start.17 = (bf16[8,3968]{1,0:T(8,128)(2,1)S(1)}, bf16[8,3968]{1,0:T(8,128)(2,1)S(1)}, u32[]{:S(2)}, u32[]{:S(2)}) collective-permute-start(bf16[8,3968]{1,0:T(8,128)(2,1)S(1)} %collective-permute-done.11.refs_1_), channel_id=1, source_target_pairs={{0,2},{1,3},{2,0},{3,1},{4,6},{5,7},{6,4},{7,5},{8,10},{9,11},{10,... | collective-permute-start | bytes 190472 | tf_op jit(solution)/shard_map/ppermute | solution.py:280
  28.2 7.3 %collective-permute-start.13 = (bf16[16,3968]{1,0:T(8,128)(2,1)S(1)}, bf16[16,3968]{1,0:T(8,128)(2,1)S(1)}, u32[]{:S(2)}, u32[]{:S(2)}) collective-permute-start(bf16[16,3968]{1,0:T(8,128)(2,1)S(1)} %get-tuple-element.45.refs_0_), channel_id=1, source_target_pairs={{0,1},{1,0},{2,3},{3,2},{4,5},{5,4},{6,7},{7,6},{8,9},{9,8},{10,11... | collective-permute-start | bytes 380936 | tf_op jit(solution)/shard_map/ppermute | solution.py:280
  28.2 4.3 %collective-permute-start.14 = (bf16[8,3968]{1,0:T(8,128)(2,1)S(1)}, bf16[8,3968]{1,0:T(8,128)(2,1)S(1)}, u32[]{:S(2)}, u32[]{:S(2)}) collective-permute-start(bf16[8,3968]{1,0:T(8,128)(2,1)S(1)} %collective-permute-done.11.refs_1_), channel_id=1, source_target_pairs={{0,1},{1,0},{2,3},{3,2},{4,5},{5,4},{6,7},{7,6},{8,9},{9,8},{10,11... | collective-permute-start | bytes 190472 | tf_op jit(solution)/shard_map/ppermute | solution.py:280
  31.3 4.2 %collective-permute-start.18 = (bf16[8,3968]{1,0:T(8,128)(2,1)S(1)}, bf16[8,3968]{1,0:T(8,128)(2,1)S(1)}, u32[]{:S(2)}, u32[]{:S(2)}) collective-permute-start(bf16[8,3968]{1,0:T(8,128)(2,1)S(1)} %collective-permute-done.12.refs_2_), channel_id=1, source_target_pairs={{0,2},{1,3},{2,0},{3,1},{4,6},{5,7},{6,4},{7,5},{8,10},{9,11},{10,... | collective-permute-start | bytes 190472 | tf_op jit(solution)/shard_map/ppermute | solution.py:280
  32.0 4.8 %collective-permute-start.19 = (bf16[16,3968]{1,0:T(8,128)(2,1)S(1)}, bf16[16,3968]{1,0:T(8,128)(2,1)S(1)}, u32[]{:S(2)}, u32[]{:S(2)}) collective-permute-start(bf16[16,3968]{1,0:T(8,128)(2,1)S(1)} %collective-permute-done.16.refs_6_), channel_id=1, source_target_pairs={{0,1},{1,0},{2,3},{3,2},{4,5},{5,4},{6,7},{7,6},{8,9},{9,8},{10,11... | collective-permute-start | bytes 380936 | tf_op jit(solution)/shard_map/ppermute | solution.py:280
  32.0 3.5 %collective-permute-start.15 = (bf16[8,3968]{1,0:T(8,128)(2,1)S(1)}, bf16[8,3968]{1,0:T(8,128)(2,1)S(1)}, u32[]{:S(2)}, u32[]{:S(2)}) collective-permute-start(bf16[8,3968]{1,0:T(8,128)(2,1)S(1)} %collective-permute-done.12.refs_2_), channel_id=1, source_target_pairs={{0,1},{1,0},{2,3},{3,2},{4,5},{5,4},{6,7},{7,6},{8,9},{9,8},{10,11... | collective-permute-start | bytes 190472 | tf_op jit(solution)/shard_map/ppermute | solution.py:280
  32.5 3.0 %collective-permute-start.20 = (bf16[8,3968]{1,0:T(8,128)(2,1)S(1)}, bf16[8,3968]{1,0:T(8,128)(2,1)S(1)}, u32[]{:S(2)}, u32[]{:S(2)}) collective-permute-start(bf16[8,3968]{1,0:T(8,128)(2,1)S(1)} %collective-permute-done.17.refs_7_), channel_id=1, source_target_pairs={{0,1},{1,0},{2,3},{3,2},{4,5},{5,4},{6,7},{7,6},{8,9},{9,8},{10,11... | collective-permute-start | bytes 190472 | tf_op jit(solution)/shard_map/ppermute | solution.py:280
  35.5 1.3 %collective-permute-start.21 = (bf16[8,3968]{1,0:T(8,128)(2,1)S(1)}, bf16[8,3968]{1,0:T(8,128)(2,1)S(1)}, u32[]{:S(2)}, u32[]{:S(2)}) collective-permute-start(bf16[8,3968]{1,0:T(8,128)(2,1)S(1)} %collective-permute-done.18.refs_8_), channel_id=1, source_target_pairs={{0,1},{1,0},{2,3},{3,2},{4,5},{5,4},{6,7},{7,6},{8,9},{9,8},{10,11... | collective-permute-start | bytes 190472 | tf_op jit(solution)/shard_map/ppermute | solution.py:280

commit v3 on v2

v3 whole, which is shorter than its diff:
```python
import functools
import math

import jax
import jax.numpy as jnp
from jax import lax
from jax.experimental import pallas as pl
from jax.experimental.pallas import tpu as pltpu
from jax.sharding import PartitionSpec as P


HIGHEST = lax.Precision.HIGHEST
BF16 = jnp.bfloat16
F32 = jnp.float32
ORDERS = (1, 2)
VMEM = pl.BlockSpec(memory_space=pltpu.VMEM)


def near(*arrays):
    return [pltpu.with_memory_space_constraint(array, pltpu.VMEM) for array in arrays]


def away(*arrays):
    return [pltpu.with_memory_space_constraint(array, pltpu.HBM) for array in arrays]


def slot_index(degree, azimuth_order):
    return degree * degree + degree + azimuth_order


def slot_groups(degrees):
    groups = [[slot_index(degree, 0) for degree in range(degrees)]]
    for order in ORDERS:
        groups.append([slot_index(degree, order) for degree in range(order, degrees)])
        groups.append([slot_index(degree, -order) for degree in range(order, degrees)])
    return groups


def slot_order(degrees):
    return [slot for group in slot_groups(degrees) for slot in group]


def unused_slots(coeffs):
    order = slot_order(math.isqrt(coeffs))
    return [slot for slot in range(coeffs) if slot not in order]


def odd_slab():
    return lax.axis_index("slab") % 2 == 1


def dot(left, right, contract=((1,), (0,)), precision=None):
    return lax.dot_general(
        left, right, (contract, ((), ())), precision=precision, preferred_element_type=F32
    )


def lent_picks(low_ref, high_ref):
    odd = odd_slab()
    low, high = low_ref[...], high_ref[...]
    return jnp.concatenate([jnp.where(odd, low, high), jnp.where(odd, high, low)], axis=1)


def lent_hot(picks, atoms):
    rows = lax.broadcasted_iota(jnp.int32, (atoms, picks.shape[1]), 0)
    return (rows == picks).astype(F32)


def lent_rows(hot, rows):
    return dot(hot.astype(BF16), rows, ((0,), (0,))).astype(BF16)


def pack_kernel(
    emb_ref, low_ref, high_ref, nbr_ref, valid_ref, dist_ref, azi_ref, pol_ref,
    own_ref, pair_ref, other_ref, rest_ref, facts_ref,
):
    coeffs, atoms, channels = emb_ref.shape
    ghosts = low_ref.shape[1]
    edges = nbr_ref.shape[1]
    order = slot_order(math.isqrt(coeffs))
    for place, slot in enumerate(order):
        own_ref[:, place * channels : (place + 1) * channels] = emb_ref[slot]
    for place, slot in enumerate(unused_slots(coeffs)):
        rest_ref[place] = emb_ref[slot]
    picks = lent_picks(low_ref, high_ref)
    lent = lent_rows(lent_hot(picks, atoms), own_ref[...])
    pair_ref[...] = lent[:ghosts]
    other_ref[...] = lent[ghosts:]
    facts_ref[...] = jnp.zeros(facts_ref.shape, F32)
    facts_ref[0:1, :edges] = nbr_ref[...].astype(F32)
    facts_ref[1:2, :edges] = valid_ref[...].astype(F32)
    facts_ref[2:3, :edges] = dist_ref[...]
    facts_ref[3:4, :edges] = azi_ref[...]
    facts_ref[4:5, :edges] = pol_ref[...]
    facts_ref[5:6, : 2 * ghosts] = picks.astype(F32)


def scale_kernel(
    atoms, ghosts, slab_devices,
    facts_ref, partner_ref, rw_ref, readout_ref, *refs,
):
    count = (len(refs) - 6) // 2
    far, held = refs[:count], refs[count + 5 : -1]
    hot_ref, radial_ref, flags_ref, vector_ref, lent_ref = refs[count : count + 5]
    sems = refs[-1]
    copies = [pltpu.make_async_copy(far[i], held[i], sems.at[i]) for i in range(count)]
    for copy in copies:
        copy.start()
    layers, centers = rw_ref.shape[0], rw_ref.shape[1]
    own_count, ghost_count = slab_devices * atoms, slab_devices * ghosts
    half = slab_devices // 2
    me = lax.axis_index("yz")
    odd = odd_slab()
    vector_ref[...] = 0.125 * readout_ref[...]
    for side, ref in enumerate((facts_ref, partner_ref)):
        edges = hot_ref.shape[0] // 2
        nbr = ref[0:1, :edges].astype(jnp.int32)
        is_own = nbr < own_count
        ghost = nbr - own_count
        below = ghost < ghost_count
        ghost = jnp.where(below, ghost, ghost - ghost_count)
        paired = jnp.where(odd, below.astype(jnp.int32), 1 - below.astype(jnp.int32))
        slot = jnp.where(is_own, nbr // atoms, ghost // ghosts) ^ me
        upper = slot // half
        inner = jnp.where(
            is_own,
            upper * atoms + nbr % atoms,
            2 * atoms + (1 - paired) * (2 * ghosts) + upper * ghosts + ghost % ghosts,
        )
        place = (slot % half) * (2 * atoms + 4 * ghosts) + inner
        rows = lax.broadcasted_iota(jnp.int32, (flags_ref.shape[0], edges), 0)
        hot = jnp.where((rows == place) & (ref[1:2, :edges] != 0.0), 1.0, 0.0).astype(F32)
        span = slice(side * edges, (side + 1) * edges)
        flags_ref[:, span] = hot
        hot_cols = jnp.transpose(hot).astype(BF16)
        hot_ref[span, :] = jnp.concatenate([hot_cols, hot_cols], axis=1)
        middle = 1.0 + 0.5 * lax.broadcasted_iota(jnp.int32, (centers, edges), 0).astype(F32)
        basis = jnp.exp(-jnp.square((ref[2:3, :edges] - middle) / 0.5))
        for layer in range(layers):
            scale = dot(basis, rw_ref[layer], ((0,), (0,)), HIGHEST)
            radial_ref[layer, span, :] = scale / (1.0 + jnp.exp(-scale))
        picks = ref[5:6, : 2 * ghosts].astype(jnp.int32)
        lent_ref[side] = lent_hot(picks, atoms)
    for copy in copies:
        copy.wait()


def pull_kernel(facts_ref, partner_ref, radial_ref, flags_ref, dirs_ref, pulls_ref):
    edges = flags_ref.shape[1] // 2
    channels = radial_ref.shape[2]
    for side, ref in enumerate((facts_ref, partner_ref)):
        azimuth, polar = ref[3:4, :edges], ref[4:5, :edges]
        sin_polar = jnp.sin(polar)
        dirs = [sin_polar * jnp.cos(azimuth), sin_polar * jnp.sin(azimuth), jnp.cos(polar)]
        dirs_ref[:, side * edges : (side + 1) * edges] = jnp.concatenate(dirs, axis=0)
    radial = radial_ref[radial_ref.shape[0] - 1]
    high = radial.astype(BF16)
    both = jnp.concatenate([high, (radial - high.astype(F32)).astype(BF16)], axis=1)
    for axis in range(3):
        along = flags_ref[...] * dirs_ref[axis : axis + 1, :]
        high = along.astype(BF16)
        low = (along - high.astype(F32)).astype(BF16)
        got = dot(jnp.concatenate([high, low], axis=0), both)
        rows = flags_ref.shape[0]
        got = got[:rows, :channels] + got[:rows, channels:] + got[rows:, :channels]
        pulls_ref[:, axis * channels : (axis + 1) * channels] = got.astype(BF16)


def layer_sums(layer, degrees, channels, atoms, per_atom, tables, weights, hot_ref, radial_ref, scratch):
    joined, mixed = scratch
    groups = slot_groups(degrees)
    w_zero, w_one_re, w_one_im, w_two_re, w_two_im = (ref[layer] for ref in weights)
    width = joined.shape[1]
    start = 0
    for ref in tables:
        count = ref.shape[0]
        joined[start : start + count] = ref[:, :width].astype(F32)
        start += count
    rows = start

    def put(column, value):
        high = value.astype(BF16)
        low = (value - high.astype(F32)).astype(BF16)
        mixed[:rows, column : column + value.shape[1]] = high
        mixed[rows:, column : column + value.shape[1]] = low

    span = len(groups[0]) * channels
    zero = dot(joined[:, :span].astype(BF16), w_zero)
    put(0, zero)
    column = span
    for index, (real, imag) in enumerate(((w_one_re, w_one_im), (w_two_re, w_two_im))):
        span = len(groups[2 * index + 1]) * channels
        both = jnp.concatenate(
            [joined[:, column : column + span], joined[:, column + span : column + 2 * span]], axis=0
        ).astype(BF16)
        by_real = dot(both, real)
        by_imag = dot(both, imag)
        put(column, by_real[:rows] - by_imag[rows:])
        put(column + span, by_imag[:rows] + by_real[rows:])
        column += 2 * span
    edges = atoms * per_atom
    radial = radial_ref[layer, :edges, :]
    hot = hot_ref[:edges, :]
    sums = []
    first = None
    step = 2 * channels
    for begin in range(0, width, step):
        got = dot(hot, mixed[:, begin : min(begin + step, width)])
        for inner in range(0, got.shape[1], channels):
            message = got[:, inner : inner + channels] * radial
            if first is None:
                first = message
            sums.append(message.reshape(atoms, per_atom, channels).sum(axis=1))
    return sums, first, zero


def first_kernel(
    layer, last, degrees, channels, per_atom, count,
    lent_ref, hot_ref, radial_ref, pulls_ref, *refs,
):
    tables, weights = refs[:count], refs[count : count + 5]
    own_ref, pair_ref, other_ref = refs[count + 5 : count + 8]
    scratch = refs[count + 8 :]
    joined = scratch[0]
    both = own_ref.shape[0]
    atoms, ghosts = both // 2, lent_ref.shape[2] // 2
    sums, _, _ = layer_sums(
        layer, degrees, channels, both, per_atom, tables, weights, hot_ref, radial_ref, scratch
    )
    width = len(sums) * channels
    for place, total in enumerate(sums):
        cols = slice(place * channels, (place + 1) * channels)
        own_ref[:, cols] = (joined[:both, cols] + 0.18 * total).astype(BF16)
    for side in range(2):
        lent = lent_rows(lent_ref[side], own_ref[side * atoms : (side + 1) * atoms, :width])
        pair_ref[side * ghosts : (side + 1) * ghosts, :width] = lent[:ghosts]
        other_ref[side * ghosts : (side + 1) * ghosts, :width] = lent[ghosts:]
    if last:
        part = pulls_ref.shape[1]
        block = 2 * atoms + 4 * ghosts
        for slot in range(pulls_ref.shape[0] // block):
            cols = slice(width + slot // 2 * part, width + (slot // 2 + 1) * part)
            at = slot * block
            for ref, size in ((own_ref, atoms), (pair_ref, ghosts), (other_ref, ghosts)):
                to = slot % 2 * size
                ref[to : to + size, cols] = pulls_ref[at : at + size]
                at += 2 * size


def last_kernel(
    layer, degrees, channels, atoms, per_atom, count,
    rest_ref, lent_ref, hot_ref, radial_ref, dirs_ref, readout_ref, *refs,
):
    tables, weights = refs[:count], refs[count : count + 5]
    out_ref, force_ref = refs[count + 5 : count + 7]
    scratch = refs[count + 7 :]
    joined = scratch[0]
    sums, first, zero = layer_sums(
        layer, degrees, channels, atoms, per_atom, tables, weights, hot_ref, radial_ref, scratch
    )
    order = slot_order(degrees)
    for place, slot in enumerate(order):
        cols = slice(place * channels, (place + 1) * channels)
        out_ref[slot] = (joined[:atoms, cols] + 0.18 * sums[place]).astype(BF16)
    for place, slot in enumerate(unused_slots(degrees * degrees)):
        out_ref[slot] = rest_ref[place]

    readout = readout_ref[...]
    strength = dot(readout, first, ((1,), (1,)), HIGHEST)
    edges = atoms * per_atom
    pull = dirs_ref[:, :edges] * strength
    edge = lax.broadcasted_iota(jnp.int32, (atoms, edges), 1)
    atom = lax.broadcasted_iota(jnp.int32, (atoms, edges), 0)
    owner = (edge // per_atom == atom).astype(F32)
    own_force = dot(pull, owner, ((1,), (1,)), HIGHEST)

    width = len(sums) * channels
    part = 3 * channels
    ghosts = lent_ref.shape[2] // 2
    kinds = [0.0, 0.0, 0.0]
    for slot in range(count // 3):
        cols = slice(width + slot // 2 * part, width + (slot // 2 + 1) * part)
        for kind, size in enumerate((atoms, ghosts, ghosts)):
            at = slot % 2 * size
            kinds[kind] += tables[3 * slot + kind][at : at + size, cols].astype(F32)
    lent = jnp.concatenate(kinds[1:], axis=0)
    pulls = kinds[0] + dot(lent_ref[0], lent, precision=HIGHEST)
    mine = zero[:atoms, :channels] * readout
    ones = jnp.ones((1, channels), F32)
    for axis in range(3):
        back = dot(
            ones, mine * pulls[:, axis * channels : (axis + 1) * channels], ((1,), (1,)), HIGHEST
        )
        force_ref[axis : axis + 1, :] = own_force[axis : axis + 1] - back


def across(block, bit, slab_devices):
    return lax.ppermute(block, "yz", [(q, q ^ bit) for q in range(slab_devices)])


def toward(block, step, slabs):
    route = []
    for slab in range(slabs):
        to = slab + 1 if (slab % 2 == 0) == (step > 0) else slab - 1
        route.append((slab, to % slabs))
    return lax.ppermute(block, "slab", route)


def spread(held, bits, slab_devices):
    for bit in bits:
        for slot in sorted(held):
            held[slot | bit] = tuple(across(block, bit, slab_devices) for block in held[slot])
    return held


def order_bits(slab_devices):
    bits, bit = [], slab_devices // 2
    while bit:
        bits.append(bit)
        bit //= 2
    return bits


def body(
    embeddings, neighbours, valid, azimuth, polar, distance, send_low, send_high,
    w_zero, w_one_re, w_one_im, w_two_re, w_two_im, radial_weight, readout,
):
    atoms, coeffs, channels = embeddings.shape
    degrees = math.isqrt(coeffs)
    ghosts = send_low.shape[0]
    edges = neighbours.shape[0]
    layers = w_zero.shape[0]
    slabs, slab_devices = lax.axis_size("slab"), lax.axis_size("yz")
    rows = slab_devices * (atoms + 2 * ghosts)
    width = len(slot_order(degrees)) * channels
    low, high = send_low.reshape(1, -1), send_high.reshape(1, -1)
    held, shape = pltpu.VMEM, jax.ShapeDtypeStruct
    embeddings = embeddings.transpose(1, 0, 2)
    params = pltpu.CompilerParams(vmem_limit_bytes=24 * 2**20)
    row = lambda value: value.reshape(1, -1)
    far = pl.BlockSpec(memory_space=pl.ANY)

    half = slab_devices // 2
    own, pair, other, rest, facts = pl.pallas_call(
        pack_kernel,
        out_shape=[
            held((atoms, width), BF16), held((ghosts, width), BF16), held((ghosts, width), BF16),
            held((len(unused_slots(coeffs)), atoms, channels), BF16),
            held((8, max(edges, 2 * ghosts)), F32),
        ],
        in_specs=[VMEM] * 8,
        out_specs=[VMEM] * 5,
        compiler_params=params,
        name="pack",
    )(*away(embeddings, low, high, *map(row, (neighbours, valid, distance, azimuth, polar))))

    partner = across(facts, half, slab_devices)
    got_other = toward(other, -1, slabs)
    got_pair = toward(pair, 1, slabs)
    got_own = across(own, half, slab_devices)
    weights = (w_zero, w_one_re, w_one_im, w_two_re, w_two_im)
    hot, radial, flags, vector, lent, *weights = pl.pallas_call(
        functools.partial(scale_kernel, atoms, ghosts, slab_devices),
        out_shape=[
            held((2 * edges, 2 * rows), BF16), held((layers, 2 * edges, channels), F32),
            held((rows, 2 * edges), F32), held((1, channels), F32), held((2, atoms, 2 * ghosts), F32),
            *(held(array.shape, array.dtype) for array in weights),
        ],
        in_specs=[VMEM] * 4 + [far] * len(weights),
        out_specs=[VMEM] * (5 + len(weights)),
        scratch_shapes=[pltpu.SemaphoreType.DMA((len(weights),))],
        compiler_params=params,
        name="scales",
    )(*near(facts, partner), *away(radial_weight, row(readout), *weights))
    dirs, pulls = pl.pallas_call(
        pull_kernel,
        out_shape=[held((3, 2 * edges), F32), held((rows, 3 * channels), BF16)],
        in_specs=[VMEM] * 4,
        out_specs=[VMEM] * 2,
        compiler_params=params,
        name="pulls",
    )(*near(facts, partner, radial, flags))

    bits = order_bits(slab_devices)
    got_pair, hot, radial = lax.optimization_barrier((got_pair, hot, radial))
    blocks = {0: (own, got_pair, got_other)}
    pair_y = across(got_pair, half, slab_devices)
    other_y = across(got_other, half, slab_devices)
    blocks[half] = (got_own, pair_y, other_y)
    blocks = spread(blocks, bits[1:], slab_devices)
    tables = [
        blocks[slot + upper][kind]
        for slot in range(half) for kind in range(3) for upper in (0, half)
    ]
    scratch = [pltpu.VMEM((rows, width), F32), pltpu.VMEM((2 * rows, width), BF16)]
    per_atom = edges // atoms
    for layer in range(layers):
        if layer < layers - 1:
            last = layer == layers - 2
            wide = width + ((half + 1) // 2 * 3 * channels if last else 0)
            own, pair, other = pl.pallas_call(
                functools.partial(first_kernel, layer, last, degrees, channels, per_atom, len(tables)),
                out_shape=[
                    held((2 * atoms, wide), BF16), held((2 * ghosts, wide), BF16),
                    held((2 * ghosts, wide), BF16),
                ],
                in_specs=[VMEM] * (4 + len(tables) + len(weights)),
                out_specs=[VMEM] * 3,
                scratch_shapes=scratch,
                compiler_params=params,
                name="layer",
            )(*near(lent, hot, radial, pulls, *tables, *weights))
            got_other = toward(other, -1, slabs)
            got_pair = toward(pair, 1, slabs)
            blocks = spread({0: (own, got_pair, got_other)}, bits[1:], slab_devices)
            tables = [block for slot in range(half) for block in blocks[slot]]
        else:
            updated, forces = pl.pallas_call(
                functools.partial(
                    last_kernel, layer, degrees, channels, atoms, per_atom, len(tables)
                ),
                out_shape=[shape((coeffs, atoms, channels), BF16), shape((3, atoms), F32)],
                in_specs=[VMEM] * (6 + len(tables) + len(weights)),
                out_specs=[VMEM] * 2,
                scratch_shapes=scratch,
                compiler_params=params,
                name="last_layer",
            )(*near(rest, lent, hot, radial, dirs, vector, *tables, *weights))
    return (updated.transpose(1, 0, 2), forces)


def solution(mesh):
    both = ("slab", "yz")
    in_specs = (P(both, None, None), *([P(both)] * 7), *([P()] * 7))
    out_specs = (P(both, None, None), P(None, both))
    return jax.shard_map(body, mesh=mesh, in_specs=in_specs, out_specs=out_specs, check_vma=False)
```

time: 39.7 us -> 38 us (0.957)
  starting transfers between devices: 17.4 us -> 13.7 us
  waiting for transfers between devices: 11 us -> 12.3 us
  Pallas kernels: 10.4 us -> 11.1 us
    ppermute x18 -> x13, starting transfers between devices: 9.75 us -> 6.69 us  [across(): lax.ppermute(block, 'yz', [(q, q ^ bit) for q in range(slab_devices)])]
    ppermute x4, waiting for transfers between devices: 4.75 us -> 5.71 us  [toward(): return lax.ppermute(block, 'slab', route)]
    pallas_call x2, Pallas kernels: 4.23 us -> 3.42 us  [the longest x1 2.72 us: body(): pl.pallas_call(functools.partial(last_kernel, layer, degrees, channels, a...]
    pallas_call x1, Pallas kernels: 1.71 us -> 2.45 us  [body(): pl.pallas_call(functools.partial(first_kernel, layer, last, degrees, chan...]
    pallas_call x1, Pallas kernels: 3.27 us -> 4 us  [body(): pl.pallas_call(functools.partial(scale_kernel, atoms, ghosts, slab_device...]
    ppermute x4, starting transfers between devices: 7.63 us -> 6.98 us  [toward(): return lax.ppermute(block, 'slab', route)]
    ppermute x18 -> x13, waiting for transfers between devices: 6.23 us -> 6.61 us  [across(): lax.ppermute(block, 'yz', [(q, q ^ bit) for q in range(slab_devices)])]
  transfers between devices with their start and end apart: 22 -> 17, of which waited for: 7 -> 7; matrix products, arithmetic and copies ran while one was open for 0% -> 0% of each run, Pallas kernels for 12% -> 12%
where the time goes in v3:
time: 38 us; the launch traced here: 37.8 us
  starting transfers between devices  13.7 us (36%)
  waiting for transfers between devices  12.3 us (32%)
  Pallas kernels  11.1 us (29%)
  between operations  0.7 us (2%)
    ppermute x4, starting transfers between devices, toward(): return lax.ppermute(block, 'slab', route)  6.98 us
    ppermute x13, starting transfers between devices, across(): lax.ppermute(block, 'yz', [(q, q ^ bit) for q in range(slab_devices)])  6.69 us
    ppermute x13, waiting for transfers between devices, across(): lax.ppermute(block, 'yz', [(q, q ^ bit) for q in range(slab_devices)])  6.61 us
    ppermute x4, waiting for transfers between devices, toward(): return lax.ppermute(block, 'slab', route)  5.71 us
    pallas_call x1, Pallas kernels, body(): pl.pallas_call(functools.partial(scale_kernel, atoms, ghosts, slab_device...  4 us
    pallas_call x1, Pallas kernels, body(): pl.pallas_call(functools.partial(last_kernel, layer, degrees, channels, a...  2.72 us
    pallas_call x1, Pallas kernels, body(): pl.pallas_call(functools.partial(first_kernel, layer, last, degrees, chan...  2.45 us
    pallas_call x1, Pallas kernels, body(): pl.pallas_call(pack_kernel, out_shape=[held((atoms, width), BF16), held((...  1.24 us
  transfers between devices with their start and end apart: 17, of which 7 were waited for; matrix products, arithmetic and copies ran while one was open for 0% of the time, Pallas kernels for 12%

profile of v3, /device:TPU:0, one launch (start us, length us, event | category | flops | bytes accessed | tf_op | source)
XLA Modules:
  0.0 37.8 jit_solution(12087367731910114071)
XLA Ops:
  0.6 1.2 %pack.1 = (bf16[16,2432]{1,0:T(8,128)(2,1)S(1)}, bf16[8,2432]{1,0:T(8,128)(2,1)S(1)}, bf16[8,2432]{1,0:T(8,128)(2,1)S(1)}, bf16[6,16,128]{2,1,0:T(8,128)(2,1)S(1)}, f32[8,512]{1,0:T(8,128)S(1)}) custom-call(bf16[25,16,128]{2,1,0:T(8,128)(2,1)} %bitcast.10, s32[1,8]{1,0:T(1,128)} %bitcast.16, s32[1,8]{1,0:T(1,128)} %bitcast.17, s32[1,512]{1,0:T(1,128)} %bitcast.11, ...), custom_call_target="tpu_custom_call" | custom-call | tf_op jit(solution)/shard_map/pack/pallas_call | solution.py:344
  1.9 3.1 %collective-permute-start.2 = (bf16[16,2432]{1,0:T(8,128)(2,1)S(1)}, bf16[16,2432]{1,0:T(8,128)(2,1)S(1)}, u32[]{:S(2)}, u32[]{:S(2)}) collective-permute-start(bf16[16,2432]{1,0:T(8,128)(2,1)S(1)} %get-tuple-element.39.refs_0_), channel_id=1, source_target_pairs={{0,2},{1,3},{2,0},{3,1},{4,6},{5,7},{6,4},{7,5},{8,10},{9,11},{10,... | collective-permute-start | bytes 233480 | tf_op jit(solution)/shard_map/ppermute | solution.py:298
  4.9 1.5 %collective-permute-start.1 = (bf16[8,2432]{1,0:T(8,128)(2,1)S(1)}, bf16[8,2432]{1,0:T(8,128)(2,1)S(1)}, u32[]{:S(2)}, u32[]{:S(2)}) collective-permute-start(bf16[8,2432]{1,0:T(8,128)(2,1)S(1)} %get-tuple-element.30), channel_id=1, source_target_pairs={{0,4},{4,0},{8,12},{12,8},{16,20},{20,16},{24,28},{28,24},{1,5},{5... | collective-permute-start | bytes 116744 | tf_op jit(solution)/shard_map/ppermute | solution.py:306
  6.4 3.6 %collective-permute-start.4 = (bf16[8,2432]{1,0:T(8,128)(2,1)S(1)}, bf16[8,2432]{1,0:T(8,128)(2,1)S(1)}, u32[]{:S(2)}, u32[]{:S(2)}) collective-permute-start(bf16[8,2432]{1,0:T(8,128)(2,1)S(1)} %get-tuple-element.41), channel_id=1, source_target_pairs={{0,28},{4,8},{8,4},{12,16},{16,12},{20,24},{24,20},{28,0},{1,29},{... | collective-permute-start | bytes 116744 | tf_op jit(solution)/shard_map/ppermute | solution.py:306
  10.0 0.0 collective-permute-start.6
  10.0 0.5 %collective-permute-start = (f32[8,512]{1,0:T(8,128)S(1)}, f32[8,512]{1,0:T(8,128)S(1)}, u32[]{:S(2)}, u32[]{:S(2)}) collective-permute-start(f32[8,512]{1,0:T(8,128)S(1)} %get-tuple-element.28.facts_ref), channel_id=1, source_target_pairs={{0,2},{1,3},{2,0},{3,1},{4,6},{5,7},{6,4},{7,5},{8,10},{9,11},{10,... | collective-permute-start | bytes 49160 | tf_op jit(solution)/shard_map/ppermute | solution.py:298
  10.5 3.2 %collective-permute-done.partner_ref = f32[8,512]{1,0:T(8,128)S(1)} collective-permute-done((f32[8,512]{1,0:T(8,128)S(1)}, f32[8,512]{1,0:T(8,128)S(1)}, u32[]{:S(2)}, u32[]{:S(2)}) %collective-permute-start) | collective-permute-done | bytes 16416 | tf_op jit(solution)/shard_map/ppermute | solution.py:298
  13.7 4.0 %scales.1 = (bf16[1024,256]{1,0:T(8,128)(2,1)S(1)}, f32[2,1024,128]{2,1,0:T(8,128)S(1)}, f32[128,1024]{1,0:T(8,128)S(1)}, f32[1,128]{1,0:T(1,128)S(1)}, f32[2,16...) custom-call(f32[8,512]{1,0:T(8,128)S(1)} %get-tuple-element.28.facts, ...), custom_call_target="tpu_custom_call" | custom-call | tf_op jit(solution)/shard_map/scales/pallas_call | solution.py:362
  17.7 0.0 collective-permute-done.1.refs_2_
  17.8 0.6 %collective-permute-start.3 = (bf16[8,2432]{1,0:T(8,128)(2,1)S(1)}, bf16[8,2432]{1,0:T(8,128)(2,1)S(1)}, u32[]{:S(2)}, u32[]{:S(2)}) collective-permute-start(bf16[8,2432]{1,0:T(8,128)(2,1)S(1)} %collective-permute-done.1.refs_2_), channel_id=1, source_target_pairs={{0,2},{1,3},{2,0},{3,1},{4,6},{5,7},{6,4},{7,5},{8,10},{9,11},{10,... | collective-permute-start | bytes 116744 | tf_op jit(solution)/shard_map/ppermute | solution.py:298
  18.3 0.0 collective-permute-done.4.refs_4_
  18.3 1.5 %collective-permute-start.5 = (bf16[8,2432]{1,0:T(8,128)(2,1)S(1)}, bf16[8,2432]{1,0:T(8,128)(2,1)S(1)}, u32[]{:S(2)}, u32[]{:S(2)}) collective-permute-start(bf16[8,2432]{1,0:T(8,128)(2,1)S(1)} %collective-permute-done.4.refs_4_), channel_id=1, source_target_pairs={{0,2},{1,3},{2,0},{3,1},{4,6},{5,7},{6,4},{7,5},{8,10},{9,11},{10,... | collective-permute-start | bytes 116744 | tf_op jit(solution)/shard_map/ppermute | solution.py:298
  19.9 0.0 collective-permute-done.2.refs_1_
  19.9 0.0 collective-permute-start.7
  19.9 0.5 %collective-permute-start.8 = (bf16[8,2432]{1,0:T(8,128)(2,1)S(1)}, bf16[8,2432]{1,0:T(8,128)(2,1)S(1)}, u32[]{:S(2)}, u32[]{:S(2)}) collective-permute-start(bf16[8,2432]{1,0:T(8,128)(2,1)S(1)} %collective-permute-done.1.refs_2_), channel_id=1, source_target_pairs={{0,1},{1,0},{2,3},{3,2},{4,5},{5,4},{6,7},{7,6},{8,9},{9,8},{10,11... | collective-permute-start | bytes 116744 | tf_op jit(solution)/shard_map/ppermute | solution.py:298
  20.4 1.4 %collective-permute-done.3.refs_3_ = bf16[8,2432]{1,0:T(8,128)(2,1)S(1)} collective-permute-done((bf16[8,2432]{1,0:T(8,128)(2,1)S(1)}, bf16[8,2432]{1,0:T(8,128)(2,1)S(1)}, u32[]{:S(2)}, u32[]{:S(2)}) %collective-permute-start.3) | collective-permute-done | bytes 38944 | tf_op jit(solution)/shard_map/ppermute | solution.py:298
  21.8 0.0 collective-permute-start.10
  21.8 0.5 %collective-permute-done.5.refs_5_ = bf16[8,2432]{1,0:T(8,128)(2,1)S(1)} collective-permute-done((bf16[8,2432]{1,0:T(8,128)(2,1)S(1)}, bf16[8,2432]{1,0:T(8,128)(2,1)S(1)}, u32[]{:S(2)}, u32[]{:S(2)}) %collective-permute-start.5) | collective-permute-done | bytes 38944 | tf_op jit(solution)/shard_map/ppermute | solution.py:298
  22.3 0.0 collective-permute-start.9
  22.3 0.0 collective-permute-done.6.refs_6_
  22.3 0.5 %collective-permute-start.11 = (bf16[8,2432]{1,0:T(8,128)(2,1)S(1)}, bf16[8,2432]{1,0:T(8,128)(2,1)S(1)}, u32[]{:S(2)}, u32[]{:S(2)}) collective-permute-start(bf16[8,2432]{1,0:T(8,128)(2,1)S(1)} %collective-permute-done.5.refs_5_), channel_id=1, source_target_pairs={{0,1},{1,0},{2,3},{3,2},{4,5},{5,4},{6,7},{7,6},{8,9},{9,8},{10,11... | collective-permute-start | bytes 116744 | tf_op jit(solution)/shard_map/ppermute | solution.py:298
  22.8 0.7 %pulls.1 = (f32[3,1024]{1,0:T(4,128)S(1)}, bf16[128,384]{1,0:T(8,128)(2,1)S(1)}) custom-call(f32[8,512]{1,0:T(8,128)S(1)} %get-tuple-element.28.facts_ref, f32[8,512]{1,0:T(8,128)S(1)} %collective-permute-done.partner_ref, f32[2,1024,128]{2,1,0:T(8,128)S(1)} %get-tuple-element.34.radial_ref, f32[128,1024]{1,0:T(8,128)S(1)} %get-tuple-element.35.flags_ref), custom_call_target="tpu_custom_call" | custom-call | tf_op jit(solution)/shard_map/pulls/pallas_call | solution.py:375
  23.5 0.0 collective-permute-done.10.refs_10_
  23.6 0.0 collective-permute-done.9.refs_9_
  23.6 0.1 collective-permute-done.11.refs_11_
  23.7 2.5 %layer.1 = (bf16[32,2816]{1,0:T(8,128)(2,1)S(1)}, bf16[16,2816]{1,0:T(8,128)(2,1)S(1)}, bf16[16,2816]{1,0:T(8,128)(2,1)S(1)}) custom-call(f32[2,16,16]{2,1,0:T(8,128)S(1)} %get-tuple-element.29.lent_ref, bf16[1024,256]{1,0:T(8,128)(2,1)S(1)} %get-tuple-element.33.hot_ref, f32[2,1024,128]{2,1,0:T(8,128)S(1)} %get-tuple-element.34.radial_ref, ...), custom_call_target="tpu_custom_call" | custom-call | tf_op jit(solution)/shard_map/layer/pallas_call | solution.py:401
  26.2 1.9 %collective-permute-start.13 = (bf16[16,2816]{1,0:T(8,128)(2,1)S(1)}, bf16[16,2816]{1,0:T(8,128)(2,1)S(1)}, u32[]{:S(2)}, u32[]{:S(2)}) collective-permute-start(bf16[16,2816]{1,0:T(8,128)(2,1)S(1)} %get-tuple-element.49), channel_id=1, source_target_pairs={{0,28},{4,8},{8,4},{12,16},{16,12},{20,24},{24,20},{28,0},{1,29},{... | collective-permute-start | bytes 270344 | tf_op jit(solution)/shard_map/ppermute | solution.py:306
  28.1 3.0 %collective-permute-done.12.refs_1_ = bf16[16,2816]{1,0:T(8,128)(2,1)S(1)} collective-permute-done((bf16[16,2816]{1,0:T(8,128)(2,1)S(1)}, bf16[16,2816]{1,0:T(8,128)(2,1)S(1)}, u32[]{:S(2)}, u32[]{:S(2)}) %collective-permute-start.12) | collective-permute-done | bytes 90144 | tf_op jit(solution)/shard_map/ppermute | solution.py:306
  31.0 0.0 collective-permute-start.15
  31.0 2.7 %collective-permute-done.13.refs_2_ = bf16[16,2816]{1,0:T(8,128)(2,1)S(1)} collective-permute-done((bf16[16,2816]{1,0:T(8,128)(2,1)S(1)}, bf16[16,2816]{1,0:T(8,128)(2,1)S(1)}, u32[]{:S(2)}, u32[]{:S(2)}) %collective-permute-start.13) | collective-permute-done | bytes 90144 | tf_op jit(solution)/shard_map/ppermute | solution.py:306
  33.8 1.3 %collective-permute-done.16.refs_5_ = bf16[16,2816]{1,0:T(8,128)(2,1)S(1)} collective-permute-done((bf16[16,2816]{1,0:T(8,128)(2,1)S(1)}, bf16[16,2816]{1,0:T(8,128)(2,1)S(1)}, u32[]{:S(2)}, u32[]{:S(2)}) %collective-permute-start.16) | collective-permute-done | bytes 90144 | tf_op jit(solution)/shard_map/ppermute | solution.py:298
  35.1 2.7 %last_layer.1 = (bf16[25,16,128]{2,1,0:T(8,128)(2,1)}, f32[3,16]{1,0:T(4,128)}) custom-call(bf16[6,16,128]{2,1,0:T(8,128)(2,1)S(1)} %get-tuple-element.27.rest_ref, f32[2,16,16]{2,1,0:T(8,128)S(1)} %get-tuple-element.29.lent_ref, bf16[1024,256]{1,0:T(8,128)(2,1)S(1)} %get-tuple-element.33.hot_ref, f32[2,1024,128]{2,1,0:T(8,128)S(1)} %get-tuple-element.34.radial_ref, ...), custom_call_target="tpu_custom_call" | custom-call | tf_op jit(solution)/shard_map/last_layer/pallas_call | solution.py:418
  (7 shorter events, 0.0 us)
Async XLA Ops:
  1.9 18.0 %collective-permute-start.2 = (bf16[16,2432]{1,0:T(8,128)(2,1)S(1)}, bf16[16,2432]{1,0:T(8,128)(2,1)S(1)}, u32[]{:S(2)}, u32[]{:S(2)}) collective-permute-start(bf16[16,2432]{1,0:T(8,128)(2,1)S(1)} %get-tuple-element.39.refs_0_), channel_id=1, source_target_pairs={{0,2},{1,3},{2,0},{3,1},{4,6},{5,7},{6,4},{7,5},{8,10},{9,11},{10,... | collective-permute-start | bytes 233480 | tf_op jit(solution)/shard_map/ppermute | solution.py:298
  4.9 12.8 %collective-permute-start.1 = (bf16[8,2432]{1,0:T(8,128)(2,1)S(1)}, bf16[8,2432]{1,0:T(8,128)(2,1)S(1)}, u32[]{:S(2)}, u32[]{:S(2)}) collective-permute-start(bf16[8,2432]{1,0:T(8,128)(2,1)S(1)} %get-tuple-element.30), channel_id=1, source_target_pairs={{0,4},{4,0},{8,12},{12,8},{16,20},{20,16},{24,28},{28,24},{1,5},{5... | collective-permute-start | bytes 116744 | tf_op jit(solution)/shard_map/ppermute | solution.py:306
  6.4 11.9 %collective-permute-start.4 = (bf16[8,2432]{1,0:T(8,128)(2,1)S(1)}, bf16[8,2432]{1,0:T(8,128)(2,1)S(1)}, u32[]{:S(2)}, u32[]{:S(2)}) collective-permute-start(bf16[8,2432]{1,0:T(8,128)(2,1)S(1)} %get-tuple-element.41), channel_id=1, source_target_pairs={{0,28},{4,8},{8,4},{12,16},{16,12},{20,24},{24,20},{28,0},{1,29},{... | collective-permute-start | bytes 116744 | tf_op jit(solution)/shard_map/ppermute | solution.py:306
  10.0 12.3 %collective-permute-start.6 = (bf16[16,2432]{1,0:T(8,128)(2,1)S(1)}, bf16[16,2432]{1,0:T(8,128)(2,1)S(1)}, u32[]{:S(2)}, u32[]{:S(2)}) collective-permute-start(bf16[16,2432]{1,0:T(8,128)(2,1)S(1)} %get-tuple-element.39.refs_0_), channel_id=1, source_target_pairs={{0,1},{1,0},{2,3},{3,2},{4,5},{5,4},{6,7},{7,6},{8,9},{9,8},{10,11... | collective-permute-start | bytes 233480 | tf_op jit(solution)/shard_map/ppermute | solution.py:298
  10.0 3.7 %collective-permute-start = (f32[8,512]{1,0:T(8,128)S(1)}, f32[8,512]{1,0:T(8,128)S(1)}, u32[]{:S(2)}, u32[]{:S(2)}) collective-permute-start(f32[8,512]{1,0:T(8,128)S(1)} %get-tuple-element.28.facts_ref), channel_id=1, source_target_pairs={{0,2},{1,3},{2,0},{3,1},{4,6},{5,7},{6,4},{7,5},{8,10},{9,11},{10,... | collective-permute-start | bytes 49160 | tf_op jit(solution)/shard_map/ppermute | solution.py:298
  17.8 4.0 %collective-permute-start.3 = (bf16[8,2432]{1,0:T(8,128)(2,1)S(1)}, bf16[8,2432]{1,0:T(8,128)(2,1)S(1)}, u32[]{:S(2)}, u32[]{:S(2)}) collective-permute-start(bf16[8,2432]{1,0:T(8,128)(2,1)S(1)} %collective-permute-done.1.refs_2_), channel_id=1, source_target_pairs={{0,2},{1,3},{2,0},{3,1},{4,6},{5,7},{6,4},{7,5},{8,10},{9,11},{10,... | collective-permute-start | bytes 116744 | tf_op jit(solution)/shard_map/ppermute | solution.py:298
  18.3 4.0 %collective-permute-start.5 = (bf16[8,2432]{1,0:T(8,128)(2,1)S(1)}, bf16[8,2432]{1,0:T(8,128)(2,1)S(1)}, u32[]{:S(2)}, u32[]{:S(2)}) collective-permute-start(bf16[8,2432]{1,0:T(8,128)(2,1)S(1)} %collective-permute-done.4.refs_4_), channel_id=1, source_target_pairs={{0,2},{1,3},{2,0},{3,1},{4,6},{5,7},{6,4},{7,5},{8,10},{9,11},{10,... | collective-permute-start | bytes 116744 | tf_op jit(solution)/shard_map/ppermute | solution.py:298
  19.9 3.8 %collective-permute-start.7 = (bf16[16,2432]{1,0:T(8,128)(2,1)S(1)}, bf16[16,2432]{1,0:T(8,128)(2,1)S(1)}, u32[]{:S(2)}, u32[]{:S(2)}) collective-permute-start(bf16[16,2432]{1,0:T(8,128)(2,1)S(1)} %collective-permute-done.2.refs_1_), channel_id=1, source_target_pairs={{0,1},{1,0},{2,3},{3,2},{4,5},{5,4},{6,7},{7,6},{8,9},{9,8},{10,11... | collective-permute-start | bytes 233480 | tf_op jit(solution)/shard_map/ppermute | solution.py:298
  19.9 3.7 %collective-permute-start.8 = (bf16[8,2432]{1,0:T(8,128)(2,1)S(1)}, bf16[8,2432]{1,0:T(8,128)(2,1)S(1)}, u32[]{:S(2)}, u32[]{:S(2)}) collective-permute-start(bf16[8,2432]{1,0:T(8,128)(2,1)S(1)} %collective-permute-done.1.refs_2_), channel_id=1, source_target_pairs={{0,1},{1,0},{2,3},{3,2},{4,5},{5,4},{6,7},{7,6},{8,9},{9,8},{10,11... | collective-permute-start | bytes 116744 | tf_op jit(solution)/shard_map/ppermute | solution.py:298
  21.8 1.7 %collective-permute-start.10 = (bf16[8,2432]{1,0:T(8,128)(2,1)S(1)}, bf16[8,2432]{1,0:T(8,128)(2,1)S(1)}, u32[]{:S(2)}, u32[]{:S(2)}) collective-permute-start(bf16[8,2432]{1,0:T(8,128)(2,1)S(1)} %collective-permute-done.4.refs_4_), channel_id=1, source_target_pairs={{0,1},{1,0},{2,3},{3,2},{4,5},{5,4},{6,7},{7,6},{8,9},{9,8},{10,11... | collective-permute-start | bytes 116744 | tf_op jit(solution)/shard_map/ppermute | solution.py:298
  22.3 1.2 %collective-permute-start.9 = (bf16[8,2432]{1,0:T(8,128)(2,1)S(1)}, bf16[8,2432]{1,0:T(8,128)(2,1)S(1)}, u32[]{:S(2)}, u32[]{:S(2)}) collective-permute-start(bf16[8,2432]{1,0:T(8,128)(2,1)S(1)} %collective-permute-done.3.refs_3_), channel_id=1, source_target_pairs={{0,1},{1,0},{2,3},{3,2},{4,5},{5,4},{6,7},{7,6},{8,9},{9,8},{10,11... | collective-permute-start | bytes 116744 | tf_op jit(solution)/shard_map/ppermute | solution.py:298
  22.3 1.4 %collective-permute-start.11 = (bf16[8,2432]{1,0:T(8,128)(2,1)S(1)}, bf16[8,2432]{1,0:T(8,128)(2,1)S(1)}, u32[]{:S(2)}, u32[]{:S(2)}) collective-permute-start(bf16[8,2432]{1,0:T(8,128)(2,1)S(1)} %collective-permute-done.5.refs_5_), channel_id=1, source_target_pairs={{0,1},{1,0},{2,3},{3,2},{4,5},{5,4},{6,7},{7,6},{8,9},{9,8},{10,11... | collective-permute-start | bytes 116744 | tf_op jit(solution)/shard_map/ppermute | solution.py:298
  26.1 4.9 %collective-permute-start.12 = (bf16[16,2816]{1,0:T(8,128)(2,1)S(1)}, bf16[16,2816]{1,0:T(8,128)(2,1)S(1)}, u32[]{:S(2)}, u32[]{:S(2)}) collective-permute-start(bf16[16,2816]{1,0:T(8,128)(2,1)S(1)} %get-tuple-element.48), channel_id=1, source_target_pairs={{0,4},{4,0},{8,12},{12,8},{16,20},{20,16},{24,28},{28,24},{1,5},{5... | collective-permute-start | bytes 270344 | tf_op jit(solution)/shard_map/ppermute | solution.py:306
  26.2 7.6 %collective-permute-start.13 = (bf16[16,2816]{1,0:T(8,128)(2,1)S(1)}, bf16[16,2816]{1,0:T(8,128)(2,1)S(1)}, u32[]{:S(2)}, u32[]{:S(2)}) collective-permute-start(bf16[16,2816]{1,0:T(8,128)(2,1)S(1)} %get-tuple-element.49), channel_id=1, source_target_pairs={{0,28},{4,8},{8,4},{12,16},{16,12},{20,24},{24,20},{28,0},{1,29},{... | collective-permute-start | bytes 270344 | tf_op jit(solution)/shard_map/ppermute | solution.py:306
  28.1 7.0 %collective-permute-start.14 = (bf16[32,2816]{1,0:T(8,128)(2,1)S(1)}, bf16[32,2816]{1,0:T(8,128)(2,1)S(1)}, u32[]{:S(2)}, u32[]{:S(2)}) collective-permute-start(bf16[32,2816]{1,0:T(8,128)(2,1)S(1)} %get-tuple-element.47.refs_0_), channel_id=1, source_target_pairs={{0,1},{1,0},{2,3},{3,2},{4,5},{5,4},{6,7},{7,6},{8,9},{9,8},{10,11... | collective-permute-start | bytes 540680 | tf_op jit(solution)/shard_map/ppermute | solution.py:298
  31.0 2.7 %collective-permute-start.15 = (bf16[16,2816]{1,0:T(8,128)(2,1)S(1)}, bf16[16,2816]{1,0:T(8,128)(2,1)S(1)}, u32[]{:S(2)}, u32[]{:S(2)}) collective-permute-start(bf16[16,2816]{1,0:T(8,128)(2,1)S(1)} %collective-permute-done.12.refs_1_), channel_id=1, source_target_pairs={{0,1},{1,0},{2,3},{3,2},{4,5},{5,4},{6,7},{7,6},{8,9},{9,8},{10,11... | collective-permute-start | bytes 270344 | tf_op jit(solution)/shard_map/ppermute | solution.py:298
  33.8 1.3 %collective-permute-start.16 = (bf16[16,2816]{1,0:T(8,128)(2,1)S(1)}, bf16[16,2816]{1,0:T(8,128)(2,1)S(1)}, u32[]{:S(2)}, u32[]{:S(2)}) collective-permute-start(bf16[16,2816]{1,0:T(8,128)(2,1)S(1)} %collective-permute-done.13.refs_2_), channel_id=1, source_target_pairs={{0,1},{1,0},{2,3},{3,2},{4,5},{5,4},{6,7},{7,6},{8,9},{9,8},{10,11... | collective-permute-start | bytes 270344 | tf_op jit(solution)/shard_map/ppermute | solution.py:298

commit v4 on v3

--- a/solution.py
+++ b/solution.py
@@ -95,81 +95,115 @@
     facts_ref[5:6, : 2 * ghosts] = picks.astype(F32)
 
 
-def scale_kernel(
-    atoms, ghosts, slab_devices,
-    facts_ref, partner_ref, rw_ref, readout_ref, *refs,
-):
-    count = (len(refs) - 6) // 2
-    far, held = refs[:count], refs[count + 5 : -1]
-    hot_ref, radial_ref, flags_ref, vector_ref, lent_ref = refs[count : count + 5]
-    sems = refs[-1]
-    copies = [pltpu.make_async_copy(far[i], held[i], sems.at[i]) for i in range(count)]
+def start_fetch(refs, layer):
+    count = len(refs) // 2
+    copies = [
+        pltpu.make_async_copy(refs[i].at[layer], refs[count + i], refs[-1].at[i])
+        for i in range(count)
+    ]
     for copy in copies:
         copy.start()
+    return copies
+
+
+def edge_scales(
+    atoms, ghosts, slab_devices, facts_ref, rw_ref, hot_ref, radial_ref, flags_ref, lent_ref
+):
     layers, centers = rw_ref.shape[0], rw_ref.shape[1]
     own_count, ghost_count = slab_devices * atoms, slab_devices * ghosts
     half = slab_devices // 2
     me = lax.axis_index("yz")
     odd = odd_slab()
+    edges = hot_ref.shape[0]
+    nbr = facts_ref[0:1, :edges].astype(jnp.int32)
+    is_own = nbr < own_count
+    ghost = nbr - own_count
+    below = ghost < ghost_count
+    ghost = jnp.where(below, ghost, ghost - ghost_count)
+    paired = jnp.where(odd, below.astype(jnp.int32), 1 - below.astype(jnp.int32))
+    slot = jnp.where(is_own, nbr // atoms, ghost // ghosts) ^ me
+    upper = slot // half
+    inner = jnp.where(
+        is_own,
+        upper * atoms + nbr % atoms,
+        2 * atoms + (1 - paired) * (2 * ghosts) + upper * ghosts + ghost % ghosts,
+    )
+    place = (slot % half) * (2 * atoms + 4 * ghosts) + inner
+    rows = lax.broadcasted_iota(jnp.int32, (flags_ref.shape[0], edges), 0)
+    hot = jnp.where((rows == place) & (facts_ref[1:2, :edges] != 0.0), 1.0, 0.0).astype(F32)
+    flags_ref[...] = hot
+    hot_cols = jnp.transpose(hot).astype(BF16)
+    hot_ref[...] = jnp.concatenate([hot_cols, hot_cols], axis=1)
+    middle = 1.0 + 0.5 * lax.broadcasted_iota(jnp.int32, (centers, edges), 0).astype(F32)
+    basis = jnp.exp(-jnp.square((facts_ref[2:3, :edges] - middle) / 0.5))
+    for layer in range(layers):
+        scale = dot(basis, rw_ref[layer], ((0,), (0,)), HIGHEST)
+        radial_ref[layer] = scale / (1.0 + jnp.exp(-scale))
+    lent_ref[...] = lent_hot(facts_ref[5:6, : 2 * ghosts].astype(jnp.int32), atoms)
+
+
+def own_scale_kernel(
+    atoms, ghosts, slab_devices, count,
+    facts_ref, rw_ref, readout_ref, *refs,
+):
+    far, refs = refs[:count], refs[count:]
+    hot_ref, radial_ref, flags_ref, lent_ref, vector_ref, scales_ref = refs[:6]
+    copies = start_fetch((*far, *refs[6:]), 0)
     vector_ref[...] = 0.125 * readout_ref[...]
-    for side, ref in enumerate((facts_ref, partner_ref)):
-        edges = hot_ref.shape[0] // 2
-        nbr = ref[0:1, :edges].astype(jnp.int32)
-        is_own = nbr < own_count
-        ghost = nbr - own_count
-        below = ghost < ghost_count
-        ghost = jnp.where(below, ghost, ghost - ghost_count)
-        paired = jnp.where(odd, below.astype(jnp.int32), 1 - below.astype(jnp.int32))
-        slot = jnp.where(is_own, nbr // atoms, ghost // ghosts) ^ me
-        upper = slot // half
-        inner = jnp.where(
-            is_own,
-            upper * atoms + nbr % atoms,
-            2 * atoms + (1 - paired) * (2 * ghosts) + upper * ghosts + ghost % ghosts,
-        )
-        place = (slot % half) * (2 * atoms + 4 * ghosts) + inner
-        rows = lax.broadcasted_iota(jnp.int32, (flags_ref.shape[0], edges), 0)
-        hot = jnp.where((rows == place) & (ref[1:2, :edges] != 0.0), 1.0, 0.0).astype(F32)
-        span = slice(side * edges, (side + 1) * edges)
-        flags_ref[:, span] = hot
-        hot_cols = jnp.transpose(hot).astype(BF16)
-        hot_ref[span, :] = jnp.concatenate([hot_cols, hot_cols], axis=1)
-        middle = 1.0 + 0.5 * lax.broadcasted_iota(jnp.int32, (centers, edges), 0).astype(F32)
-        basis = jnp.exp(-jnp.square((ref[2:3, :edges] - middle) / 0.5))
-        for layer in range(layers):
-            scale = dot(basis, rw_ref[layer], ((0,), (0,)), HIGHEST)
-            radial_ref[layer, span, :] = scale / (1.0 + jnp.exp(-scale))
-        picks = ref[5:6, : 2 * ghosts].astype(jnp.int32)
-        lent_ref[side] = lent_hot(picks, atoms)
+    scales_ref[...] = rw_ref[...]
+    edge_scales(
+        atoms, ghosts, slab_devices, facts_ref, rw_ref, hot_ref, radial_ref, flags_ref, lent_ref
+    )
     for copy in copies:
         copy.wait()
 
 
-def pull_kernel(facts_ref, partner_ref, radial_ref, flags_ref, dirs_ref, pulls_ref):
-    edges = flags_ref.shape[1] // 2
-    channels = radial_ref.shape[2]
-    for side, ref in enumerate((facts_ref, partner_ref)):
+def partner_scale_kernel(
+    atoms, ghosts, slab_devices, count, fetched,
+    facts_ref, rw_ref, *refs,
+):
+    far, refs = refs[:count], refs[count:]
+    copies = [start_fetch((*far, *refs[4 + count * i : 4 + count * (i + 1)], refs[-1].at[i]), layer)
+              for i, layer in enumerate(fetched)]
+    edge_scales(atoms, ghosts, slab_devices, facts_ref, rw_ref, *refs[:4])
+    for group in copies:
+        for copy in group:
+            copy.wait()
+
+
+def pull_kernel(
+    facts_ref, radial_ref, flags_ref, partner_ref, radial_y_ref, flags_y_ref, dirs_ref, pulls_ref
+):
+    edges, channels = radial_ref.shape[1:]
+    last = radial_ref.shape[0] - 1
+    rows = flags_ref.shape[0]
+    totals = [0.0, 0.0, 0.0]
+    for ref, scale_ref, hot_ref in (
+        (facts_ref, radial_ref, flags_ref), (partner_ref, radial_y_ref, flags_y_ref)
+    ):
         azimuth, polar = ref[3:4, :edges], ref[4:5, :edges]
         sin_polar = jnp.sin(polar)
         dirs = [sin_polar * jnp.cos(azimuth), sin_polar * jnp.sin(azimuth), jnp.cos(polar)]
-        dirs_ref[:, side * edges : (side + 1) * edges] = jnp.concatenate(dirs, axis=0)
-    radial = radial_ref[radial_ref.shape[0] - 1]
-    high = radial.astype(BF16)
-    both = jnp.concatenate([high, (radial - high.astype(F32)).astype(BF16)], axis=1)
-    for axis in range(3):
-        along = flags_ref[...] * dirs_ref[axis : axis + 1, :]
-        high = along.astype(BF16)
-        low = (along - high.astype(F32)).astype(BF16)
-        got = dot(jnp.concatenate([high, low], axis=0), both)
-        rows = flags_ref.shape[0]
-        got = got[:rows, :channels] + got[:rows, channels:] + got[rows:, :channels]
-        pulls_ref[:, axis * channels : (axis + 1) * channels] = got.astype(BF16)
-
-
-def layer_sums(layer, degrees, channels, atoms, per_atom, tables, weights, hot_ref, radial_ref, scratch):
+        if ref is facts_ref:
+            dirs_ref[...] = jnp.concatenate(dirs, axis=0)
+        radial = scale_ref[last]
+        high = radial.astype(BF16)
+        both = jnp.concatenate([high, (radial - high.astype(F32)).astype(BF16)], axis=1)
+        for axis in range(3):
+            along = hot_ref[...] * dirs[axis]
+            high = along.astype(BF16)
+            low = (along - high.astype(F32)).astype(BF16)
+            got = dot(jnp.concatenate([high, low], axis=0), both)
+            totals[axis] += (
+                got[:rows, :channels] + got[:rows, channels:] + got[rows:, :channels]
+            )
+    pulls_ref[...] = jnp.concatenate(totals, axis=1).astype(BF16)
+
+
+def layer_sums(layer, degrees, channels, atoms, per_atom, tables, weights, hots, radials, scratch):
     joined, mixed = scratch
     groups = slot_groups(degrees)
-    w_zero, w_one_re, w_one_im, w_two_re, w_two_im = (ref[layer] for ref in weights)
+    w_zero, w_one_re, w_one_im, w_two_re, w_two_im = (ref[...] for ref in weights)
     width = joined.shape[1]
     start = 0
     for ref in tables:
@@ -198,41 +232,46 @@
         put(column, by_real[:rows] - by_imag[rows:])
         put(column + span, by_imag[:rows] + by_real[rows:])
         column += 2 * span
-    edges = atoms * per_atom
-    radial = radial_ref[layer, :edges, :]
-    hot = hot_ref[:edges, :]
+    part = atoms // len(hots)
     sums = []
     first = None
     step = 2 * channels
     for begin in range(0, width, step):
-        got = dot(hot, mixed[:, begin : min(begin + step, width)])
-        for inner in range(0, got.shape[1], channels):
-            message = got[:, inner : inner + channels] * radial
-            if first is None:
-                first = message
-            sums.append(message.reshape(atoms, per_atom, channels).sum(axis=1))
+        end = min(begin + step, width)
+        pieces = []
+        for hot_ref, radial_ref in zip(hots, radials):
+            got = dot(hot_ref[...], mixed[:, begin:end])
+            for inner in range(0, end - begin, channels):
+                message = got[:, inner : inner + channels] * radial_ref[layer]
+                if first is None:
+                    first = message
+                pieces.append(message.reshape(part, per_atom, channels).sum(axis=1))
+        count = (end - begin) // channels
+        for inner in range(count):
+            sums.append(jnp.concatenate(pieces[inner::count], axis=0))
     return sums, first, zero
 
 
 def first_kernel(
     layer, last, degrees, channels, per_atom, count,
-    lent_ref, hot_ref, radial_ref, pulls_ref, *refs,
+    lent_ref, hot_ref, radial_ref, lent_y_ref, hot_y_ref, radial_y_ref, pulls_ref, *refs,
 ):
     tables, weights = refs[:count], refs[count : count + 5]
     own_ref, pair_ref, other_ref = refs[count + 5 : count + 8]
     scratch = refs[count + 8 :]
     joined = scratch[0]
     both = own_ref.shape[0]
-    atoms, ghosts = both // 2, lent_ref.shape[2] // 2
+    atoms, ghosts = both // 2, lent_ref.shape[1] // 2
     sums, _, _ = layer_sums(
-        layer, degrees, channels, both, per_atom, tables, weights, hot_ref, radial_ref, scratch
+        layer, degrees, channels, both, per_atom, tables, weights,
+        (hot_ref, hot_y_ref), (radial_ref, radial_y_ref), scratch,
     )
     width = len(sums) * channels
     for place, total in enumerate(sums):
         cols = slice(place * channels, (place + 1) * channels)
         own_ref[:, cols] = (joined[:both, cols] + 0.18 * total).astype(BF16)
-    for side in range(2):
-        lent = lent_rows(lent_ref[side], own_ref[side * atoms : (side + 1) * atoms, :width])
+    for side, hot in enumerate((lent_ref, lent_y_ref)):
+        lent = lent_rows(hot[...], own_ref[side * atoms : (side + 1) * atoms, :width])
         pair_ref[side * ghosts : (side + 1) * ghosts, :width] = lent[:ghosts]
         other_ref[side * ghosts : (side + 1) * ghosts, :width] = lent[ghosts:]
     if last:
@@ -256,7 +295,7 @@
     scratch = refs[count + 7 :]
     joined = scratch[0]
     sums, first, zero = layer_sums(
-        layer, degrees, channels, atoms, per_atom, tables, weights, hot_ref, radial_ref, scratch
+        layer, degrees, channels, atoms, per_atom, tables, weights, (hot_ref,), (radial_ref,), scratch
     )
     order = slot_order(degrees)
     for place, slot in enumerate(order):
@@ -268,7 +307,7 @@
     readout = readout_ref[...]
     strength = dot(readout, first, ((1,), (1,)), HIGHEST)
     edges = atoms * per_atom
-    pull = dirs_ref[:, :edges] * strength
+    pull = dirs_ref[...] * strength
     edge = lax.broadcasted_iota(jnp.int32, (atoms, edges), 1)
     atom = lax.broadcasted_iota(jnp.int32, (atoms, edges), 0)
     owner = (edge // per_atom == atom).astype(F32)
@@ -276,7 +315,7 @@
 
     width = len(sums) * channels
     part = 3 * channels
-    ghosts = lent_ref.shape[2] // 2
+    ghosts = lent_ref.shape[1] // 2
     kinds = [0.0, 0.0, 0.0]
     for slot in range(count // 3):
         cols = slice(width + slot // 2 * part, width + (slot // 2 + 1) * part)
@@ -284,7 +323,7 @@
             at = slot % 2 * size
             kinds[kind] += tables[3 * slot + kind][at : at + size, cols].astype(F32)
     lent = jnp.concatenate(kinds[1:], axis=0)
-    pulls = kinds[0] + dot(lent_ref[0], lent, precision=HIGHEST)
+    pulls = kinds[0] + dot(lent_ref[...], lent, precision=HIGHEST)
     mine = zero[:atoms, :channels] * readout
     ones = jnp.ones((1, channels), F32)
     for axis in range(3):
@@ -359,33 +398,49 @@
     got_pair = toward(pair, 1, slabs)
     got_own = across(own, half, slab_devices)
     weights = (w_zero, w_one_re, w_one_im, w_two_re, w_two_im)
-    hot, radial, flags, vector, lent, *weights = pl.pallas_call(
-        functools.partial(scale_kernel, atoms, ghosts, slab_devices),
+    count = len(weights)
+    near_weights = [held(array.shape[1:], array.dtype) for array in weights]
+    side_shapes = [
+        held((edges, 2 * rows), BF16), held((layers, edges, channels), F32),
+        held((rows, edges), F32), held((atoms, 2 * ghosts), F32),
+    ]
+    hot, radial, flags, lent, vector, radial_weight, *first_weights = pl.pallas_call(
+        functools.partial(own_scale_kernel, atoms, ghosts, slab_devices, count),
         out_shape=[
-            held((2 * edges, 2 * rows), BF16), held((layers, 2 * edges, channels), F32),
-            held((rows, 2 * edges), F32), held((1, channels), F32), held((2, atoms, 2 * ghosts), F32),
-            *(held(array.shape, array.dtype) for array in weights),
+            *side_shapes, held((1, channels), F32), held(radial_weight.shape, F32),
+            *near_weights,
         ],
-        in_specs=[VMEM] * 4 + [far] * len(weights),
-        out_specs=[VMEM] * (5 + len(weights)),
-        scratch_shapes=[pltpu.SemaphoreType.DMA((len(weights),))],
+        in_specs=[VMEM] * 3 + [far] * count,
+        out_specs=[VMEM] * (6 + count),
+        scratch_shapes=[pltpu.SemaphoreType.DMA((count,))],
         compiler_params=params,
         name="scales",
-    )(*near(facts, partner), *away(radial_weight, row(readout), *weights))
+    )(*near(facts), *away(radial_weight, row(readout), *weights))
+    got_pair, facts, radial_weight = lax.optimization_barrier((got_pair, facts, radial_weight))
+    pair_y = across(got_pair, half, slab_devices)
+    other_y = across(got_other, half, slab_devices)
+    fetched = tuple(range(1, layers))
+    hot_y, radial_y, flags_y, lent_y, *later_weights = pl.pallas_call(
+        functools.partial(partner_scale_kernel, atoms, ghosts, slab_devices, count, fetched),
+        out_shape=[*side_shapes, *(near_weights * len(fetched))],
+        in_specs=[VMEM] * 2 + [far] * count,
+        out_specs=[VMEM] * (4 + count * len(fetched)),
+        scratch_shapes=[pltpu.SemaphoreType.DMA((len(fetched), count))],
+        compiler_params=params,
+        name="scales_y",
+    )(*near(partner, radial_weight), *away(*weights))
     dirs, pulls = pl.pallas_call(
         pull_kernel,
-        out_shape=[held((3, 2 * edges), F32), held((rows, 3 * channels), BF16)],
-        in_specs=[VMEM] * 4,
+        out_shape=[held((3, edges), F32), held((rows, 3 * channels), BF16)],
+        in_specs=[VMEM] * 6,
         out_specs=[VMEM] * 2,
         compiler_params=params,
         name="pulls",
-    )(*near(facts, partner, radial, flags))
+    )(*near(facts, radial, flags, partner, radial_y, flags_y))
+    weights = (*first_weights, *later_weights)
 
     bits = order_bits(slab_devices)
-    got_pair, hot, radial = lax.optimization_barrier((got_pair, hot, radial))
     blocks = {0: (own, got_pair, got_other)}
-    pair_y = across(got_pair, half, slab_devices)
-    other_y = across(got_other, half, slab_devices)
     blocks[half] = (got_own, pair_y, other_y)
     blocks = spread(blocks, bits[1:], slab_devices)
     tables = [
@@ -395,6 +450,7 @@
     scratch = [pltpu.VMEM((rows, width), F32), pltpu.VMEM((2 * rows, width), BF16)]
     per_atom = edges // atoms
     for layer in range(layers):
+        now = weights[layer * count : (layer + 1) * count]
         if layer < layers - 1:
             last = layer == layers - 2
             wide = width + ((half + 1) // 2 * 3 * channels if last else 0)
@@ -404,12 +460,12 @@
                     held((2 * atoms, wide), BF16), held((2 * ghosts, wide), BF16),
                     held((2 * ghosts, wide), BF16),
                 ],
-                in_specs=[VMEM] * (4 + len(tables) + len(weights)),
+                in_specs=[VMEM] * (7 + len(tables) + count),
                 out_specs=[VMEM] * 3,
                 scratch_shapes=scratch,
                 compiler_params=params,
                 name="layer",
-            )(*near(lent, hot, radial, pulls, *tables, *weights))
+            )(*near(lent, hot, radial, lent_y, hot_y, radial_y, pulls, *tables, *now))
             got_other = toward(other, -1, slabs)
             got_pair = toward(pair, 1, slabs)
             blocks = spread({0: (own, got_pair, got_other)}, bits[1:], slab_devices)
@@ -420,12 +476,12 @@
                     last_kernel, layer, degrees, channels, atoms, per_atom, len(tables)
                 ),
                 out_shape=[shape((coeffs, atoms, channels), BF16), shape((3, atoms), F32)],
-                in_specs=[VMEM] * (6 + len(tables) + len(weights)),
+                in_specs=[VMEM] * (6 + len(tables) + count),
                 out_specs=[VMEM] * 2,
                 scratch_shapes=scratch,
                 compiler_params=params,
                 name="last_layer",
-            )(*near(rest, lent, hot, radial, dirs, vector, *tables, *weights))
+            )(*near(rest, lent, hot, radial, dirs, vector, *tables, *now))
     return (updated.transpose(1, 0, 2), forces)
 
 

time: 38 us -> 35.7 us (0.939)
  waiting for transfers between devices: 12.3 us -> 9.17 us
  starting transfers between devices: 13.7 us -> 14.5 us
    ppermute x13, waiting for transfers between devices: 6.61 us -> 4.52 us  [across(): lax.ppermute(block, 'yz', [(q, q ^ bit) for q in range(slab_devices)])]
    ppermute x4, waiting for transfers between devices: 5.71 us -> 4.65 us  [toward(): return lax.ppermute(block, 'slab', route)]
    ppermute x4, starting transfers between devices: 6.98 us -> 7.86 us  [toward(): return lax.ppermute(block, 'slab', route)]
    pallas_call x2 -> x3, Pallas kernels: 4.7 us -> 4.76 us  [the longest x1 2.48 us: body(): pl.pallas_call(functools.partial(own_scale_kernel, atoms, ghosts, slab_de...]
  transfers between devices with their start and end apart: 17 -> 17, of which waited for: 7 -> 4; matrix products, arithmetic and copies ran while one was open for 0% -> 0% of each run, Pallas kernels for 12% -> 13%
where the time goes in v4:
time: 35.7 us; the launch traced here: 35.5 us
  starting transfers between devices  14.5 us (41%)
  Pallas kernels  11 us (31%)
  waiting for transfers between devices  9.17 us (26%)
  between operations  0.73 us (2%)
    ppermute x4, starting transfers between devices, toward(): return lax.ppermute(block, 'slab', route)  7.86 us
    ppermute x13, starting transfers between devices, across(): lax.ppermute(block, 'yz', [(q, q ^ bit) for q in range(slab_devices)])  6.69 us
    ppermute x4, waiting for transfers between devices, toward(): return lax.ppermute(block, 'slab', route)  4.65 us
    ppermute x13, waiting for transfers between devices, across(): lax.ppermute(block, 'yz', [(q, q ^ bit) for q in range(slab_devices)])  4.52 us
    pallas_call x1, Pallas kernels, body(): pl.pallas_call(functools.partial(last_kernel, layer, degrees, channels, a...  2.66 us
    pallas_call x1, Pallas kernels, body(): pl.pallas_call(functools.partial(own_scale_kernel, atoms, ghosts, slab_de...  2.48 us
    pallas_call x1, Pallas kernels, body(): pl.pallas_call(functools.partial(first_kernel, layer, last, degrees, chan...  2.39 us
    pallas_call x1, Pallas kernels, body(): pl.pallas_call(functools.partial(partner_scale_kernel, atoms, ghosts, sla...  1.67 us
  transfers between devices with their start and end apart: 17, of which 4 were waited for; matrix products, arithmetic and copies ran while one was open for 0% of the time, Pallas kernels for 13%

profile of v4, /device:TPU:0, one launch (start us, length us, event | category | flops | bytes accessed | tf_op | source)
XLA Modules:
  0.0 35.5 jit_solution(10427024492864854468)
XLA Ops:
  0.6 1.2 %pack.1 = (bf16[16,2432]{1,0:T(8,128)(2,1)S(1)}, bf16[8,2432]{1,0:T(8,128)(2,1)S(1)}, bf16[8,2432]{1,0:T(8,128)(2,1)S(1)}, bf16[6,16,128]{2,1,0:T(8,128)(2,1)S(1)}, f32[8,512]{1,0:T(8,128)S(1)}) custom-call(bf16[25,16,128]{2,1,0:T(8,128)(2,1)} %bitcast.10, s32[1,8]{1,0:T(1,128)} %bitcast.16, s32[1,8]{1,0:T(1,128)} %bitcast.17, s32[1,512]{1,0:T(1,128)} %bitcast.11, ...), custom_call_target="tpu_custom_call" | custom-call | tf_op jit(solution)/shard_map/pack/pallas_call | solution.py:383
  1.9 3.1 %collective-permute-start.2 = (bf16[16,2432]{1,0:T(8,128)(2,1)S(1)}, bf16[16,2432]{1,0:T(8,128)(2,1)S(1)}, u32[]{:S(2)}, u32[]{:S(2)}) collective-permute-start(bf16[16,2432]{1,0:T(8,128)(2,1)S(1)} %get-tuple-element.54.refs_0_), channel_id=1, source_target_pairs={{0,2},{1,3},{2,0},{3,1},{4,6},{5,7},{6,4},{7,5},{8,10},{9,11},{10,... | collective-permute-start | bytes 233480 | tf_op jit(solution)/shard_map/ppermute | solution.py:337
  4.9 1.5 %collective-permute-start = (bf16[8,2432]{1,0:T(8,128)(2,1)S(1)}, bf16[8,2432]{1,0:T(8,128)(2,1)S(1)}, u32[]{:S(2)}, u32[]{:S(2)}) collective-permute-start(bf16[8,2432]{1,0:T(8,128)(2,1)S(1)} %get-tuple-element.42), channel_id=1, source_target_pairs={{0,4},{4,0},{8,12},{12,8},{16,20},{20,16},{24,28},{28,24},{1,5},{5... | collective-permute-start | bytes 116744 | tf_op jit(solution)/shard_map/ppermute | solution.py:345
  6.4 3.6 %collective-permute-start.4 = (bf16[8,2432]{1,0:T(8,128)(2,1)S(1)}, bf16[8,2432]{1,0:T(8,128)(2,1)S(1)}, u32[]{:S(2)}, u32[]{:S(2)}) collective-permute-start(bf16[8,2432]{1,0:T(8,128)(2,1)S(1)} %get-tuple-element.56), channel_id=1, source_target_pairs={{0,28},{4,8},{8,4},{12,16},{16,12},{20,24},{24,20},{28,0},{1,29},{... | collective-permute-start | bytes 116744 | tf_op jit(solution)/shard_map/ppermute | solution.py:345
  10.0 0.0 collective-permute-start.6
  10.0 2.5 %scales.1 = (bf16[512,256]{1,0:T(8,128)(2,1)S(1)}, f32[2,512,128]{2,1,0:T(8,128)S(1)}, f32[128,512]{1,0:T(8,128)S(1)}, f32[16,16]{1,0:T(8,128)S(1)}, f32[1,128]{...) custom-call(f32[8,512]{1,0:T(8,128)S(1)} %get-tuple-element.44.facts, ...), custom_call_target="tpu_custom_call" | custom-call | tf_op jit(solution)/shard_map/scales/pallas_call | solution.py:407
  12.5 0.0 collective-permute-done.refs_2_
  12.5 0.6 %collective-permute-start.3 = (bf16[8,2432]{1,0:T(8,128)(2,1)S(1)}, bf16[8,2432]{1,0:T(8,128)(2,1)S(1)}, u32[]{:S(2)}, u32[]{:S(2)}) collective-permute-start(bf16[8,2432]{1,0:T(8,128)(2,1)S(1)} %collective-permute-done.refs_2_), channel_id=1, source_target_pairs={{0,2},{1,3},{2,0},{3,1},{4,6},{5,7},{6,4},{7,5},{8,10},{9,11},{10,... | collective-permute-start | bytes 116744 | tf_op jit(solution)/shard_map/ppermute | solution.py:337
  13.1 0.0 collective-permute-done.4.refs_4_
  13.1 1.5 %collective-permute-start.5 = (bf16[8,2432]{1,0:T(8,128)(2,1)S(1)}, bf16[8,2432]{1,0:T(8,128)(2,1)S(1)}, u32[]{:S(2)}, u32[]{:S(2)}) collective-permute-start(bf16[8,2432]{1,0:T(8,128)(2,1)S(1)} %collective-permute-done.4.refs_4_), channel_id=1, source_target_pairs={{0,2},{1,3},{2,0},{3,1},{4,6},{5,7},{6,4},{7,5},{8,10},{9,11},{10,... | collective-permute-start | bytes 116744 | tf_op jit(solution)/shard_map/ppermute | solution.py:337
  14.6 0.0 collective-permute-done.2.refs_1_
  14.6 0.0 collective-permute-start.7
  14.6 0.5 %collective-permute-start.1 = (f32[8,512]{1,0:T(8,128)S(1)}, f32[8,512]{1,0:T(8,128)S(1)}, u32[]{:S(2)}, u32[]{:S(2)}) collective-permute-start(f32[8,512]{1,0:T(8,128)S(1)} %get-tuple-element.44.facts_ref), channel_id=1, source_target_pairs={{0,2},{1,3},{2,0},{3,1},{4,6},{5,7},{6,4},{7,5},{8,10},{9,11},{10,... | collective-permute-start | bytes 49160 | tf_op jit(solution)/shard_map/ppermute | solution.py:337
  15.1 3.2 %collective-permute-done.1.facts_ref.partner_ref = f32[8,512]{1,0:T(8,128)S(1)} collective-permute-done((f32[8,512]{1,0:T(8,128)S(1)}, f32[8,512]{1,0:T(8,128)S(1)}, u32[]{:S(2)}, u32[]{:S(2)}) %collective-permute-start.1) | collective-permute-done | bytes 16416 | tf_op jit(solution)/shard_map/ppermute | solution.py:337
  18.3 0.0 collective-permute-start.8
  18.3 0.0 collective-permute-done.3.refs_3_
  18.3 0.5 %collective-permute-start.10 = (bf16[8,2432]{1,0:T(8,128)(2,1)S(1)}, bf16[8,2432]{1,0:T(8,128)(2,1)S(1)}, u32[]{:S(2)}, u32[]{:S(2)}) collective-permute-start(bf16[8,2432]{1,0:T(8,128)(2,1)S(1)} %collective-permute-done.4.refs_4_), channel_id=1, source_target_pairs={{0,1},{1,0},{2,3},{3,2},{4,5},{5,4},{6,7},{7,6},{8,9},{9,8},{10,11... | collective-permute-start | bytes 116744 | tf_op jit(solution)/shard_map/ppermute | solution.py:337
  18.9 0.0 collective-permute-done.5.refs_5_
  18.9 0.1 collective-permute-start.9
  18.9 0.4 %collective-permute-start.11 = (bf16[8,2432]{1,0:T(8,128)(2,1)S(1)}, bf16[8,2432]{1,0:T(8,128)(2,1)S(1)}, u32[]{:S(2)}, u32[]{:S(2)}) collective-permute-start(bf16[8,2432]{1,0:T(8,128)(2,1)S(1)} %collective-permute-done.5.refs_5_), channel_id=1, source_target_pairs={{0,1},{1,0},{2,3},{3,2},{4,5},{5,4},{6,7},{7,6},{8,9},{9,8},{10,11... | collective-permute-start | bytes 116744 | tf_op jit(solution)/shard_map/ppermute | solution.py:337
  19.4 1.7 %scales_y.1 = (bf16[512,256]{1,0:T(8,128)(2,1)S(1)}, f32[2,512,128]{2,1,0:T(8,128)S(1)}, f32[128,512]{1,0:T(8,128)S(1)}, f32[16,16]{1,0:T(8,128)S(1)}, bf16[640,...) custom-call(f32[8,512]{1,0:T(8,128)S(1)} %collective-permute-done.1., ...), custom_call_target="tpu_custom_call" | custom-call | tf_op jit(solution)/shard_map/scales_y/pallas_call | solution.py:423
  21.0 0.6 %pulls.1 = (f32[3,512]{1,0:T(4,128)S(1)}, bf16[128,384]{1,0:T(8,128)(2,1)S(1)}) custom-call(f32[8,512]{1,0:T(8,128)S(1)} %get-tuple-element.44.facts_ref, f32[2,512,128]{2,1,0:T(8,128)S(1)} %get-tuple-element.41.radial_ref, f32[128,512]{1,0:T(8,128)S(1)} %get-tuple-element.45.flags_ref, f32[8,512]{1,0:T(8,128)S(1)} %collective-permute-done.1.facts_ref.partner_ref, ...), custom_call_target="tpu_custom_call" | custom-call | tf_op jit(solution)/shard_map/pulls/pallas_call | solution.py:432
  21.7 0.0 collective-permute-done.10.refs_10_
  21.7 0.0 collective-permute-done.9.refs_9_
  21.7 2.4 %layer.1 = (bf16[32,2816]{1,0:T(8,128)(2,1)S(1)}, bf16[16,2816]{1,0:T(8,128)(2,1)S(1)}, bf16[16,2816]{1,0:T(8,128)(2,1)S(1)}) custom-call(f32[16,16]{1,0:T(8,128)S(1)} %get-tuple-element.39.lent_ref, bf16[512,256]{1,0:T(8,128)(2,1)S(1)} %get-tuple-element.40.hot_ref, f32[2,512,128]{2,1,0:T(8,128)S(1)} %get-tuple-element.41.radial_ref, ...), custom_call_target="tpu_custom_call" | custom-call | tf_op jit(solution)/shard_map/layer/pallas_call | solution.py:457
  24.1 0.1 collective-permute-start.12
  24.2 2.7 %collective-permute-start.13 = (bf16[16,2816]{1,0:T(8,128)(2,1)S(1)}, bf16[16,2816]{1,0:T(8,128)(2,1)S(1)}, u32[]{:S(2)}, u32[]{:S(2)}) collective-permute-start(bf16[16,2816]{1,0:T(8,128)(2,1)S(1)} %get-tuple-element.64), channel_id=1, source_target_pairs={{0,28},{4,8},{8,4},{12,16},{16,12},{20,24},{24,20},{28,0},{1,29},{... | collective-permute-start | bytes 270344 | tf_op jit(solution)/shard_map/ppermute | solution.py:345
  26.9 1.8 %collective-permute-done.12.refs_1_ = bf16[16,2816]{1,0:T(8,128)(2,1)S(1)} collective-permute-done((bf16[16,2816]{1,0:T(8,128)(2,1)S(1)}, bf16[16,2816]{1,0:T(8,128)(2,1)S(1)}, u32[]{:S(2)}, u32[]{:S(2)}) %collective-permute-start.12) | collective-permute-done | bytes 90144 | tf_op jit(solution)/shard_map/ppermute | solution.py:345
  28.8 0.0 collective-permute-start.15
  28.8 2.8 %collective-permute-done.13.refs_2_ = bf16[16,2816]{1,0:T(8,128)(2,1)S(1)} collective-permute-done((bf16[16,2816]{1,0:T(8,128)(2,1)S(1)}, bf16[16,2816]{1,0:T(8,128)(2,1)S(1)}, u32[]{:S(2)}, u32[]{:S(2)}) %collective-permute-start.13) | collective-permute-done | bytes 90144 | tf_op jit(solution)/shard_map/ppermute | solution.py:345
  31.5 1.3 %collective-permute-done.16.refs_5_ = bf16[16,2816]{1,0:T(8,128)(2,1)S(1)} collective-permute-done((bf16[16,2816]{1,0:T(8,128)(2,1)S(1)}, bf16[16,2816]{1,0:T(8,128)(2,1)S(1)}, u32[]{:S(2)}, u32[]{:S(2)}) %collective-permute-start.16) | collective-permute-done | bytes 90144 | tf_op jit(solution)/shard_map/ppermute | solution.py:337
  32.8 2.7 %last_layer.1 = (bf16[25,16,128]{2,1,0:T(8,128)(2,1)}, f32[3,16]{1,0:T(4,128)}) custom-call(bf16[6,16,128]{2,1,0:T(8,128)(2,1)S(1)} %get-tuple-element.37.rest_ref, f32[16,16]{1,0:T(8,128)S(1)} %get-tuple-element.39.lent_ref, bf16[512,256]{1,0:T(8,128)(2,1)S(1)} %get-tuple-element.40.hot_ref, f32[2,512,128]{2,1,0:T(8,128)S(1)} %get-tuple-element.41.radial_ref, ...), custom_call_target="tpu_custom_call" | custom-call | tf_op jit(solution)/shard_map/last_layer/pallas_call | solution.py:474
  (8 shorter events, 0.0 us)
Async XLA Ops:
  1.9 12.7 %collective-permute-start.2 = (bf16[16,2432]{1,0:T(8,128)(2,1)S(1)}, bf16[16,2432]{1,0:T(8,128)(2,1)S(1)}, u32[]{:S(2)}, u32[]{:S(2)}) collective-permute-start(bf16[16,2432]{1,0:T(8,128)(2,1)S(1)} %get-tuple-element.54.refs_0_), channel_id=1, source_target_pairs={{0,2},{1,3},{2,0},{3,1},{4,6},{5,7},{6,4},{7,5},{8,10},{9,11},{10,... | collective-permute-start | bytes 233480 | tf_op jit(solution)/shard_map/ppermute | solution.py:337
  4.9 7.6 %collective-permute-start = (bf16[8,2432]{1,0:T(8,128)(2,1)S(1)}, bf16[8,2432]{1,0:T(8,128)(2,1)S(1)}, u32[]{:S(2)}, u32[]{:S(2)}) collective-permute-start(bf16[8,2432]{1,0:T(8,128)(2,1)S(1)} %get-tuple-element.42), channel_id=1, source_target_pairs={{0,4},{4,0},{8,12},{12,8},{16,20},{20,16},{24,28},{28,24},{1,5},{5... | collective-permute-start | bytes 116744 | tf_op jit(solution)/shard_map/ppermute | solution.py:345
  6.4 6.7 %collective-permute-start.4 = (bf16[8,2432]{1,0:T(8,128)(2,1)S(1)}, bf16[8,2432]{1,0:T(8,128)(2,1)S(1)}, u32[]{:S(2)}, u32[]{:S(2)}) collective-permute-start(bf16[8,2432]{1,0:T(8,128)(2,1)S(1)} %get-tuple-element.56), channel_id=1, source_target_pairs={{0,28},{4,8},{8,4},{12,16},{16,12},{20,24},{24,20},{28,0},{1,29},{... | collective-permute-start | bytes 116744 | tf_op jit(solution)/shard_map/ppermute | solution.py:345
  10.0 8.9 %collective-permute-start.6 = (bf16[16,2432]{1,0:T(8,128)(2,1)S(1)}, bf16[16,2432]{1,0:T(8,128)(2,1)S(1)}, u32[]{:S(2)}, u32[]{:S(2)}) collective-permute-start(bf16[16,2432]{1,0:T(8,128)(2,1)S(1)} %get-tuple-element.54.refs_0_), channel_id=1, source_target_pairs={{0,1},{1,0},{2,3},{3,2},{4,5},{5,4},{6,7},{7,6},{8,9},{9,8},{10,11... | collective-permute-start | bytes 233480 | tf_op jit(solution)/shard_map/ppermute | solution.py:337
  12.5 5.8 %collective-permute-start.3 = (bf16[8,2432]{1,0:T(8,128)(2,1)S(1)}, bf16[8,2432]{1,0:T(8,128)(2,1)S(1)}, u32[]{:S(2)}, u32[]{:S(2)}) collective-permute-start(bf16[8,2432]{1,0:T(8,128)(2,1)S(1)} %collective-permute-done.refs_2_), channel_id=1, source_target_pairs={{0,2},{1,3},{2,0},{3,1},{4,6},{5,7},{6,4},{7,5},{8,10},{9,11},{10,... | collective-permute-start | bytes 116744 | tf_op jit(solution)/shard_map/ppermute | solution.py:337
  13.1 5.8 %collective-permute-start.5 = (bf16[8,2432]{1,0:T(8,128)(2,1)S(1)}, bf16[8,2432]{1,0:T(8,128)(2,1)S(1)}, u32[]{:S(2)}, u32[]{:S(2)}) collective-permute-start(bf16[8,2432]{1,0:T(8,128)(2,1)S(1)} %collective-permute-done.4.refs_4_), channel_id=1, source_target_pairs={{0,2},{1,3},{2,0},{3,1},{4,6},{5,7},{6,4},{7,5},{8,10},{9,11},{10,... | collective-permute-start | bytes 116744 | tf_op jit(solution)/shard_map/ppermute | solution.py:337
  14.6 7.1 %collective-permute-start.7 = (bf16[16,2432]{1,0:T(8,128)(2,1)S(1)}, bf16[16,2432]{1,0:T(8,128)(2,1)S(1)}, u32[]{:S(2)}, u32[]{:S(2)}) collective-permute-start(bf16[16,2432]{1,0:T(8,128)(2,1)S(1)} %collective-permute-done.2.refs_1_), channel_id=1, source_target_pairs={{0,1},{1,0},{2,3},{3,2},{4,5},{5,4},{6,7},{7,6},{8,9},{9,8},{10,11... | collective-permute-start | bytes 233480 | tf_op jit(solution)/shard_map/ppermute | solution.py:337
  14.6 3.7 %collective-permute-start.1 = (f32[8,512]{1,0:T(8,128)S(1)}, f32[8,512]{1,0:T(8,128)S(1)}, u32[]{:S(2)}, u32[]{:S(2)}) collective-permute-start(f32[8,512]{1,0:T(8,128)S(1)} %get-tuple-element.44.facts_ref), channel_id=1, source_target_pairs={{0,2},{1,3},{2,0},{3,1},{4,6},{5,7},{6,4},{7,5},{8,10},{9,11},{10,... | collective-permute-start | bytes 49160 | tf_op jit(solution)/shard_map/ppermute | solution.py:337
  18.3 3.3 %collective-permute-start.8 = (bf16[8,2432]{1,0:T(8,128)(2,1)S(1)}, bf16[8,2432]{1,0:T(8,128)(2,1)S(1)}, u32[]{:S(2)}, u32[]{:S(2)}) collective-permute-start(bf16[8,2432]{1,0:T(8,128)(2,1)S(1)} %collective-permute-done.refs_2_), channel_id=1, source_target_pairs={{0,1},{1,0},{2,3},{3,2},{4,5},{5,4},{6,7},{7,6},{8,9},{9,8},{10,11... | collective-permute-start | bytes 116744 | tf_op jit(solution)/shard_map/ppermute | solution.py:337
  18.3 3.3 %collective-permute-start.10 = (bf16[8,2432]{1,0:T(8,128)(2,1)S(1)}, bf16[8,2432]{1,0:T(8,128)(2,1)S(1)}, u32[]{:S(2)}, u32[]{:S(2)}) collective-permute-start(bf16[8,2432]{1,0:T(8,128)(2,1)S(1)} %collective-permute-done.4.refs_4_), channel_id=1, source_target_pairs={{0,1},{1,0},{2,3},{3,2},{4,5},{5,4},{6,7},{7,6},{8,9},{9,8},{10,11... | collective-permute-start | bytes 116744 | tf_op jit(solution)/shard_map/ppermute | solution.py:337
  18.9 2.8 %collective-permute-start.9 = (bf16[8,2432]{1,0:T(8,128)(2,1)S(1)}, bf16[8,2432]{1,0:T(8,128)(2,1)S(1)}, u32[]{:S(2)}, u32[]{:S(2)}) collective-permute-start(bf16[8,2432]{1,0:T(8,128)(2,1)S(1)} %collective-permute-done.3.refs_3_), channel_id=1, source_target_pairs={{0,1},{1,0},{2,3},{3,2},{4,5},{5,4},{6,7},{7,6},{8,9},{9,8},{10,11... | collective-permute-start | bytes 116744 | tf_op jit(solution)/shard_map/ppermute | solution.py:337
  18.9 2.8 %collective-permute-start.11 = (bf16[8,2432]{1,0:T(8,128)(2,1)S(1)}, bf16[8,2432]{1,0:T(8,128)(2,1)S(1)}, u32[]{:S(2)}, u32[]{:S(2)}) collective-permute-start(bf16[8,2432]{1,0:T(8,128)(2,1)S(1)} %collective-permute-done.5.refs_5_), channel_id=1, source_target_pairs={{0,1},{1,0},{2,3},{3,2},{4,5},{5,4},{6,7},{7,6},{8,9},{9,8},{10,11... | collective-permute-start | bytes 116744 | tf_op jit(solution)/shard_map/ppermute | solution.py:337
  24.1 4.7 %collective-permute-start.12 = (bf16[16,2816]{1,0:T(8,128)(2,1)S(1)}, bf16[16,2816]{1,0:T(8,128)(2,1)S(1)}, u32[]{:S(2)}, u32[]{:S(2)}) collective-permute-start(bf16[16,2816]{1,0:T(8,128)(2,1)S(1)} %get-tuple-element.63), channel_id=1, source_target_pairs={{0,4},{4,0},{8,12},{12,8},{16,20},{20,16},{24,28},{28,24},{1,5},{5... | collective-permute-start | bytes 270344 | tf_op jit(solution)/shard_map/ppermute | solution.py:345
  24.2 7.4 %collective-permute-start.13 = (bf16[16,2816]{1,0:T(8,128)(2,1)S(1)}, bf16[16,2816]{1,0:T(8,128)(2,1)S(1)}, u32[]{:S(2)}, u32[]{:S(2)}) collective-permute-start(bf16[16,2816]{1,0:T(8,128)(2,1)S(1)} %get-tuple-element.64), channel_id=1, source_target_pairs={{0,28},{4,8},{8,4},{12,16},{16,12},{20,24},{24,20},{28,0},{1,29},{... | collective-permute-start | bytes 270344 | tf_op jit(solution)/shard_map/ppermute | solution.py:345
  26.9 5.9 %collective-permute-start.14 = (bf16[32,2816]{1,0:T(8,128)(2,1)S(1)}, bf16[32,2816]{1,0:T(8,128)(2,1)S(1)}, u32[]{:S(2)}, u32[]{:S(2)}) collective-permute-start(bf16[32,2816]{1,0:T(8,128)(2,1)S(1)} %get-tuple-element.62.refs_0_), channel_id=1, source_target_pairs={{0,1},{1,0},{2,3},{3,2},{4,5},{5,4},{6,7},{7,6},{8,9},{9,8},{10,11... | collective-permute-start | bytes 540680 | tf_op jit(solution)/shard_map/ppermute | solution.py:337
  28.8 2.8 %collective-permute-start.15 = (bf16[16,2816]{1,0:T(8,128)(2,1)S(1)}, bf16[16,2816]{1,0:T(8,128)(2,1)S(1)}, u32[]{:S(2)}, u32[]{:S(2)}) collective-permute-start(bf16[16,2816]{1,0:T(8,128)(2,1)S(1)} %collective-permute-done.12.refs_1_), channel_id=1, source_target_pairs={{0,1},{1,0},{2,3},{3,2},{4,5},{5,4},{6,7},{7,6},{8,9},{9,8},{10,11... | collective-permute-start | bytes 270344 | tf_op jit(solution)/shard_map/ppermute | solution.py:337
  31.5 1.3 %collective-permute-start.16 = (bf16[16,2816]{1,0:T(8,128)(2,1)S(1)}, bf16[16,2816]{1,0:T(8,128)(2,1)S(1)}, u32[]{:S(2)}, u32[]{:S(2)}) collective-permute-start(bf16[16,2816]{1,0:T(8,128)(2,1)S(1)} %collective-permute-done.13.refs_2_), channel_id=1, source_target_pairs={{0,1},{1,0},{2,3},{3,2},{4,5},{5,4},{6,7},{7,6},{8,9},{9,8},{10,11... | collective-permute-start | bytes 270344 | tf_op jit(solution)/shard_map/ppermute | solution.py:337

commit v5 on v4

--- a/solution.py
+++ b/solution.py
@@ -13,6 +13,7 @@
 BF16 = jnp.bfloat16
 F32 = jnp.float32
 ORDERS = (1, 2)
+DIGIT = 128
 VMEM = pl.BlockSpec(memory_space=pltpu.VMEM)
 
 
@@ -70,29 +71,52 @@
     return dot(hot.astype(BF16), rows, ((0,), (0,))).astype(BF16)
 
 
+def thirds(value):
+    parts = []
+    for _ in range(3):
+        part = value.astype(BF16).astype(F32)
+        parts.append(part)
+        value = value - part
+    return parts
+
+
 def pack_kernel(
-    emb_ref, low_ref, high_ref, nbr_ref, valid_ref, dist_ref, azi_ref, pol_ref,
-    own_ref, pair_ref, other_ref, rest_ref, facts_ref,
+    emb_ref, low_ref, high_ref, nbr_ref, valid_ref, dist_ref, azi_ref, pol_ref, rw_ref, readout_ref,
+    own_ref, pair_ref, other_ref, rest_ref, scales_ref, vector_ref,
 ):
     coeffs, atoms, channels = emb_ref.shape
     ghosts = low_ref.shape[1]
     edges = nbr_ref.shape[1]
     order = slot_order(math.isqrt(coeffs))
+    width = len(order) * channels
     for place, slot in enumerate(order):
         own_ref[:, place * channels : (place + 1) * channels] = emb_ref[slot]
     for place, slot in enumerate(unused_slots(coeffs)):
         rest_ref[place] = emb_ref[slot]
     picks = lent_picks(low_ref, high_ref)
-    lent = lent_rows(lent_hot(picks, atoms), own_ref[...])
+    lent = lent_rows(lent_hot(picks, atoms), own_ref[:, :width])
     pair_ref[...] = lent[:ghosts]
     other_ref[...] = lent[ghosts:]
-    facts_ref[...] = jnp.zeros(facts_ref.shape, F32)
-    facts_ref[0:1, :edges] = nbr_ref[...].astype(F32)
-    facts_ref[1:2, :edges] = valid_ref[...].astype(F32)
-    facts_ref[2:3, :edges] = dist_ref[...]
-    facts_ref[3:4, :edges] = azi_ref[...]
-    facts_ref[4:5, :edges] = pol_ref[...]
-    facts_ref[5:6, : 2 * ghosts] = picks.astype(F32)
+    nbr = nbr_ref[...]
+    picks = jnp.concatenate(
+        [picks, jnp.zeros((1, edges - 2 * ghosts), jnp.int32)], axis=1
+    ).astype(F32)
+    facts = [
+        (nbr // DIGIT).astype(F32), (nbr % DIGIT).astype(F32), valid_ref[...].astype(F32), picks,
+        *thirds(dist_ref[...]), *thirds(azi_ref[...]), *thirds(pol_ref[...]),
+    ]
+    facts.append(jnp.zeros((atoms - len(facts), edges), F32))
+    own_ref[:, width:] = jnp.concatenate(facts, axis=0).astype(BF16)
+    scales_ref[...] = rw_ref[...]
+    vector_ref[...] = 0.125 * readout_ref[...]
+
+
+def edge_facts(ref, edges):
+    rows = ref[:, ref.shape[1] - edges :].astype(F32)
+    row = lambda at: rows[at : at + 1]
+    whole = lambda at: row(at) + row(at + 1) + row(at + 2)
+    nbr = (row(0) * DIGIT + row(1)).astype(jnp.int32)
+    return nbr, row(2), row(3).astype(jnp.int32), whole(4), whole(7), whole(10)
 
 
 def start_fetch(refs, layer):
@@ -115,7 +139,7 @@
     me = lax.axis_index("yz")
     odd = odd_slab()
     edges = hot_ref.shape[0]
-    nbr = facts_ref[0:1, :edges].astype(jnp.int32)
+    nbr, valid, picks, distance, _, _ = edge_facts(facts_ref, edges)
     is_own = nbr < own_count
     ghost = nbr - own_count
     below = ghost < ghost_count
@@ -130,45 +154,24 @@
     )
     place = (slot % half) * (2 * atoms + 4 * ghosts) + inner
     rows = lax.broadcasted_iota(jnp.int32, (flags_ref.shape[0], edges), 0)
-    hot = jnp.where((rows == place) & (facts_ref[1:2, :edges] != 0.0), 1.0, 0.0).astype(F32)
+    hot = jnp.where((rows == place) & (valid != 0.0), 1.0, 0.0).astype(F32)
     flags_ref[...] = hot
     hot_cols = jnp.transpose(hot).astype(BF16)
     hot_ref[...] = jnp.concatenate([hot_cols, hot_cols], axis=1)
     middle = 1.0 + 0.5 * lax.broadcasted_iota(jnp.int32, (centers, edges), 0).astype(F32)
-    basis = jnp.exp(-jnp.square((facts_ref[2:3, :edges] - middle) / 0.5))
+    basis = jnp.exp(-jnp.square((distance - middle) / 0.5))
     for layer in range(layers):
         scale = dot(basis, rw_ref[layer], ((0,), (0,)), HIGHEST)
         radial_ref[layer] = scale / (1.0 + jnp.exp(-scale))
-    lent_ref[...] = lent_hot(facts_ref[5:6, : 2 * ghosts].astype(jnp.int32), atoms)
-
-
-def own_scale_kernel(
-    atoms, ghosts, slab_devices, count,
-    facts_ref, rw_ref, readout_ref, *refs,
-):
+    lent_ref[...] = lent_hot(picks[:, : 2 * ghosts], atoms)
+
+
+def scale_kernel(atoms, ghosts, slab_devices, count, facts_ref, rw_ref, *refs):
     far, refs = refs[:count], refs[count:]
-    hot_ref, radial_ref, flags_ref, lent_ref, vector_ref, scales_ref = refs[:6]
-    copies = start_fetch((*far, *refs[6:]), 0)
-    vector_ref[...] = 0.125 * readout_ref[...]
-    scales_ref[...] = rw_ref[...]
-    edge_scales(
-        atoms, ghosts, slab_devices, facts_ref, rw_ref, hot_ref, radial_ref, flags_ref, lent_ref
-    )
+    copies = start_fetch((*far, *refs[4:]), 0) if count else ()
+    edge_scales(atoms, ghosts, slab_devices, facts_ref, rw_ref, *refs[:4])
     for copy in copies:
         copy.wait()
-
-
-def partner_scale_kernel(
-    atoms, ghosts, slab_devices, count, fetched,
-    facts_ref, rw_ref, *refs,
-):
-    far, refs = refs[:count], refs[count:]
-    copies = [start_fetch((*far, *refs[4 + count * i : 4 + count * (i + 1)], refs[-1].at[i]), layer)
-              for i, layer in enumerate(fetched)]
-    edge_scales(atoms, ghosts, slab_devices, facts_ref, rw_ref, *refs[:4])
-    for group in copies:
-        for copy in group:
-            copy.wait()
 
 
 def pull_kernel(
@@ -181,11 +184,13 @@
     for ref, scale_ref, hot_ref in (
         (facts_ref, radial_ref, flags_ref), (partner_ref, radial_y_ref, flags_y_ref)
     ):
-        azimuth, polar = ref[3:4, :edges], ref[4:5, :edges]
+        _, _, _, _, azimuth, polar = edge_facts(ref, edges)
         sin_polar = jnp.sin(polar)
         dirs = [sin_polar * jnp.cos(azimuth), sin_polar * jnp.sin(azimuth), jnp.cos(polar)]
         if ref is facts_ref:
-            dirs_ref[...] = jnp.concatenate(dirs, axis=0)
+            columns = jnp.transpose(jnp.concatenate([*dirs, *dirs, *dirs[:2]], axis=0))
+            for axis in range(3):
+                dirs_ref[axis] = jnp.broadcast_to(columns[:, axis : axis + 1], (edges, channels))
         radial = scale_ref[last]
         high = radial.astype(BF16)
         both = jnp.concatenate([high, (radial - high.astype(F32)).astype(BF16)], axis=1)
@@ -256,9 +261,10 @@
     layer, last, degrees, channels, per_atom, count,
     lent_ref, hot_ref, radial_ref, lent_y_ref, hot_y_ref, radial_y_ref, pulls_ref, *refs,
 ):
-    tables, weights = refs[:count], refs[count : count + 5]
-    own_ref, pair_ref, other_ref = refs[count + 5 : count + 8]
-    scratch = refs[count + 8 :]
+    tables, weights, far = refs[:count], refs[count : count + 5], refs[count + 5 : count + 10]
+    own_ref, pair_ref, other_ref = refs[count + 10 : count + 13]
+    scratch = refs[count + 18 : count + 20]
+    copies = start_fetch((*far, *refs[count + 13 : count + 18], refs[-1]), layer + 1)
     joined = scratch[0]
     both = own_ref.shape[0]
     atoms, ghosts = both // 2, lent_ref.shape[1] // 2
@@ -284,6 +290,8 @@
                 to = slot % 2 * size
                 ref[to : to + size, cols] = pulls_ref[at : at + size]
                 at += 2 * size
+    for copy in copies:
+        copy.wait()
 
 
 def last_kernel(
@@ -304,33 +312,30 @@
     for place, slot in enumerate(unused_slots(degrees * degrees)):
         out_ref[slot] = rest_ref[place]
 
-    readout = readout_ref[...]
-    strength = dot(readout, first, ((1,), (1,)), HIGHEST)
-    edges = atoms * per_atom
-    pull = dirs_ref[...] * strength
-    edge = lax.broadcasted_iota(jnp.int32, (atoms, edges), 1)
-    atom = lax.broadcasted_iota(jnp.int32, (atoms, edges), 0)
-    owner = (edge // per_atom == atom).astype(F32)
-    own_force = dot(pull, owner, ((1,), (1,)), HIGHEST)
-
     width = len(sums) * channels
     part = 3 * channels
     ghosts = lent_ref.shape[1] // 2
-    kinds = [0.0, 0.0, 0.0]
+    own, lent = 0.0, []
     for slot in range(count // 3):
         cols = slice(width + slot // 2 * part, width + (slot // 2 + 1) * part)
-        for kind, size in enumerate((atoms, ghosts, ghosts)):
-            at = slot % 2 * size
-            kinds[kind] += tables[3 * slot + kind][at : at + size, cols].astype(F32)
-    lent = jnp.concatenate(kinds[1:], axis=0)
-    pulls = kinds[0] + dot(lent_ref[...], lent, precision=HIGHEST)
-    mine = zero[:atoms, :channels] * readout
-    ones = jnp.ones((1, channels), F32)
+        own_rows, *lent_blocks = (
+            tables[3 * slot + kind][slot % 2 * size : (slot % 2 + 1) * size, cols].astype(F32)
+            for kind, size in enumerate((atoms, ghosts, ghosts))
+        )
+        own += own_rows
+        lent += lent_blocks
+    hot = jnp.concatenate([lent_ref[...]] * (count // 3), axis=1).astype(BF16)
+    pulls = own + dot(hot, jnp.concatenate(lent, axis=0).astype(BF16))
+    readout = readout_ref[...]
+    parts = []
     for axis in range(3):
-        back = dot(
-            ones, mine * pulls[:, axis * channels : (axis + 1) * channels], ((1,), (1,)), HIGHEST
-        )
-        force_ref[axis : axis + 1, :] = own_force[axis : axis + 1] - back
+        pull = (first * dirs_ref[axis]).reshape(atoms, per_atom, channels).sum(axis=1)
+        back = zero[:atoms, :channels] * pulls[:, axis * channels : (axis + 1) * channels]
+        parts.append((pull - back) * readout)
+    ones = jnp.ones((8, channels), F32)
+    total = dot(ones, jnp.concatenate(parts, axis=0), ((1,), (1,)), HIGHEST)
+    for axis in range(3):
+        force_ref[axis : axis + 1, :] = total[:1, axis * atoms : (axis + 1) * atoms]
 
 
 def across(block, bit, slab_devices):
@@ -380,20 +385,22 @@
     far = pl.BlockSpec(memory_space=pl.ANY)
 
     half = slab_devices // 2
-    own, pair, other, rest, facts = pl.pallas_call(
+    own, pair, other, rest, radial_weight, vector = pl.pallas_call(
         pack_kernel,
         out_shape=[
-            held((atoms, width), BF16), held((ghosts, width), BF16), held((ghosts, width), BF16),
-            held((len(unused_slots(coeffs)), atoms, channels), BF16),
-            held((8, max(edges, 2 * ghosts)), F32),
+            held((atoms, width + edges), BF16), held((ghosts, width), BF16),
+            held((ghosts, width), BF16), held((len(unused_slots(coeffs)), atoms, channels), BF16),
+            held(radial_weight.shape, F32), held((1, channels), F32),
         ],
-        in_specs=[VMEM] * 8,
-        out_specs=[VMEM] * 5,
+        in_specs=[VMEM] * 10,
+        out_specs=[VMEM] * 6,
         compiler_params=params,
         name="pack",
-    )(*away(embeddings, low, high, *map(row, (neighbours, valid, distance, azimuth, polar))))
-
-    partner = across(facts, half, slab_devices)
+    )(*away(
+        embeddings, low, high, *map(row, (neighbours, valid, distance, azimuth, polar)),
+        radial_weight, row(readout),
+    ))
+
     got_other = toward(other, -1, slabs)
     got_pair = toward(pair, 1, slabs)
     got_own = across(own, half, slab_devices)
@@ -404,40 +411,34 @@
         held((edges, 2 * rows), BF16), held((layers, edges, channels), F32),
         held((rows, edges), F32), held((atoms, 2 * ghosts), F32),
     ]
-    hot, radial, flags, lent, vector, radial_weight, *first_weights = pl.pallas_call(
-        functools.partial(own_scale_kernel, atoms, ghosts, slab_devices, count),
-        out_shape=[
-            *side_shapes, held((1, channels), F32), held(radial_weight.shape, F32),
-            *near_weights,
-        ],
-        in_specs=[VMEM] * 3 + [far] * count,
-        out_specs=[VMEM] * (6 + count),
+    hot, radial, flags, lent = pl.pallas_call(
+        functools.partial(scale_kernel, atoms, ghosts, slab_devices, 0),
+        out_shape=side_shapes,
+        in_specs=[VMEM] * 2,
+        out_specs=[VMEM] * 4,
+        compiler_params=params,
+        name="scales",
+    )(*near(own, radial_weight))
+    got_pair, flags = lax.optimization_barrier((got_pair, flags))
+    pair_y = across(got_pair, half, slab_devices)
+    other_y = across(got_other, half, slab_devices)
+    hot_y, radial_y, flags_y, lent_y, *now = pl.pallas_call(
+        functools.partial(scale_kernel, atoms, ghosts, slab_devices, count),
+        out_shape=[*side_shapes, *near_weights],
+        in_specs=[VMEM] * 2 + [far] * count,
+        out_specs=[VMEM] * (4 + count),
         scratch_shapes=[pltpu.SemaphoreType.DMA((count,))],
         compiler_params=params,
-        name="scales",
-    )(*near(facts), *away(radial_weight, row(readout), *weights))
-    got_pair, facts, radial_weight = lax.optimization_barrier((got_pair, facts, radial_weight))
-    pair_y = across(got_pair, half, slab_devices)
-    other_y = across(got_other, half, slab_devices)
-    fetched = tuple(range(1, layers))
-    hot_y, radial_y, flags_y, lent_y, *later_weights = pl.pallas_call(
-        functools.partial(partner_scale_kernel, atoms, ghosts, slab_devices, count, fetched),
-        out_shape=[*side_shapes, *(near_weights * len(fetched))],
-        in_specs=[VMEM] * 2 + [far] * count,
-        out_specs=[VMEM] * (4 + count * len(fetched)),
-        scratch_shapes=[pltpu.SemaphoreType.DMA((len(fetched), count))],
-        compiler_params=params,
         name="scales_y",
-    )(*near(partner, radial_weight), *away(*weights))
+    )(*near(got_own, radial_weight), *away(*weights))
     dirs, pulls = pl.pallas_call(
         pull_kernel,
-        out_shape=[held((3, edges), F32), held((rows, 3 * channels), BF16)],
+        out_shape=[held((3, edges, channels), F32), held((rows, 3 * channels), BF16)],
         in_specs=[VMEM] * 6,
         out_specs=[VMEM] * 2,
         compiler_params=params,
         name="pulls",
-    )(*near(facts, radial, flags, partner, radial_y, flags_y))
-    weights = (*first_weights, *later_weights)
+    )(*near(own, radial, flags, got_own, radial_y, flags_y))
 
     bits = order_bits(slab_devices)
     blocks = {0: (own, got_pair, got_other)}
@@ -450,22 +451,21 @@
     scratch = [pltpu.VMEM((rows, width), F32), pltpu.VMEM((2 * rows, width), BF16)]
     per_atom = edges // atoms
     for layer in range(layers):
-        now = weights[layer * count : (layer + 1) * count]
         if layer < layers - 1:
             last = layer == layers - 2
             wide = width + ((half + 1) // 2 * 3 * channels if last else 0)
-            own, pair, other = pl.pallas_call(
+            own, pair, other, *now = pl.pallas_call(
                 functools.partial(first_kernel, layer, last, degrees, channels, per_atom, len(tables)),
                 out_shape=[
                     held((2 * atoms, wide), BF16), held((2 * ghosts, wide), BF16),
-                    held((2 * ghosts, wide), BF16),
+                    held((2 * ghosts, wide), BF16), *near_weights,
                 ],
-                in_specs=[VMEM] * (7 + len(tables) + count),
-                out_specs=[VMEM] * 3,
-                scratch_shapes=scratch,
+                in_specs=[VMEM] * (7 + len(tables) + count) + [far] * count,
+                out_specs=[VMEM] * (3 + count),
+                scratch_shapes=[*scratch, pltpu.SemaphoreType.DMA((count,))],
                 compiler_params=params,
                 name="layer",
-            )(*near(lent, hot, radial, lent_y, hot_y, radial_y, pulls, *tables, *now))
+            )(*near(lent, hot, radial, lent_y, hot_y, radial_y, pulls, *tables, *now), *away(*weights))
             got_other = toward(other, -1, slabs)
             got_pair = toward(pair, 1, slabs)
             blocks = spread({0: (own, got_pair, got_other)}, bits[1:], slab_devices)

time: 35.7 us -> 36 us (level)
  waiting for transfers between devices: 9.17 us -> 10.1 us
  starting transfers between devices: 14.5 us -> 14 us
    pallas_call x1, Pallas kernels: 2.39 us -> 3.95 us  [body(): pl.pallas_call(functools.partial(first_kernel, layer, last, degrees, chan...]
    ppermute x13 -> x12, starting transfers between devices: 6.69 us -> 5.23 us  [across(): lax.ppermute(block, 'yz', [(q, q ^ bit) for q in range(slab_devices)])]
    pallas_call x4, Pallas kernels: 5.99 us -> 4.59 us  [the longest x2 2.5 us: body(): pl.pallas_call(functools.partial(scale_kernel, atoms, ghosts, slab_device...]
    ppermute x4, starting transfers between devices: 7.86 us -> 8.78 us  [toward(): return lax.ppermute(block, 'slab', route)]
    ppermute x4, waiting for transfers between devices: 4.65 us -> 5.35 us  [toward(): return lax.ppermute(block, 'slab', route)]
    ppermute x13 -> x12, waiting for transfers between devices: 4.52 us -> 4.77 us  [across(): lax.ppermute(block, 'yz', [(q, q ^ bit) for q in range(slab_devices)])]
  transfers between devices with their start and end apart: 17 -> 16, of which waited for: 4 -> 6; matrix products, arithmetic and copies ran while one was open for 0% -> 0% of each run, Pallas kernels for 13% -> 9%
where the time goes in v5:
time: 36 us; the launch traced here: 35.8 us
  starting transfers between devices  14 us (39%)
  Pallas kernels  10.9 us (30%)
  waiting for transfers between devices  10.1 us (28%)
  between operations  0.75 us (2%)
    ppermute x4, starting transfers between devices, toward(): return lax.ppermute(block, 'slab', route)  8.78 us
    ppermute x4, waiting for transfers between devices, toward(): return lax.ppermute(block, 'slab', route)  5.35 us
    ppermute x12, starting transfers between devices, across(): lax.ppermute(block, 'yz', [(q, q ^ bit) for q in range(slab_devices)])  5.23 us
    ppermute x12, waiting for transfers between devices, across(): lax.ppermute(block, 'yz', [(q, q ^ bit) for q in range(slab_devices)])  4.77 us
    pallas_call x1, Pallas kernels, body(): pl.pallas_call(functools.partial(first_kernel, layer, last, degrees, chan...  3.95 us
    pallas_call x2, Pallas kernels, body(): pl.pallas_call(functools.partial(scale_kernel, atoms, ghosts, slab_device...  2.5 us
    pallas_call x1, Pallas kernels, body(): pl.pallas_call(functools.partial(last_kernel, layer, degrees, channels, a...  2.36 us
    pallas_call x1, Pallas kernels, body(): pl.pallas_call(pack_kernel, out_shape=[held((atoms, width + edges), BF16)...  1.25 us
  transfers between devices with their start and end apart: 16, of which 6 were waited for; matrix products, arithmetic and copies ran while one was open for 0% of the time, Pallas kernels for 9%

profile of v5, /device:TPU:0, one launch (start us, length us, event | category | flops | bytes accessed | tf_op | source)
XLA Modules:
  0.0 35.8 jit_solution(3531963492881438628)
XLA Ops:
  0.6 1.3 %pack.1 = (bf16[16,2944]{1,0:T(8,128)(2,1)S(1)}, bf16[8,2432]{1,0:T(8,128)(2,1)S(1)}, bf16[8,2432]{1,0:T(8,128)(2,1)S(1)}, bf16[6,16,128]{2,1,0:T(8,128)(2,1)S(1...) custom-call(bf16[25,16,128]{2,1,0:T(8,128)(2,1)} %bitcast.10, s32[1,8]{1,0:T(1,128)} %bitcast.16, s32[1,8]{1,0:T(1,128)} %bitcast.17, ...), custom_call_target="tpu_custom_call" | custom-call | tf_op jit(solution)/shard_map/pack/pallas_call | solution.py:388
  1.9 3.1 %collective-permute-start.1 = (bf16[16,2944]{1,0:T(8,128)(2,1)S(1)}, bf16[16,2944]{1,0:T(8,128)(2,1)S(1)}, u32[]{:S(2)}, u32[]{:S(2)}) collective-permute-start(bf16[16,2944]{1,0:T(8,128)(2,1)S(1)} %get-tuple-element.36.facts_ref.refs_0_), channel_id=1, source_target_pairs={{0,2},{1,3},{2,0},{3,1},{4,6},{5,7},{6,4},{7,5},{8,10},{9,11},{10,... | collective-permute-start | bytes 282632 | tf_op jit(solution)/shard_map/ppermute | solution.py:342
  5.0 1.5 %collective-permute-start = (bf16[8,2432]{1,0:T(8,128)(2,1)S(1)}, bf16[8,2432]{1,0:T(8,128)(2,1)S(1)}, u32[]{:S(2)}, u32[]{:S(2)}) collective-permute-start(bf16[8,2432]{1,0:T(8,128)(2,1)S(1)} %get-tuple-element.41), channel_id=1, source_target_pairs={{0,4},{4,0},{8,12},{12,8},{16,20},{20,16},{24,28},{28,24},{1,5},{5... | collective-permute-start | bytes 116744 | tf_op jit(solution)/shard_map/ppermute | solution.py:350
  6.4 3.6 %collective-permute-start.3 = (bf16[8,2432]{1,0:T(8,128)(2,1)S(1)}, bf16[8,2432]{1,0:T(8,128)(2,1)S(1)}, u32[]{:S(2)}, u32[]{:S(2)}) collective-permute-start(bf16[8,2432]{1,0:T(8,128)(2,1)S(1)} %get-tuple-element.52), channel_id=1, source_target_pairs={{0,28},{4,8},{8,4},{12,16},{16,12},{20,24},{24,20},{28,0},{1,29},{... | collective-permute-start | bytes 116744 | tf_op jit(solution)/shard_map/ppermute | solution.py:350
  10.0 0.0 collective-permute-start.5
  10.0 0.0 collective-permute-done.1.facts_ref.partner_ref.refs_1_
  10.0 0.5 %collective-permute-start.6 = (bf16[16,2944]{1,0:T(8,128)(2,1)S(1)}, bf16[16,2944]{1,0:T(8,128)(2,1)S(1)}, u32[]{:S(2)}, u32[]{:S(2)}) collective-permute-start(bf16[16,2944]{1,0:T(8,128)(2,1)S(1)} %collective-permute-done.1.facts_ref.partner_ref.refs_1_), channel_id=1, source_target_pairs={{0,1},{1,0},{2,3},{3,2},{4,5},{5,4},{6,7},{7,6},{8,9},{9,8},{10,11... | collective-permute-start | bytes 282632 | tf_op jit(solution)/shard_map/ppermute | solution.py:342
  10.5 0.7 %scales.1 = (bf16[512,256]{1,0:T(8,128)(2,1)S(1)}, f32[2,512,128]{2,1,0:T(8,128)S(1)}, f32[128,512]{1,0:T(8,128)S(1)}, f32[16,16]{1,0:T(8,128)S(1)}) custom-call(bf16[16,2944]{1,0:T(8,128)(2,1)S(1)} %get-tuple-element.36.facts_ref.refs_0_, f32[2,8,128]{2,1,0:T(8,128)S(1)} %get-tuple-element.37.rw_ref), custom_call_target="tpu_custom_call" | custom-call | tf_op jit(solution)/shard_map/scales/pallas_call | solution.py:414
  11.3 0.0 collective-permute-done.refs_2_
  11.3 0.6 %collective-permute-start.2 = (bf16[8,2432]{1,0:T(8,128)(2,1)S(1)}, bf16[8,2432]{1,0:T(8,128)(2,1)S(1)}, u32[]{:S(2)}, u32[]{:S(2)}) collective-permute-start(bf16[8,2432]{1,0:T(8,128)(2,1)S(1)} %collective-permute-done.refs_2_), channel_id=1, source_target_pairs={{0,2},{1,3},{2,0},{3,1},{4,6},{5,7},{6,4},{7,5},{8,10},{9,11},{10,... | collective-permute-start | bytes 116744 | tf_op jit(solution)/shard_map/ppermute | solution.py:342
  11.8 1.3 %collective-permute-done.3.refs_4_ = bf16[8,2432]{1,0:T(8,128)(2,1)S(1)} collective-permute-done((bf16[8,2432]{1,0:T(8,128)(2,1)S(1)}, bf16[8,2432]{1,0:T(8,128)(2,1)S(1)}, u32[]{:S(2)}, u32[]{:S(2)}) %collective-permute-start.3) | collective-permute-done | bytes 38944 | tf_op jit(solution)/shard_map/ppermute | solution.py:350
  13.1 0.5 %collective-permute-start.4 = (bf16[8,2432]{1,0:T(8,128)(2,1)S(1)}, bf16[8,2432]{1,0:T(8,128)(2,1)S(1)}, u32[]{:S(2)}, u32[]{:S(2)}) collective-permute-start(bf16[8,2432]{1,0:T(8,128)(2,1)S(1)} %collective-permute-done.3.refs_4_), channel_id=1, source_target_pairs={{0,2},{1,3},{2,0},{3,1},{4,6},{5,7},{6,4},{7,5},{8,10},{9,11},{10,... | collective-permute-start | bytes 116744 | tf_op jit(solution)/shard_map/ppermute | solution.py:342
  13.6 0.0 collective-permute-start.7
  13.6 1.7 %collective-permute-done.2.refs_3_ = bf16[8,2432]{1,0:T(8,128)(2,1)S(1)} collective-permute-done((bf16[8,2432]{1,0:T(8,128)(2,1)S(1)}, bf16[8,2432]{1,0:T(8,128)(2,1)S(1)}, u32[]{:S(2)}, u32[]{:S(2)}) %collective-permute-start.2) | collective-permute-done | bytes 38944 | tf_op jit(solution)/shard_map/ppermute | solution.py:342
  15.3 1.8 %collective-permute-done.4.refs_5_ = bf16[8,2432]{1,0:T(8,128)(2,1)S(1)} collective-permute-done((bf16[8,2432]{1,0:T(8,128)(2,1)S(1)}, bf16[8,2432]{1,0:T(8,128)(2,1)S(1)}, u32[]{:S(2)}, u32[]{:S(2)}) %collective-permute-start.4) | collective-permute-done | bytes 38944 | tf_op jit(solution)/shard_map/ppermute | solution.py:342
  17.1 0.0 collective-permute-start.8
  17.1 0.0 collective-permute-done.7.refs_8_
  17.1 0.5 %collective-permute-start.10 = (bf16[8,2432]{1,0:T(8,128)(2,1)S(1)}, bf16[8,2432]{1,0:T(8,128)(2,1)S(1)}, u32[]{:S(2)}, u32[]{:S(2)}) collective-permute-start(bf16[8,2432]{1,0:T(8,128)(2,1)S(1)} %collective-permute-done.4.refs_5_), channel_id=1, source_target_pairs={{0,1},{1,0},{2,3},{3,2},{4,5},{5,4},{6,7},{7,6},{8,9},{9,8},{10,11... | collective-permute-start | bytes 116744 | tf_op jit(solution)/shard_map/ppermute | solution.py:342
  17.6 1.8 %scales_y.1 = (bf16[512,256]{1,0:T(8,128)(2,1)S(1)}, f32[2,512,128]{2,1,0:T(8,128)S(1)}, f32[128,512]{1,0:T(8,128)S(1)}, f32[16,16]{1,0:T(8,128)S(1)}, bf16[640,...) custom-call(bf16[16,2944]{1,0:T(8,128)(2,1)S(1)} %collective-permute, ...), custom_call_target="tpu_custom_call" | custom-call | tf_op jit(solution)/shard_map/scales_y/pallas_call | solution.py:425
  19.4 0.8 %pulls.1 = (f32[3,512,128]{2,1,0:T(8,128)S(1)}, bf16[128,384]{1,0:T(8,128)(2,1)S(1)}) custom-call(bf16[16,2944]{1,0:T(8,128)(2,1)S(1)} %get-tuple-element.36.facts_ref.refs_0_, f32[2,512,128]{2,1,0:T(8,128)S(1)} %get-tuple-element.40.radial_ref, f32[128,512]{1,0:T(8,128)S(1)} %get-tuple-element.43.flags_ref, ...), custom_call_target="tpu_custom_call" | custom-call | tf_op jit(solution)/shard_map/pulls/pallas_call | solution.py:434
  20.2 0.0 collective-permute-done.9.refs_10_
  20.3 0.0 collective-permute-done.8.refs_9_
  20.3 0.0 collective-permute-done.10.refs_11_
  20.3 3.9 %layer.1 = (bf16[32,2816]{1,0:T(8,128)(2,1)S(1)}, bf16[16,2816]{1,0:T(8,128)(2,1)S(1)}, bf16[16,2816]{1,0:T(8,128)(2,1)S(1)}, bf16[640,640]{1,0:T(8,128)(2,1)S(1...) custom-call(f32[16,16]{1,0:T(8,128)S(1)} %get-tuple-element.38.lent_, ...), custom_call_target="tpu_custom_call" | custom-call | tf_op jit(solution)/shard_map/layer/pallas_call | solution.py:457
  24.3 0.1 collective-permute-start.11
  24.3 0.1 collective-permute-start.13
  24.4 3.6 %collective-permute-start.12 = (bf16[16,2816]{1,0:T(8,128)(2,1)S(1)}, bf16[16,2816]{1,0:T(8,128)(2,1)S(1)}, u32[]{:S(2)}, u32[]{:S(2)}) collective-permute-start(bf16[16,2816]{1,0:T(8,128)(2,1)S(1)} %get-tuple-element.60), channel_id=1, source_target_pairs={{0,28},{4,8},{8,4},{12,16},{16,12},{20,24},{24,20},{28,0},{1,29},{... | collective-permute-start | bytes 270344 | tf_op jit(solution)/shard_map/ppermute | solution.py:350
  28.1 0.8 %collective-permute-done.11.refs_1_ = bf16[16,2816]{1,0:T(8,128)(2,1)S(1)} collective-permute-done((bf16[16,2816]{1,0:T(8,128)(2,1)S(1)}, bf16[16,2816]{1,0:T(8,128)(2,1)S(1)}, u32[]{:S(2)}, u32[]{:S(2)}) %collective-permute-start.11) | collective-permute-done | bytes 90144 | tf_op jit(solution)/shard_map/ppermute | solution.py:350
  28.8 0.0 collective-permute-start.14
  28.8 3.3 %collective-permute-done.12.refs_2_ = bf16[16,2816]{1,0:T(8,128)(2,1)S(1)} collective-permute-done((bf16[16,2816]{1,0:T(8,128)(2,1)S(1)}, bf16[16,2816]{1,0:T(8,128)(2,1)S(1)}, u32[]{:S(2)}, u32[]{:S(2)}) %collective-permute-start.12) | collective-permute-done | bytes 90144 | tf_op jit(solution)/shard_map/ppermute | solution.py:350
  32.1 1.3 %collective-permute-done.15.refs_5_ = bf16[16,2816]{1,0:T(8,128)(2,1)S(1)} collective-permute-done((bf16[16,2816]{1,0:T(8,128)(2,1)S(1)}, bf16[16,2816]{1,0:T(8,128)(2,1)S(1)}, u32[]{:S(2)}, u32[]{:S(2)}) %collective-permute-start.15) | collective-permute-done | bytes 90144 | tf_op jit(solution)/shard_map/ppermute | solution.py:342
  33.4 2.4 %last_layer.1 = (bf16[25,16,128]{2,1,0:T(8,128)(2,1)}, f32[3,16]{1,0:T(4,128)}) custom-call(bf16[6,16,128]{2,1,0:T(8,128)(2,1)S(1)} %get-tuple-element.35.rest_ref, f32[16,16]{1,0:T(8,128)S(1)} %get-tuple-element.38.lent_ref, bf16[512,256]{1,0:T(8,128)(2,1)S(1)} %get-tuple-element.39.hot_ref, f32[2,512,128]{2,1,0:T(8,128)S(1)} %get-tuple-element.40.radial_ref, ...), custom_call_target="tpu_custom_call" | custom-call | tf_op jit(solution)/shard_map/last_layer/pallas_call | solution.py:474
  (6 shorter events, 0.0 us)
Async XLA Ops:
  1.9 8.1 %collective-permute-start.1 = (bf16[16,2944]{1,0:T(8,128)(2,1)S(1)}, bf16[16,2944]{1,0:T(8,128)(2,1)S(1)}, u32[]{:S(2)}, u32[]{:S(2)}) collective-permute-start(bf16[16,2944]{1,0:T(8,128)(2,1)S(1)} %get-tuple-element.36.facts_ref.refs_0_), channel_id=1, source_target_pairs={{0,2},{1,3},{2,0},{3,1},{4,6},{5,7},{6,4},{7,5},{8,10},{9,11},{10,... | collective-permute-start | bytes 282632 | tf_op jit(solution)/shard_map/ppermute | solution.py:342
  5.0 6.3 %collective-permute-start = (bf16[8,2432]{1,0:T(8,128)(2,1)S(1)}, bf16[8,2432]{1,0:T(8,128)(2,1)S(1)}, u32[]{:S(2)}, u32[]{:S(2)}) collective-permute-start(bf16[8,2432]{1,0:T(8,128)(2,1)S(1)} %get-tuple-element.41), channel_id=1, source_target_pairs={{0,4},{4,0},{8,12},{12,8},{16,20},{20,16},{24,28},{28,24},{1,5},{5... | collective-permute-start | bytes 116744 | tf_op jit(solution)/shard_map/ppermute | solution.py:350
  6.4 6.7 %collective-permute-start.3 = (bf16[8,2432]{1,0:T(8,128)(2,1)S(1)}, bf16[8,2432]{1,0:T(8,128)(2,1)S(1)}, u32[]{:S(2)}, u32[]{:S(2)}) collective-permute-start(bf16[8,2432]{1,0:T(8,128)(2,1)S(1)} %get-tuple-element.52), channel_id=1, source_target_pairs={{0,28},{4,8},{8,4},{12,16},{16,12},{20,24},{24,20},{28,0},{1,29},{... | collective-permute-start | bytes 116744 | tf_op jit(solution)/shard_map/ppermute | solution.py:350
  10.0 10.2 %collective-permute-start.5 = (bf16[16,2944]{1,0:T(8,128)(2,1)S(1)}, bf16[16,2944]{1,0:T(8,128)(2,1)S(1)}, u32[]{:S(2)}, u32[]{:S(2)}) collective-permute-start(bf16[16,2944]{1,0:T(8,128)(2,1)S(1)} %get-tuple-element.36.facts_ref.refs_0_), channel_id=1, source_target_pairs={{0,1},{1,0},{2,3},{3,2},{4,5},{5,4},{6,7},{7,6},{8,9},{9,8},{10,11... | collective-permute-start | bytes 282632 | tf_op jit(solution)/shard_map/ppermute | solution.py:342
  10.0 10.3 %collective-permute-start.6 = (bf16[16,2944]{1,0:T(8,128)(2,1)S(1)}, bf16[16,2944]{1,0:T(8,128)(2,1)S(1)}, u32[]{:S(2)}, u32[]{:S(2)}) collective-permute-start(bf16[16,2944]{1,0:T(8,128)(2,1)S(1)} %collective-permute-done.1.facts_ref.partner_ref.refs_1_), channel_id=1, source_target_pairs={{0,1},{1,0},{2,3},{3,2},{4,5},{5,4},{6,7},{7,6},{8,9},{9,8},{10,11... | collective-permute-start | bytes 282632 | tf_op jit(solution)/shard_map/ppermute | solution.py:342
  11.3 4.0 %collective-permute-start.2 = (bf16[8,2432]{1,0:T(8,128)(2,1)S(1)}, bf16[8,2432]{1,0:T(8,128)(2,1)S(1)}, u32[]{:S(2)}, u32[]{:S(2)}) collective-permute-start(bf16[8,2432]{1,0:T(8,128)(2,1)S(1)} %collective-permute-done.refs_2_), channel_id=1, source_target_pairs={{0,2},{1,3},{2,0},{3,1},{4,6},{5,7},{6,4},{7,5},{8,10},{9,11},{10,... | collective-permute-start | bytes 116744 | tf_op jit(solution)/shard_map/ppermute | solution.py:342
  13.1 4.0 %collective-permute-start.4 = (bf16[8,2432]{1,0:T(8,128)(2,1)S(1)}, bf16[8,2432]{1,0:T(8,128)(2,1)S(1)}, u32[]{:S(2)}, u32[]{:S(2)}) collective-permute-start(bf16[8,2432]{1,0:T(8,128)(2,1)S(1)} %collective-permute-done.3.refs_4_), channel_id=1, source_target_pairs={{0,2},{1,3},{2,0},{3,1},{4,6},{5,7},{6,4},{7,5},{8,10},{9,11},{10,... | collective-permute-start | bytes 116744 | tf_op jit(solution)/shard_map/ppermute | solution.py:342
  13.6 3.5 %collective-permute-start.7 = (bf16[8,2432]{1,0:T(8,128)(2,1)S(1)}, bf16[8,2432]{1,0:T(8,128)(2,1)S(1)}, u32[]{:S(2)}, u32[]{:S(2)}) collective-permute-start(bf16[8,2432]{1,0:T(8,128)(2,1)S(1)} %collective-permute-done.refs_2_), channel_id=1, source_target_pairs={{0,1},{1,0},{2,3},{3,2},{4,5},{5,4},{6,7},{7,6},{8,9},{9,8},{10,11... | collective-permute-start | bytes 116744 | tf_op jit(solution)/shard_map/ppermute | solution.py:342
  15.3 4.9 %collective-permute-start.9 = (bf16[8,2432]{1,0:T(8,128)(2,1)S(1)}, bf16[8,2432]{1,0:T(8,128)(2,1)S(1)}, u32[]{:S(2)}, u32[]{:S(2)}) collective-permute-start(bf16[8,2432]{1,0:T(8,128)(2,1)S(1)} %collective-permute-done.3.refs_4_), channel_id=1, source_target_pairs={{0,1},{1,0},{2,3},{3,2},{4,5},{5,4},{6,7},{7,6},{8,9},{9,8},{10,11... | collective-permute-start | bytes 116744 | tf_op jit(solution)/shard_map/ppermute | solution.py:342
  17.1 3.2 %collective-permute-start.8 = (bf16[8,2432]{1,0:T(8,128)(2,1)S(1)}, bf16[8,2432]{1,0:T(8,128)(2,1)S(1)}, u32[]{:S(2)}, u32[]{:S(2)}) collective-permute-start(bf16[8,2432]{1,0:T(8,128)(2,1)S(1)} %collective-permute-done.2.refs_3_), channel_id=1, source_target_pairs={{0,1},{1,0},{2,3},{3,2},{4,5},{5,4},{6,7},{7,6},{8,9},{9,8},{10,11... | collective-permute-start | bytes 116744 | tf_op jit(solution)/shard_map/ppermute | solution.py:342
  17.1 3.2 %collective-permute-start.10 = (bf16[8,2432]{1,0:T(8,128)(2,1)S(1)}, bf16[8,2432]{1,0:T(8,128)(2,1)S(1)}, u32[]{:S(2)}, u32[]{:S(2)}) collective-permute-start(bf16[8,2432]{1,0:T(8,128)(2,1)S(1)} %collective-permute-done.4.refs_5_), channel_id=1, source_target_pairs={{0,1},{1,0},{2,3},{3,2},{4,5},{5,4},{6,7},{7,6},{8,9},{9,8},{10,11... | collective-permute-start | bytes 116744 | tf_op jit(solution)/shard_map/ppermute | solution.py:342
  24.3 4.6 %collective-permute-start.11 = (bf16[16,2816]{1,0:T(8,128)(2,1)S(1)}, bf16[16,2816]{1,0:T(8,128)(2,1)S(1)}, u32[]{:S(2)}, u32[]{:S(2)}) collective-permute-start(bf16[16,2816]{1,0:T(8,128)(2,1)S(1)} %get-tuple-element.59), channel_id=1, source_target_pairs={{0,4},{4,0},{8,12},{12,8},{16,20},{20,16},{24,28},{28,24},{1,5},{5... | collective-permute-start | bytes 270344 | tf_op jit(solution)/shard_map/ppermute | solution.py:350
  24.3 7.8 %collective-permute-start.13 = (bf16[32,2816]{1,0:T(8,128)(2,1)S(1)}, bf16[32,2816]{1,0:T(8,128)(2,1)S(1)}, u32[]{:S(2)}, u32[]{:S(2)}) collective-permute-start(bf16[32,2816]{1,0:T(8,128)(2,1)S(1)} %get-tuple-element.58.refs_0_), channel_id=1, source_target_pairs={{0,1},{1,0},{2,3},{3,2},{4,5},{5,4},{6,7},{7,6},{8,9},{9,8},{10,11... | collective-permute-start | bytes 540680 | tf_op jit(solution)/shard_map/ppermute | solution.py:342
  24.4 7.7 %collective-permute-start.12 = (bf16[16,2816]{1,0:T(8,128)(2,1)S(1)}, bf16[16,2816]{1,0:T(8,128)(2,1)S(1)}, u32[]{:S(2)}, u32[]{:S(2)}) collective-permute-start(bf16[16,2816]{1,0:T(8,128)(2,1)S(1)} %get-tuple-element.60), channel_id=1, source_target_pairs={{0,28},{4,8},{8,4},{12,16},{16,12},{20,24},{24,20},{28,0},{1,29},{... | collective-permute-start | bytes 270344 | tf_op jit(solution)/shard_map/ppermute | solution.py:350
  28.8 3.3 %collective-permute-start.14 = (bf16[16,2816]{1,0:T(8,128)(2,1)S(1)}, bf16[16,2816]{1,0:T(8,128)(2,1)S(1)}, u32[]{:S(2)}, u32[]{:S(2)}) collective-permute-start(bf16[16,2816]{1,0:T(8,128)(2,1)S(1)} %collective-permute-done.11.refs_1_), channel_id=1, source_target_pairs={{0,1},{1,0},{2,3},{3,2},{4,5},{5,4},{6,7},{7,6},{8,9},{9,8},{10,11... | collective-permute-start | bytes 270344 | tf_op jit(solution)/shard_map/ppermute | solution.py:342
  32.1 1.3 %collective-permute-start.15 = (bf16[16,2816]{1,0:T(8,128)(2,1)S(1)}, bf16[16,2816]{1,0:T(8,128)(2,1)S(1)}, u32[]{:S(2)}, u32[]{:S(2)}) collective-permute-start(bf16[16,2816]{1,0:T(8,128)(2,1)S(1)} %collective-permute-done.12.refs_2_), channel_id=1, source_target_pairs={{0,1},{1,0},{2,3},{3,2},{4,5},{5,4},{6,7},{7,6},{8,9},{9,8},{10,11... | collective-permute-start | bytes 270344 | tf_op jit(solution)/shard_map/ppermute | solution.py:342

commit v6 on v5

--- a/solution.py
+++ b/solution.py
@@ -166,9 +166,12 @@
     lent_ref[...] = lent_hot(picks[:, : 2 * ghosts], atoms)
 
 
-def scale_kernel(atoms, ghosts, slab_devices, count, facts_ref, rw_ref, *refs):
+def scale_kernel(atoms, ghosts, slab_devices, count, fetched, facts_ref, rw_ref, *refs):
     far, refs = refs[:count], refs[count:]
-    copies = start_fetch((*far, *refs[4:]), 0) if count else ()
+    copies = []
+    for i, layer in enumerate(fetched):
+        near_refs = refs[4 + count * i : 4 + count * (i + 1)]
+        copies += start_fetch((*far, *near_refs, refs[-1].at[i]), layer)
     edge_scales(atoms, ghosts, slab_devices, facts_ref, rw_ref, *refs[:4])
     for copy in copies:
         copy.wait()
@@ -261,10 +264,9 @@
     layer, last, degrees, channels, per_atom, count,
     lent_ref, hot_ref, radial_ref, lent_y_ref, hot_y_ref, radial_y_ref, pulls_ref, *refs,
 ):
-    tables, weights, far = refs[:count], refs[count : count + 5], refs[count + 5 : count + 10]
-    own_ref, pair_ref, other_ref = refs[count + 10 : count + 13]
-    scratch = refs[count + 18 : count + 20]
-    copies = start_fetch((*far, *refs[count + 13 : count + 18], refs[-1]), layer + 1)
+    tables, weights = refs[:count], refs[count : count + 5]
+    own_ref, pair_ref, other_ref = refs[count + 5 : count + 8]
+    scratch = refs[count + 8 :]
     joined = scratch[0]
     both = own_ref.shape[0]
     atoms, ghosts = both // 2, lent_ref.shape[1] // 2
@@ -290,8 +292,6 @@
                 to = slot % 2 * size
                 ref[to : to + size, cols] = pulls_ref[at : at + size]
                 at += 2 * size
-    for copy in copies:
-        copy.wait()
 
 
 def last_kernel(
@@ -353,7 +353,10 @@
 def spread(held, bits, slab_devices):
     for bit in bits:
         for slot in sorted(held):
-            held[slot | bit] = tuple(across(block, bit, slab_devices) for block in held[slot])
+            got = []
+            for block in held[slot]:
+                got.append(across(block, bit, slab_devices))
+            held[slot | bit] = tuple(got)
     return held
 
 
@@ -411,26 +414,22 @@
         held((edges, 2 * rows), BF16), held((layers, edges, channels), F32),
         held((rows, edges), F32), held((atoms, 2 * ghosts), F32),
     ]
-    hot, radial, flags, lent = pl.pallas_call(
-        functools.partial(scale_kernel, atoms, ghosts, slab_devices, 0),
-        out_shape=side_shapes,
-        in_specs=[VMEM] * 2,
-        out_specs=[VMEM] * 4,
-        compiler_params=params,
-        name="scales",
-    )(*near(own, radial_weight))
+
+    def scales(facts, fetched):
+        return pl.pallas_call(
+            functools.partial(scale_kernel, atoms, ghosts, slab_devices, count, fetched),
+            out_shape=[*side_shapes, *(near_weights * len(fetched))],
+            in_specs=[VMEM] * 2 + [far] * count,
+            out_specs=[VMEM] * (4 + count * len(fetched)),
+            scratch_shapes=[pltpu.SemaphoreType.DMA((len(fetched), count))],
+            compiler_params=params,
+        )(*near(facts, radial_weight), *away(*weights))
+
+    hot, radial, flags, lent, *first_weights = scales(own, (0,))
     got_pair, flags = lax.optimization_barrier((got_pair, flags))
     pair_y = across(got_pair, half, slab_devices)
     other_y = across(got_other, half, slab_devices)
-    hot_y, radial_y, flags_y, lent_y, *now = pl.pallas_call(
-        functools.partial(scale_kernel, atoms, ghosts, slab_devices, count),
-        out_shape=[*side_shapes, *near_weights],
-        in_specs=[VMEM] * 2 + [far] * count,
-        out_specs=[VMEM] * (4 + count),
-        scratch_shapes=[pltpu.SemaphoreType.DMA((count,))],
-        compiler_params=params,
-        name="scales_y",
-    )(*near(got_own, radial_weight), *away(*weights))
+    hot_y, radial_y, flags_y, lent_y, *later_weights = scales(got_own, tuple(range(1, layers)))
     dirs, pulls = pl.pallas_call(
         pull_kernel,
         out_shape=[held((3, edges, channels), F32), held((rows, 3 * channels), BF16)],
@@ -450,22 +449,24 @@
     ]
     scratch = [pltpu.VMEM((rows, width), F32), pltpu.VMEM((2 * rows, width), BF16)]
     per_atom = edges // atoms
+    weights = (*first_weights, *later_weights)
     for layer in range(layers):
+        now = weights[layer * count : (layer + 1) * count]
         if layer < layers - 1:
             last = layer == layers - 2
             wide = width + ((half + 1) // 2 * 3 * channels if last else 0)
-            own, pair, other, *now = pl.pallas_call(
+            own, pair, other = pl.pallas_call(
                 functools.partial(first_kernel, layer, last, degrees, channels, per_atom, len(tables)),
                 out_shape=[
                     held((2 * atoms, wide), BF16), held((2 * ghosts, wide), BF16),
-                    held((2 * ghosts, wide), BF16), *near_weights,
+                    held((2 * ghosts, wide), BF16),
                 ],
-                in_specs=[VMEM] * (7 + len(tables) + count) + [far] * count,
-                out_specs=[VMEM] * (3 + count),
-                scratch_shapes=[*scratch, pltpu.SemaphoreType.DMA((count,))],
+                in_specs=[VMEM] * (7 + len(tables) + count),
+                out_specs=[VMEM] * 3,
+                scratch_shapes=scratch,
                 compiler_params=params,
                 name="layer",
-            )(*near(lent, hot, radial, lent_y, hot_y, radial_y, pulls, *tables, *now), *away(*weights))
+            )(*near(lent, hot, radial, lent_y, hot_y, radial_y, pulls, *tables, *now))
             got_other = toward(other, -1, slabs)
             got_pair = toward(pair, 1, slabs)
             blocks = spread({0: (own, got_pair, got_other)}, bits[1:], slab_devices)

time: 36 us -> 34.3 us (0.953)
  waiting for transfers between devices: 10.1 us -> 8.28 us
  starting transfers between devices: 14 us -> 14.8 us
  Pallas kernels: 10.9 us -> 10.3 us
    pallas_call x1, Pallas kernels: 3.95 us -> 2.42 us  [body(): pl.pallas_call(functools.partial(first_kernel, layer, last, degrees, chan...]
    ppermute x4, waiting for transfers between devices: 5.35 us -> 4.3 us  [toward(): return lax.ppermute(block, 'slab', route)]
    pallas_call x2, Pallas kernels: 2.5 us -> 3.44 us  [scales(): pl.pallas_call(functools.partial(scale_kernel, atoms, ghosts, slab_device...]
    ppermute x12, starting transfers between devices: 5.23 us -> 6.02 us  [across(): lax.ppermute(block, 'yz', [(q, q ^ bit) for q in range(slab_devices)])]
    ppermute x12, waiting for transfers between devices: 4.77 us -> 3.97 us  [across(): lax.ppermute(block, 'yz', [(q, q ^ bit) for q in range(slab_devices)])]
  transfers between devices with their start and end apart: 16 -> 16, of which waited for: 6 -> 6; matrix products, arithmetic and copies ran while one was open for 0% -> 0% of each run, Pallas kernels for 9% -> 13%
where the time goes in v6:
time: 34.3 us; the launch traced here: 34.1 us
  starting transfers between devices  14.8 us (43%)
  Pallas kernels  10.3 us (30%)
  waiting for transfers between devices  8.28 us (24%)
  between operations  0.74 us (2%)
    ppermute x4, starting transfers between devices, toward(): return lax.ppermute(block, 'slab', route)  8.77 us
    ppermute x12, starting transfers between devices, across(): lax.ppermute(block, 'yz', [(q, q ^ bit) for q in range(slab_devices)])  6.02 us
    ppermute x4, waiting for transfers between devices, toward(): return lax.ppermute(block, 'slab', route)  4.3 us
    ppermute x12, waiting for transfers between devices, across(): lax.ppermute(block, 'yz', [(q, q ^ bit) for q in range(slab_devices)])  3.97 us
    pallas_call x2, Pallas kernels, scales(): pl.pallas_call(functools.partial(scale_kernel, atoms, ghosts, slab_device...  3.44 us
    pallas_call x1, Pallas kernels, body(): pl.pallas_call(functools.partial(first_kernel, layer, last, degrees, chan...  2.42 us
    pallas_call x1, Pallas kernels, body(): pl.pallas_call(functools.partial(last_kernel, layer, degrees, channels, a...  2.36 us
    pallas_call x1, Pallas kernels, body(): pl.pallas_call(pack_kernel, out_shape=[held((atoms, width + edges), BF16)...  1.25 us
  transfers between devices with their start and end apart: 16, of which 6 were waited for; matrix products, arithmetic and copies ran while one was open for 0% of the time, Pallas kernels for 13%

profile of v6, /device:TPU:0, one launch (start us, length us, event | category | flops | bytes accessed | tf_op | source)
XLA Modules:
  0.0 34.1 jit_solution(1727253558712334063)
XLA Ops:
  0.6 1.3 %pack.1 = (bf16[16,2944]{1,0:T(8,128)(2,1)S(1)}, bf16[8,2432]{1,0:T(8,128)(2,1)S(1)}, bf16[8,2432]{1,0:T(8,128)(2,1)S(1)}, bf16[6,16,128]{2,1,0:T(8,128)(2,1)S(1...) custom-call(bf16[25,16,128]{2,1,0:T(8,128)(2,1)} %bitcast.10, s32[1,8]{1,0:T(1,128)} %bitcast.16, s32[1,8]{1,0:T(1,128)} %bitcast.17, ...), custom_call_target="tpu_custom_call" | custom-call | tf_op jit(solution)/shard_map/pack/pallas_call | solution.py:391
  1.9 3.1 %collective-permute-start.1 = (bf16[16,2944]{1,0:T(8,128)(2,1)S(1)}, bf16[16,2944]{1,0:T(8,128)(2,1)S(1)}, u32[]{:S(2)}, u32[]{:S(2)}) collective-permute-start(bf16[16,2944]{1,0:T(8,128)(2,1)S(1)} %get-tuple-element.36.facts_ref.refs_0_), channel_id=1, source_target_pairs={{0,2},{1,3},{2,0},{3,1},{4,6},{5,7},{6,4},{7,5},{8,10},{9,11},{10,... | collective-permute-start | bytes 282632 | tf_op jit(solution)/shard_map/ppermute | solution.py:342
  5.0 1.5 %collective-permute-start = (bf16[8,2432]{1,0:T(8,128)(2,1)S(1)}, bf16[8,2432]{1,0:T(8,128)(2,1)S(1)}, u32[]{:S(2)}, u32[]{:S(2)}) collective-permute-start(bf16[8,2432]{1,0:T(8,128)(2,1)S(1)} %get-tuple-element.41), channel_id=1, source_target_pairs={{0,4},{4,0},{8,12},{12,8},{16,20},{20,16},{24,28},{28,24},{1,5},{5... | collective-permute-start | bytes 116744 | tf_op jit(solution)/shard_map/ppermute | solution.py:350
  6.4 3.6 %collective-permute-start.3 = (bf16[8,2432]{1,0:T(8,128)(2,1)S(1)}, bf16[8,2432]{1,0:T(8,128)(2,1)S(1)}, u32[]{:S(2)}, u32[]{:S(2)}) collective-permute-start(bf16[8,2432]{1,0:T(8,128)(2,1)S(1)} %get-tuple-element.52), channel_id=1, source_target_pairs={{0,28},{4,8},{8,4},{12,16},{16,12},{20,24},{24,20},{28,0},{1,29},{... | collective-permute-start | bytes 116744 | tf_op jit(solution)/shard_map/ppermute | solution.py:350
  10.0 0.0 collective-permute-start.5
  10.0 0.5 %collective-permute-start.6 = (bf16[16,2944]{1,0:T(8,128)(2,1)S(1)}, bf16[16,2944]{1,0:T(8,128)(2,1)S(1)}, u32[]{:S(2)}, u32[]{:S(2)}) collective-permute-start(bf16[16,2944]{1,0:T(8,128)(2,1)S(1)} %collective-permute-done.1.facts_ref.partner_ref.refs_1_), channel_id=1, source_target_pairs={{0,1},{1,0},{2,3},{3,2},{4,5},{5,4},{6,7},{7,6},{8,9},{9,8},{10,11... | collective-permute-start | bytes 282632 | tf_op jit(solution)/shard_map/ppermute | solution.py:342
  10.5 1.8 %shard_map.158 = (bf16[512,256]{1,0:T(8,128)(2,1)S(1)}, f32[2,512,128]{2,1,0:T(8,128)S(1)}, f32[128,512]{1,0:T(8,128)S(1)}, f32[16,16]{1,0:T(8,128)S(1)}, bf16[6...) custom-call(bf16[16,2944]{1,0:T(8,128)(2,1)S(1)} %get-tuple-element., ...), custom_call_target="tpu_custom_call" | custom-call | tf_op jit(solution)/shard_map/pallas_call | solution.py:419
  12.3 0.0 collective-permute-done.refs_2_
  12.3 0.6 %collective-permute-start.2 = (bf16[8,2432]{1,0:T(8,128)(2,1)S(1)}, bf16[8,2432]{1,0:T(8,128)(2,1)S(1)}, u32[]{:S(2)}, u32[]{:S(2)}) collective-permute-start(bf16[8,2432]{1,0:T(8,128)(2,1)S(1)} %collective-permute-done.refs_2_), channel_id=1, source_target_pairs={{0,2},{1,3},{2,0},{3,1},{4,6},{5,7},{6,4},{7,5},{8,10},{9,11},{10,... | collective-permute-start | bytes 116744 | tf_op jit(solution)/shard_map/ppermute | solution.py:342
  12.9 0.2 collective-permute-done.3.refs_4_
  13.1 1.3 %collective-permute-start.4 = (bf16[8,2432]{1,0:T(8,128)(2,1)S(1)}, bf16[8,2432]{1,0:T(8,128)(2,1)S(1)}, u32[]{:S(2)}, u32[]{:S(2)}) collective-permute-start(bf16[8,2432]{1,0:T(8,128)(2,1)S(1)} %collective-permute-done.3.refs_4_), channel_id=1, source_target_pairs={{0,2},{1,3},{2,0},{3,1},{4,6},{5,7},{6,4},{7,5},{8,10},{9,11},{10,... | collective-permute-start | bytes 116744 | tf_op jit(solution)/shard_map/ppermute | solution.py:342
  14.4 0.0 collective-permute-start.7
  14.4 1.9 %collective-permute-done.2.refs_3_ = bf16[8,2432]{1,0:T(8,128)(2,1)S(1)} collective-permute-done((bf16[8,2432]{1,0:T(8,128)(2,1)S(1)}, bf16[8,2432]{1,0:T(8,128)(2,1)S(1)}, u32[]{:S(2)}, u32[]{:S(2)}) %collective-permute-start.2) | collective-permute-done | bytes 38944 | tf_op jit(solution)/shard_map/ppermute | solution.py:342
  16.4 0.7 %collective-permute-done.4.refs_5_ = bf16[8,2432]{1,0:T(8,128)(2,1)S(1)} collective-permute-done((bf16[8,2432]{1,0:T(8,128)(2,1)S(1)}, bf16[8,2432]{1,0:T(8,128)(2,1)S(1)}, u32[]{:S(2)}, u32[]{:S(2)}) %collective-permute-start.4) | collective-permute-done | bytes 38944 | tf_op jit(solution)/shard_map/ppermute | solution.py:342
  17.1 0.0 collective-permute-start.8
  17.1 0.0 collective-permute-done.7.refs_8_
  17.1 0.5 %collective-permute-start.10 = (bf16[8,2432]{1,0:T(8,128)(2,1)S(1)}, bf16[8,2432]{1,0:T(8,128)(2,1)S(1)}, u32[]{:S(2)}, u32[]{:S(2)}) collective-permute-start(bf16[8,2432]{1,0:T(8,128)(2,1)S(1)} %collective-permute-done.4.refs_5_), channel_id=1, source_target_pairs={{0,1},{1,0},{2,3},{3,2},{4,5},{5,4},{6,7},{7,6},{8,9},{9,8},{10,11... | collective-permute-start | bytes 116744 | tf_op jit(solution)/shard_map/ppermute | solution.py:342
  17.6 1.7 %shard_map.159 = (bf16[512,256]{1,0:T(8,128)(2,1)S(1)}, f32[2,512,128]{2,1,0:T(8,128)S(1)}, f32[128,512]{1,0:T(8,128)S(1)}, f32[16,16]{1,0:T(8,128)S(1)}, bf16[6...) custom-call(bf16[16,2944]{1,0:T(8,128)(2,1)S(1)} %collective-permute, ...), custom_call_target="tpu_custom_call" | custom-call | tf_op jit(solution)/shard_map/pallas_call | solution.py:419
  19.3 0.8 %pulls.1 = (f32[3,512,128]{2,1,0:T(8,128)S(1)}, bf16[128,384]{1,0:T(8,128)(2,1)S(1)}) custom-call(bf16[16,2944]{1,0:T(8,128)(2,1)S(1)} %get-tuple-element.36.facts_ref.refs_0_, f32[2,512,128]{2,1,0:T(8,128)S(1)} %get-tuple-element.40.radial_ref, f32[128,512]{1,0:T(8,128)S(1)} %get-tuple-element.43.flags_ref, ...), custom_call_target="tpu_custom_call" | custom-call | tf_op jit(solution)/shard_map/pulls/pallas_call | solution.py:433
  20.1 0.0 collective-permute-done.5.refs_6_
  20.2 0.0 collective-permute-done.6.refs_7_
  20.2 2.4 %layer.1 = (bf16[32,2816]{1,0:T(8,128)(2,1)S(1)}, bf16[16,2816]{1,0:T(8,128)(2,1)S(1)}, bf16[16,2816]{1,0:T(8,128)(2,1)S(1)}) custom-call(f32[16,16]{1,0:T(8,128)S(1)} %get-tuple-element.38.lent_ref, bf16[512,256]{1,0:T(8,128)(2,1)S(1)} %get-tuple-element.39.hot_ref, f32[2,512,128]{2,1,0:T(8,128)S(1)} %get-tuple-element.40.radial_ref, ...), custom_call_target="tpu_custom_call" | custom-call | tf_op jit(solution)/shard_map/layer/pallas_call | solution.py:458
  22.6 0.1 collective-permute-start.11
  22.7 0.1 collective-permute-start.13
  22.8 3.6 %collective-permute-start.12 = (bf16[16,2816]{1,0:T(8,128)(2,1)S(1)}, bf16[16,2816]{1,0:T(8,128)(2,1)S(1)}, u32[]{:S(2)}, u32[]{:S(2)}) collective-permute-start(bf16[16,2816]{1,0:T(8,128)(2,1)S(1)} %get-tuple-element.60), channel_id=1, source_target_pairs={{0,28},{4,8},{8,4},{12,16},{16,12},{20,24},{24,20},{28,0},{1,29},{... | collective-permute-start | bytes 270344 | tf_op jit(solution)/shard_map/ppermute | solution.py:350
  26.4 0.8 %collective-permute-done.11.refs_1_ = bf16[16,2816]{1,0:T(8,128)(2,1)S(1)} collective-permute-done((bf16[16,2816]{1,0:T(8,128)(2,1)S(1)}, bf16[16,2816]{1,0:T(8,128)(2,1)S(1)}, u32[]{:S(2)}, u32[]{:S(2)}) %collective-permute-start.11) | collective-permute-done | bytes 90144 | tf_op jit(solution)/shard_map/ppermute | solution.py:350
  27.2 0.0 collective-permute-start.14
  27.2 3.3 %collective-permute-done.12.refs_2_ = bf16[16,2816]{1,0:T(8,128)(2,1)S(1)} collective-permute-done((bf16[16,2816]{1,0:T(8,128)(2,1)S(1)}, bf16[16,2816]{1,0:T(8,128)(2,1)S(1)}, u32[]{:S(2)}, u32[]{:S(2)}) %collective-permute-start.12) | collective-permute-done | bytes 90144 | tf_op jit(solution)/shard_map/ppermute | solution.py:350
  30.5 0.0 collective-permute-start.15
  30.5 0.0 collective-permute-done.13.refs_3_
  30.5 1.3 %collective-permute-done.15.refs_5_ = bf16[16,2816]{1,0:T(8,128)(2,1)S(1)} collective-permute-done((bf16[16,2816]{1,0:T(8,128)(2,1)S(1)}, bf16[16,2816]{1,0:T(8,128)(2,1)S(1)}, u32[]{:S(2)}, u32[]{:S(2)}) %collective-permute-start.15) | collective-permute-done | bytes 90144 | tf_op jit(solution)/shard_map/ppermute | solution.py:342
  31.8 2.4 %last_layer.1 = (bf16[25,16,128]{2,1,0:T(8,128)(2,1)}, f32[3,16]{1,0:T(4,128)}) custom-call(bf16[6,16,128]{2,1,0:T(8,128)(2,1)S(1)} %get-tuple-element.35.rest_ref, f32[16,16]{1,0:T(8,128)S(1)} %get-tuple-element.38.lent_ref, bf16[512,256]{1,0:T(8,128)(2,1)S(1)} %get-tuple-element.39.hot_ref, f32[2,512,128]{2,1,0:T(8,128)S(1)} %get-tuple-element.40.radial_ref, ...), custom_call_target="tpu_custom_call" | custom-call | tf_op jit(solution)/shard_map/last_layer/pallas_call | solution.py:475
  (6 shorter events, 0.0 us)
Async XLA Ops:
  1.9 8.1 %collective-permute-start.1 = (bf16[16,2944]{1,0:T(8,128)(2,1)S(1)}, bf16[16,2944]{1,0:T(8,128)(2,1)S(1)}, u32[]{:S(2)}, u32[]{:S(2)}) collective-permute-start(bf16[16,2944]{1,0:T(8,128)(2,1)S(1)} %get-tuple-element.36.facts_ref.refs_0_), channel_id=1, source_target_pairs={{0,2},{1,3},{2,0},{3,1},{4,6},{5,7},{6,4},{7,5},{8,10},{9,11},{10,... | collective-permute-start | bytes 282632 | tf_op jit(solution)/shard_map/ppermute | solution.py:342
  5.0 7.4 %collective-permute-start = (bf16[8,2432]{1,0:T(8,128)(2,1)S(1)}, bf16[8,2432]{1,0:T(8,128)(2,1)S(1)}, u32[]{:S(2)}, u32[]{:S(2)}) collective-permute-start(bf16[8,2432]{1,0:T(8,128)(2,1)S(1)} %get-tuple-element.41), channel_id=1, source_target_pairs={{0,4},{4,0},{8,12},{12,8},{16,20},{20,16},{24,28},{28,24},{1,5},{5... | collective-permute-start | bytes 116744 | tf_op jit(solution)/shard_map/ppermute | solution.py:350
  6.4 6.7 %collective-permute-start.3 = (bf16[8,2432]{1,0:T(8,128)(2,1)S(1)}, bf16[8,2432]{1,0:T(8,128)(2,1)S(1)}, u32[]{:S(2)}, u32[]{:S(2)}) collective-permute-start(bf16[8,2432]{1,0:T(8,128)(2,1)S(1)} %get-tuple-element.52), channel_id=1, source_target_pairs={{0,28},{4,8},{8,4},{12,16},{16,12},{20,24},{24,20},{28,0},{1,29},{... | collective-permute-start | bytes 116744 | tf_op jit(solution)/shard_map/ppermute | solution.py:350
  10.0 10.1 %collective-permute-start.5 = (bf16[16,2944]{1,0:T(8,128)(2,1)S(1)}, bf16[16,2944]{1,0:T(8,128)(2,1)S(1)}, u32[]{:S(2)}, u32[]{:S(2)}) collective-permute-start(bf16[16,2944]{1,0:T(8,128)(2,1)S(1)} %get-tuple-element.36.facts_ref.refs_0_), channel_id=1, source_target_pairs={{0,1},{1,0},{2,3},{3,2},{4,5},{5,4},{6,7},{7,6},{8,9},{9,8},{10,11... | collective-permute-start | bytes 282632 | tf_op jit(solution)/shard_map/ppermute | solution.py:342
  10.0 10.2 %collective-permute-start.6 = (bf16[16,2944]{1,0:T(8,128)(2,1)S(1)}, bf16[16,2944]{1,0:T(8,128)(2,1)S(1)}, u32[]{:S(2)}, u32[]{:S(2)}) collective-permute-start(bf16[16,2944]{1,0:T(8,128)(2,1)S(1)} %collective-permute-done.1.facts_ref.partner_ref.refs_1_), channel_id=1, source_target_pairs={{0,1},{1,0},{2,3},{3,2},{4,5},{5,4},{6,7},{7,6},{8,9},{9,8},{10,11... | collective-permute-start | bytes 282632 | tf_op jit(solution)/shard_map/ppermute | solution.py:342
  12.3 4.0 %collective-permute-start.2 = (bf16[8,2432]{1,0:T(8,128)(2,1)S(1)}, bf16[8,2432]{1,0:T(8,128)(2,1)S(1)}, u32[]{:S(2)}, u32[]{:S(2)}) collective-permute-start(bf16[8,2432]{1,0:T(8,128)(2,1)S(1)} %collective-permute-done.refs_2_), channel_id=1, source_target_pairs={{0,2},{1,3},{2,0},{3,1},{4,6},{5,7},{6,4},{7,5},{8,10},{9,11},{10,... | collective-permute-start | bytes 116744 | tf_op jit(solution)/shard_map/ppermute | solution.py:342
  13.1 4.0 %collective-permute-start.4 = (bf16[8,2432]{1,0:T(8,128)(2,1)S(1)}, bf16[8,2432]{1,0:T(8,128)(2,1)S(1)}, u32[]{:S(2)}, u32[]{:S(2)}) collective-permute-start(bf16[8,2432]{1,0:T(8,128)(2,1)S(1)} %collective-permute-done.3.refs_4_), channel_id=1, source_target_pairs={{0,2},{1,3},{2,0},{3,1},{4,6},{5,7},{6,4},{7,5},{8,10},{9,11},{10,... | collective-permute-start | bytes 116744 | tf_op jit(solution)/shard_map/ppermute | solution.py:342
  14.4 2.7 %collective-permute-start.7 = (bf16[8,2432]{1,0:T(8,128)(2,1)S(1)}, bf16[8,2432]{1,0:T(8,128)(2,1)S(1)}, u32[]{:S(2)}, u32[]{:S(2)}) collective-permute-start(bf16[8,2432]{1,0:T(8,128)(2,1)S(1)} %collective-permute-done.refs_2_), channel_id=1, source_target_pairs={{0,1},{1,0},{2,3},{3,2},{4,5},{5,4},{6,7},{7,6},{8,9},{9,8},{10,11... | collective-permute-start | bytes 116744 | tf_op jit(solution)/shard_map/ppermute | solution.py:342
  16.4 3.8 %collective-permute-start.9 = (bf16[8,2432]{1,0:T(8,128)(2,1)S(1)}, bf16[8,2432]{1,0:T(8,128)(2,1)S(1)}, u32[]{:S(2)}, u32[]{:S(2)}) collective-permute-start(bf16[8,2432]{1,0:T(8,128)(2,1)S(1)} %collective-permute-done.3.refs_4_), channel_id=1, source_target_pairs={{0,1},{1,0},{2,3},{3,2},{4,5},{5,4},{6,7},{7,6},{8,9},{9,8},{10,11... | collective-permute-start | bytes 116744 | tf_op jit(solution)/shard_map/ppermute | solution.py:342
  17.1 3.1 %collective-permute-start.8 = (bf16[8,2432]{1,0:T(8,128)(2,1)S(1)}, bf16[8,2432]{1,0:T(8,128)(2,1)S(1)}, u32[]{:S(2)}, u32[]{:S(2)}) collective-permute-start(bf16[8,2432]{1,0:T(8,128)(2,1)S(1)} %collective-permute-done.2.refs_3_), channel_id=1, source_target_pairs={{0,1},{1,0},{2,3},{3,2},{4,5},{5,4},{6,7},{7,6},{8,9},{9,8},{10,11... | collective-permute-start | bytes 116744 | tf_op jit(solution)/shard_map/ppermute | solution.py:342
  17.1 3.1 %collective-permute-start.10 = (bf16[8,2432]{1,0:T(8,128)(2,1)S(1)}, bf16[8,2432]{1,0:T(8,128)(2,1)S(1)}, u32[]{:S(2)}, u32[]{:S(2)}) collective-permute-start(bf16[8,2432]{1,0:T(8,128)(2,1)S(1)} %collective-permute-done.4.refs_5_), channel_id=1, source_target_pairs={{0,1},{1,0},{2,3},{3,2},{4,5},{5,4},{6,7},{7,6},{8,9},{9,8},{10,11... | collective-permute-start | bytes 116744 | tf_op jit(solution)/shard_map/ppermute | solution.py:342
  22.6 4.6 %collective-permute-start.11 = (bf16[16,2816]{1,0:T(8,128)(2,1)S(1)}, bf16[16,2816]{1,0:T(8,128)(2,1)S(1)}, u32[]{:S(2)}, u32[]{:S(2)}) collective-permute-start(bf16[16,2816]{1,0:T(8,128)(2,1)S(1)} %get-tuple-element.59), channel_id=1, source_target_pairs={{0,4},{4,0},{8,12},{12,8},{16,20},{20,16},{24,28},{28,24},{1,5},{5... | collective-permute-start | bytes 270344 | tf_op jit(solution)/shard_map/ppermute | solution.py:350
  22.7 7.8 %collective-permute-start.13 = (bf16[32,2816]{1,0:T(8,128)(2,1)S(1)}, bf16[32,2816]{1,0:T(8,128)(2,1)S(1)}, u32[]{:S(2)}, u32[]{:S(2)}) collective-permute-start(bf16[32,2816]{1,0:T(8,128)(2,1)S(1)} %get-tuple-element.58.refs_0_), channel_id=1, source_target_pairs={{0,1},{1,0},{2,3},{3,2},{4,5},{5,4},{6,7},{7,6},{8,9},{9,8},{10,11... | collective-permute-start | bytes 540680 | tf_op jit(solution)/shard_map/ppermute | solution.py:342
  22.8 7.7 %collective-permute-start.12 = (bf16[16,2816]{1,0:T(8,128)(2,1)S(1)}, bf16[16,2816]{1,0:T(8,128)(2,1)S(1)}, u32[]{:S(2)}, u32[]{:S(2)}) collective-permute-start(bf16[16,2816]{1,0:T(8,128)(2,1)S(1)} %get-tuple-element.60), channel_id=1, source_target_pairs={{0,28},{4,8},{8,4},{12,16},{16,12},{20,24},{24,20},{28,0},{1,29},{... | collective-permute-start | bytes 270344 | tf_op jit(solution)/shard_map/ppermute | solution.py:350
  27.2 3.3 %collective-permute-start.14 = (bf16[16,2816]{1,0:T(8,128)(2,1)S(1)}, bf16[16,2816]{1,0:T(8,128)(2,1)S(1)}, u32[]{:S(2)}, u32[]{:S(2)}) collective-permute-start(bf16[16,2816]{1,0:T(8,128)(2,1)S(1)} %collective-permute-done.11.refs_1_), channel_id=1, source_target_pairs={{0,1},{1,0},{2,3},{3,2},{4,5},{5,4},{6,7},{7,6},{8,9},{9,8},{10,11... | collective-permute-start | bytes 270344 | tf_op jit(solution)/shard_map/ppermute | solution.py:342
  30.5 1.3 %collective-permute-start.15 = (bf16[16,2816]{1,0:T(8,128)(2,1)S(1)}, bf16[16,2816]{1,0:T(8,128)(2,1)S(1)}, u32[]{:S(2)}, u32[]{:S(2)}) collective-permute-start(bf16[16,2816]{1,0:T(8,128)(2,1)S(1)} %collective-permute-done.12.refs_2_), channel_id=1, source_target_pairs={{0,1},{1,0},{2,3},{3,2},{4,5},{5,4},{6,7},{7,6},{8,9},{9,8},{10,11... | collective-permute-start | bytes 270344 | tf_op jit(solution)/shard_map/ppermute | solution.py:342

commit v7 on v6

--- a/solution.py
+++ b/solution.py
@@ -119,11 +119,10 @@
     return nbr, row(2), row(3).astype(jnp.int32), whole(4), whole(7), whole(10)
 
 
-def start_fetch(refs, layer):
-    count = len(refs) // 2
+def start_fetch(far, near_refs, sems, plan):
     copies = [
-        pltpu.make_async_copy(refs[i].at[layer], refs[count + i], refs[-1].at[i])
-        for i in range(count)
+        pltpu.make_async_copy(far[which].at[layer], near_refs[i], sems.at[i])
+        for i, (layer, which) in enumerate(plan)
     ]
     for copy in copies:
         copy.start()
@@ -131,7 +130,7 @@
 
 
 def edge_scales(
-    atoms, ghosts, slab_devices, facts_ref, rw_ref, hot_ref, radial_ref, flags_ref, lent_ref
+    atoms, ghosts, slab_devices, facts_ref, rw_ref, hot_ref, radial_ref, lent_ref
 ):
     layers, centers = rw_ref.shape[0], rw_ref.shape[1]
     own_count, ghost_count = slab_devices * atoms, slab_devices * ghosts
@@ -139,7 +138,8 @@
     me = lax.axis_index("yz")
     odd = odd_slab()
     edges = hot_ref.shape[0]
-    nbr, valid, picks, distance, _, _ = edge_facts(facts_ref, edges)
+    count = hot_ref.shape[1] // 2
+    nbr, valid, picks, distance, azimuth, polar = edge_facts(facts_ref, edges)
     is_own = nbr < own_count
     ghost = nbr - own_count
     below = ghost < ghost_count
@@ -150,62 +150,70 @@
     inner = jnp.where(
         is_own,
         upper * atoms + nbr % atoms,
-        2 * atoms + (1 - paired) * (2 * ghosts) + upper * ghosts + ghost % ghosts,
+        2 * atoms + upper * (2 * ghosts) + (1 - paired) * ghosts + ghost % ghosts,
     )
     place = (slot % half) * (2 * atoms + 4 * ghosts) + inner
-    rows = lax.broadcasted_iota(jnp.int32, (flags_ref.shape[0], edges), 0)
+    rows = lax.broadcasted_iota(jnp.int32, (count, edges), 0)
     hot = jnp.where((rows == place) & (valid != 0.0), 1.0, 0.0).astype(F32)
-    flags_ref[...] = hot
     hot_cols = jnp.transpose(hot).astype(BF16)
     hot_ref[...] = jnp.concatenate([hot_cols, hot_cols], axis=1)
     middle = 1.0 + 0.5 * lax.broadcasted_iota(jnp.int32, (centers, edges), 0).astype(F32)
     basis = jnp.exp(-jnp.square((distance - middle) / 0.5))
     for layer in range(layers):
         scale = dot(basis, rw_ref[layer], ((0,), (0,)), HIGHEST)
-        radial_ref[layer] = scale / (1.0 + jnp.exp(-scale))
+        radial = scale / (1.0 + jnp.exp(-scale))
+        radial_ref[layer] = radial
     lent_ref[...] = lent_hot(picks[:, : 2 * ghosts], atoms)
-
-
-def scale_kernel(atoms, ghosts, slab_devices, count, fetched, facts_ref, rw_ref, *refs):
-    far, refs = refs[:count], refs[count:]
-    copies = []
-    for i, layer in enumerate(fetched):
-        near_refs = refs[4 + count * i : 4 + count * (i + 1)]
-        copies += start_fetch((*far, *near_refs, refs[-1].at[i]), layer)
-    edge_scales(atoms, ghosts, slab_devices, facts_ref, rw_ref, *refs[:4])
+    sin_polar = jnp.sin(polar)
+    dirs = [sin_polar * jnp.cos(azimuth), sin_polar * jnp.sin(azimuth), jnp.cos(polar)]
+    channels = radial.shape[1]
+    high = radial.astype(BF16)
+    both = jnp.concatenate([high, (radial - high.astype(F32)).astype(BF16)], axis=1)
+    pulls = []
+    for axis in range(3):
+        along = hot * dirs[axis]
+        high = along.astype(BF16)
+        low = (along - high.astype(F32)).astype(BF16)
+        got = dot(jnp.concatenate([high, low], axis=0), both)
+        pulls.append(got[:count, :channels] + got[:count, channels:] + got[count:, :channels])
+    return dirs, pulls
+
+
+def own_scale_kernel(atoms, ghosts, slab_devices, count, plan, facts_ref, rw_ref, *refs):
+    far, (hot_ref, radial_ref, lent_ref, dirs_ref, part_ref), refs = (
+        refs[:count], refs[count : count + 5], refs[count + 5 :]
+    )
+    copies = start_fetch(far, refs[:-1], refs[-1], plan)
+    dirs, pulls = edge_scales(
+        atoms, ghosts, slab_devices, facts_ref, rw_ref, hot_ref, radial_ref, lent_ref
+    )
+    columns = jnp.transpose(jnp.concatenate([*dirs, *dirs, *dirs[:2]], axis=0))
+    for axis in range(3):
+        dirs_ref[axis] = jnp.broadcast_to(columns[:, axis : axis + 1], dirs_ref.shape[1:])
+    part_ref[...] = jnp.concatenate(pulls, axis=1)
     for copy in copies:
         copy.wait()
 
 
-def pull_kernel(
-    facts_ref, radial_ref, flags_ref, partner_ref, radial_y_ref, flags_y_ref, dirs_ref, pulls_ref
+def partner_scale_kernel(
+    atoms, ghosts, slab_devices, count, plan, facts_ref, rw_ref, part_ref, *refs
 ):
-    edges, channels = radial_ref.shape[1:]
-    last = radial_ref.shape[0] - 1
-    rows = flags_ref.shape[0]
-    totals = [0.0, 0.0, 0.0]
-    for ref, scale_ref, hot_ref in (
-        (facts_ref, radial_ref, flags_ref), (partner_ref, radial_y_ref, flags_y_ref)
-    ):
-        _, _, _, _, azimuth, polar = edge_facts(ref, edges)
-        sin_polar = jnp.sin(polar)
-        dirs = [sin_polar * jnp.cos(azimuth), sin_polar * jnp.sin(azimuth), jnp.cos(polar)]
-        if ref is facts_ref:
-            columns = jnp.transpose(jnp.concatenate([*dirs, *dirs, *dirs[:2]], axis=0))
-            for axis in range(3):
-                dirs_ref[axis] = jnp.broadcast_to(columns[:, axis : axis + 1], (edges, channels))
-        radial = scale_ref[last]
-        high = radial.astype(BF16)
-        both = jnp.concatenate([high, (radial - high.astype(F32)).astype(BF16)], axis=1)
-        for axis in range(3):
-            along = hot_ref[...] * dirs[axis]
-            high = along.astype(BF16)
-            low = (along - high.astype(F32)).astype(BF16)
-            got = dot(jnp.concatenate([high, low], axis=0), both)
-            totals[axis] += (
-                got[:rows, :channels] + got[:rows, channels:] + got[rows:, :channels]
-            )
-    pulls_ref[...] = jnp.concatenate(totals, axis=1).astype(BF16)
+    far, (hot_ref, radial_ref, lent_ref, pulls_ref), refs = (
+        refs[:count], refs[count : count + 4], refs[count + 4 :]
+    )
+    copies = start_fetch(far, refs[:-1], refs[-1], plan)
+    _, pulls = edge_scales(
+        atoms, ghosts, slab_devices, facts_ref, rw_ref, hot_ref, radial_ref, lent_ref
+    )
+    pulls_ref[...] = (part_ref[...] + jnp.concatenate(pulls, axis=1)).astype(BF16)
+    for copy in copies:
+        copy.wait()
+
+
+def join_kernel(pair_ref, other_ref, both_ref):
+    ghosts = pair_ref.shape[0]
+    both_ref[:ghosts] = pair_ref[...]
+    both_ref[ghosts:] = other_ref[...]
 
 
 def layer_sums(layer, degrees, channels, atoms, per_atom, tables, weights, hots, radials, scratch):
@@ -214,10 +222,9 @@
     w_zero, w_one_re, w_one_im, w_two_re, w_two_im = (ref[...] for ref in weights)
     width = joined.shape[1]
     start = 0
-    for ref in tables:
-        count = ref.shape[0]
-        joined[start : start + count] = ref[:, :width].astype(F32)
-        start += count
+    for ref, begin, end in tables:
+        joined[start : start + end - begin] = ref[begin:end, :width].astype(F32)
+        start += end - begin
     rows = start
 
     def put(column, value):
@@ -271,7 +278,7 @@
     both = own_ref.shape[0]
     atoms, ghosts = both // 2, lent_ref.shape[1] // 2
     sums, _, _ = layer_sums(
-        layer, degrees, channels, both, per_atom, tables, weights,
+        layer, degrees, channels, both, per_atom, [(ref, 0, ref.shape[0]) for ref in tables], weights,
         (hot_ref, hot_y_ref), (radial_ref, radial_y_ref), scratch,
     )
     width = len(sums) * channels
@@ -288,10 +295,12 @@
         for slot in range(pulls_ref.shape[0] // block):
             cols = slice(width + slot // 2 * part, width + (slot // 2 + 1) * part)
             at = slot * block
-            for ref, size in ((own_ref, atoms), (pair_ref, ghosts), (other_ref, ghosts)):
+            for ref, size, gap in (
+                (own_ref, atoms, 2 * atoms), (pair_ref, ghosts, ghosts), (other_ref, ghosts, 0)
+            ):
                 to = slot % 2 * size
                 ref[to : to + size, cols] = pulls_ref[at : at + size]
-                at += 2 * size
+                at += gap
 
 
 def last_kernel(
@@ -302,8 +311,16 @@
     out_ref, force_ref = refs[count + 5 : count + 7]
     scratch = refs[count + 7 :]
     joined = scratch[0]
+    ghosts = lent_ref.shape[1] // 2
+    pieces = []
+    for slot in range(count // 3):
+        own_rows, pair_rows, other_rows = tables[3 * slot : 3 * slot + 3]
+        pieces.append((own_rows, 0, 2 * atoms))
+        for upper in range(2):
+            span = (upper * ghosts, (upper + 1) * ghosts)
+            pieces += [(pair_rows, *span), (other_rows, *span)]
     sums, first, zero = layer_sums(
-        layer, degrees, channels, atoms, per_atom, tables, weights, (hot_ref,), (radial_ref,), scratch
+        layer, degrees, channels, atoms, per_atom, pieces, weights, (hot_ref,), (radial_ref,), scratch
     )
     order = slot_order(degrees)
     for place, slot in enumerate(order):
@@ -314,7 +331,6 @@
 
     width = len(sums) * channels
     part = 3 * channels
-    ghosts = lent_ref.shape[1] // 2
     own, lent = 0.0, []
     for slot in range(count // 3):
         cols = slice(width + slot // 2 * part, width + (slot // 2 + 1) * part)
@@ -388,6 +404,7 @@
     far = pl.BlockSpec(memory_space=pl.ANY)
 
     half = slab_devices // 2
+    bits = order_bits(slab_devices)
     own, pair, other, rest, radial_weight, vector = pl.pallas_call(
         pack_kernel,
         out_shape=[
@@ -412,46 +429,52 @@
     near_weights = [held(array.shape[1:], array.dtype) for array in weights]
     side_shapes = [
         held((edges, 2 * rows), BF16), held((layers, edges, channels), F32),
-        held((rows, edges), F32), held((atoms, 2 * ghosts), F32),
+        held((atoms, 2 * ghosts), F32),
     ]
-
-    def scales(facts, fetched):
+    later = [(layer, which) for layer in range(1, layers) for which in range(count)]
+    plans = (
+        [(0, which) for which in range(count)] + [entry for entry in later if entry[1] < 2],
+        [entry for entry in later if entry[1] >= 2],
+    )
+
+    def scales(kernel, plan, more, *arrays):
         return pl.pallas_call(
-            functools.partial(scale_kernel, atoms, ghosts, slab_devices, count, fetched),
-            out_shape=[*side_shapes, *(near_weights * len(fetched))],
-            in_specs=[VMEM] * 2 + [far] * count,
-            out_specs=[VMEM] * (4 + count * len(fetched)),
-            scratch_shapes=[pltpu.SemaphoreType.DMA((len(fetched), count))],
+            functools.partial(kernel, atoms, ghosts, slab_devices, count, plan),
+            out_shape=[*side_shapes, *more, *(near_weights[which] for _, which in plan)],
+            in_specs=[VMEM] * len(arrays) + [far] * count,
+            out_specs=[VMEM] * (3 + len(more) + len(plan)),
+            scratch_shapes=[pltpu.SemaphoreType.DMA((len(plan),))],
             compiler_params=params,
-        )(*near(facts, radial_weight), *away(*weights))
-
-    hot, radial, flags, lent, *first_weights = scales(own, (0,))
-    got_pair, flags = lax.optimization_barrier((got_pair, flags))
-    pair_y = across(got_pair, half, slab_devices)
-    other_y = across(got_other, half, slab_devices)
-    hot_y, radial_y, flags_y, lent_y, *later_weights = scales(got_own, tuple(range(1, layers)))
-    dirs, pulls = pl.pallas_call(
-        pull_kernel,
-        out_shape=[held((3, edges, channels), F32), held((rows, 3 * channels), BF16)],
-        in_specs=[VMEM] * 6,
-        out_specs=[VMEM] * 2,
+        )(*near(*arrays), *away(*weights))
+
+    hot, radial, lent, dirs, part, *first_weights = scales(
+        own_scale_kernel, plans[0],
+        [held((3, edges, channels), F32), held((rows, 3 * channels), F32)], own, radial_weight,
+    )
+    got_pair, part = lax.optimization_barrier((got_pair, part))
+    joined = pl.pallas_call(
+        join_kernel,
+        out_shape=held((2 * ghosts, width), BF16),
+        in_specs=[VMEM] * 2,
+        out_specs=VMEM,
         compiler_params=params,
-        name="pulls",
-    )(*near(own, radial, flags, got_own, radial_y, flags_y))
-
-    bits = order_bits(slab_devices)
-    blocks = {0: (own, got_pair, got_other)}
-    blocks[half] = (got_own, pair_y, other_y)
-    blocks = spread(blocks, bits[1:], slab_devices)
+        name="join",
+    )(*near(got_pair, got_other))
+    joined_y = across(joined, half, slab_devices)
+    hot_y, radial_y, lent_y, pulls, *later_weights = scales(
+        partner_scale_kernel, plans[1], [held((rows, 3 * channels), BF16)],
+        got_own, radial_weight, part,
+    )
+    blocks = spread({0: (own, joined), half: (got_own, joined_y)}, bits[1:], slab_devices)
     tables = [
         blocks[slot + upper][kind]
-        for slot in range(half) for kind in range(3) for upper in (0, half)
+        for slot in range(half) for kind in range(2) for upper in (0, half)
     ]
     scratch = [pltpu.VMEM((rows, width), F32), pltpu.VMEM((2 * rows, width), BF16)]
     per_atom = edges // atoms
-    weights = (*first_weights, *later_weights)
+    fetched = dict(zip(plans[0] + plans[1], [*first_weights, *later_weights]))
     for layer in range(layers):
-        now = weights[layer * count : (layer + 1) * count]
+        now = [fetched[layer, which] for which in range(count)]
         if layer < layers - 1:
             last = layer == layers - 2
             wide = width + ((half + 1) // 2 * 3 * channels if last else 0)

time: 34.3 us -> 32.6 us (0.950)
  starting transfers between devices: 14.8 us -> 12.9 us
  waiting for transfers between devices: 8.28 us -> 8.85 us
  Pallas kernels: 10.3 us -> 9.95 us
    ppermute x12 -> x9, starting transfers between devices: 6.02 us -> 3.23 us  [across(): lax.ppermute(block, 'yz', [(q, q ^ bit) for q in range(slab_devices)])]
    ppermute x4, starting transfers between devices: 8.77 us -> 9.67 us  [toward(): return lax.ppermute(block, 'slab', route)]
    pallas_call x3, Pallas kernels: 4.28 us -> 3.75 us  [the longest x2 3.74 us: scales(): pl.pallas_call(functools.partial(kernel, atoms, ghosts, slab_devices, cou...]
    ppermute x12 -> x9, waiting for transfers between devices: 3.97 us -> 4.29 us  [across(): lax.ppermute(block, 'yz', [(q, q ^ bit) for q in range(slab_devices)])]
  transfers between devices with their start and end apart: 16 -> 13, of which waited for: 6 -> 4; matrix products, arithmetic and copies ran while one was open for 0% -> 0% of each run, Pallas kernels for 13% -> 12%
where the time goes in v7:
time: 32.6 us; the launch traced here: 32.4 us
  starting transfers between devices  12.9 us (40%)
  Pallas kernels  9.95 us (31%)
  waiting for transfers between devices  8.85 us (27%)
  between operations  0.73 us (2%)
    ppermute x4, starting transfers between devices, toward(): return lax.ppermute(block, 'slab', route)  9.67 us
    ppermute x4, waiting for transfers between devices, toward(): return lax.ppermute(block, 'slab', route)  4.56 us
    ppermute x9, waiting for transfers between devices, across(): lax.ppermute(block, 'yz', [(q, q ^ bit) for q in range(slab_devices)])  4.29 us
    pallas_call x2, Pallas kernels, scales(): pl.pallas_call(functools.partial(kernel, atoms, ghosts, slab_devices, cou...  3.74 us
    ppermute x9, starting transfers between devices, across(): lax.ppermute(block, 'yz', [(q, q ^ bit) for q in range(slab_devices)])  3.23 us
    pallas_call x1, Pallas kernels, body(): pl.pallas_call(functools.partial(first_kernel, layer, last, degrees, chan...  2.5 us
    pallas_call x1, Pallas kernels, body(): pl.pallas_call(functools.partial(last_kernel, layer, degrees, channels, a...  2.45 us
    pallas_call x1, Pallas kernels, body(): pl.pallas_call(pack_kernel, out_shape=[held((atoms, width + edges), BF16)...  1.25 us
  transfers between devices with their start and end apart: 13, of which 4 were waited for; matrix products, arithmetic and copies ran while one was open for 0% of the time, Pallas kernels for 12%

profile of v7, /device:TPU:0, one launch (start us, length us, event | category | flops | bytes accessed | tf_op | source)
XLA Modules:
  0.0 32.4 jit_solution(7170816928846537687)
XLA Ops:
  0.6 1.3 %pack.1 = (bf16[16,2944]{1,0:T(8,128)(2,1)S(1)}, bf16[8,2432]{1,0:T(8,128)(2,1)S(1)}, bf16[8,2432]{1,0:T(8,128)(2,1)S(1)}, bf16[6,16,128]{2,1,0:T(8,128)(2,1)S(1...) custom-call(bf16[25,16,128]{2,1,0:T(8,128)(2,1)} %bitcast.10, s32[1,8]{1,0:T(1,128)} %bitcast.16, s32[1,8]{1,0:T(1,128)} %bitcast.17, ...), custom_call_target="tpu_custom_call" | custom-call | tf_op jit(solution)/shard_map/pack/pallas_call | solution.py:408
  1.9 3.0 %collective-permute-start.1 = (bf16[8,2432]{1,0:T(8,128)(2,1)S(1)}, bf16[8,2432]{1,0:T(8,128)(2,1)S(1)}, u32[]{:S(2)}, u32[]{:S(2)}) collective-permute-start(bf16[8,2432]{1,0:T(8,128)(2,1)S(1)} %get-tuple-element.42), channel_id=1, source_target_pairs={{0,4},{4,0},{8,12},{12,8},{16,20},{20,16},{24,28},{28,24},{1,5},{5... | collective-permute-start | bytes 116744 | tf_op jit(solution)/shard_map/ppermute | solution.py:366
  4.9 3.6 %collective-permute-start.2 = (bf16[8,2432]{1,0:T(8,128)(2,1)S(1)}, bf16[8,2432]{1,0:T(8,128)(2,1)S(1)}, u32[]{:S(2)}, u32[]{:S(2)}) collective-permute-start(bf16[8,2432]{1,0:T(8,128)(2,1)S(1)} %get-tuple-element.50), channel_id=1, source_target_pairs={{0,28},{4,8},{8,4},{12,16},{16,12},{20,24},{24,20},{28,0},{1,29},{... | collective-permute-start | bytes 116744 | tf_op jit(solution)/shard_map/ppermute | solution.py:366
  8.5 1.5 %collective-permute-start = (bf16[16,2944]{1,0:T(8,128)(2,1)S(1)}, bf16[16,2944]{1,0:T(8,128)(2,1)S(1)}, u32[]{:S(2)}, u32[]{:S(2)}) collective-permute-start(bf16[16,2944]{1,0:T(8,128)(2,1)S(1)} %get-tuple-element.35.facts_ref.refs_0_), channel_id=1, source_target_pairs={{0,2},{1,3},{2,0},{3,1},{4,6},{5,7},{6,4},{7,5},{8,10},{9,11},{10,... | collective-permute-start | bytes 282632 | tf_op jit(solution)/shard_map/ppermute | solution.py:358
  10.0 2.1 %shard_map.158 = (bf16[512,256]{1,0:T(8,128)(2,1)S(1)}, f32[2,512,128]{2,1,0:T(8,128)S(1)}, f32[16,16]{1,0:T(8,128)S(1)}, f32[3,512,128]{2,1,0:T(8,128)S(1)}, f3...) custom-call(bf16[16,2944]{1,0:T(8,128)(2,1)S(1)} %get-tuple-element., ...), custom_call_target="tpu_custom_call" | custom-call | tf_op jit(solution)/shard_map/pallas_call | solution.py:441
  12.1 0.0 collective-permute-done.1.pair_ref
  12.1 0.0 collective-permute-done.2.other_ref
  12.2 1.0 %collective-permute-start.3 = (bf16[16,2432]{1,0:T(8,128)(2,1)S(1)}, bf16[16,2432]{1,0:T(8,128)(2,1)S(1)}, u32[]{:S(2)}, u32[]{:S(2)}) collective-permute-start(bf16[16,2432]{1,0:T(8,128)(2,1)S(1)} %join.1.refs_2_), channel_id=1, source_target_pairs={{0,2},{1,3},{2,0},{3,1},{4,6},{5,7},{6,4},{7,5},{8,10},{9,11},{10,... | collective-permute-start | bytes 233480 | tf_op jit(solution)/shard_map/ppermute | solution.py:358
  13.1 0.0 collective-permute-start.4
  13.1 0.0 collective-permute-done.facts_ref.refs_1_
  13.1 0.5 %collective-permute-start.5 = (bf16[16,2944]{1,0:T(8,128)(2,1)S(1)}, bf16[16,2944]{1,0:T(8,128)(2,1)S(1)}, u32[]{:S(2)}, u32[]{:S(2)}) collective-permute-start(bf16[16,2944]{1,0:T(8,128)(2,1)S(1)} %collective-permute-done.facts_ref.refs_1_), channel_id=1, source_target_pairs={{0,1},{1,0},{2,3},{3,2},{4,5},{5,4},{6,7},{7,6},{8,9},{9,8},{10,11... | collective-permute-start | bytes 282632 | tf_op jit(solution)/shard_map/ppermute | solution.py:358
  13.6 0.0 collective-permute-start.6
  13.6 3.0 %collective-permute-done.3.refs_3_ = bf16[16,2432]{1,0:T(8,128)(2,1)S(1)} collective-permute-done((bf16[16,2432]{1,0:T(8,128)(2,1)S(1)}, bf16[16,2432]{1,0:T(8,128)(2,1)S(1)}, u32[]{:S(2)}, u32[]{:S(2)}) %collective-permute-start.3) | collective-permute-done | bytes 77856 | tf_op jit(solution)/shard_map/ppermute | solution.py:358
  16.6 0.0 collective-permute-start.7
  16.6 1.6 %shard_map.159 = (bf16[512,256]{1,0:T(8,128)(2,1)S(1)}, f32[2,512,128]{2,1,0:T(8,128)S(1)}, f32[16,16]{1,0:T(8,128)S(1)}, bf16[128,384]{1,0:T(8,128)(2,1)S(1)}, ...) custom-call(bf16[16,2944]{1,0:T(8,128)(2,1)S(1)} %collective-permute-done.facts_ref.refs_1_,, ...), custom_call_target="tpu_custom_call" | custom-call | tf_op jit(solution)/shard_map/pallas_call | solution.py:441
  18.3 0.0 collective-permute-done.4.refs_4_
  18.3 0.0 collective-permute-done.6.refs_6_
  18.3 0.0 collective-permute-done.5.refs_5_
  18.3 0.0 collective-permute-done.7.refs_7_
  18.3 2.5 %layer.1 = (bf16[32,2816]{1,0:T(8,128)(2,1)S(1)}, bf16[16,2816]{1,0:T(8,128)(2,1)S(1)}, bf16[16,2816]{1,0:T(8,128)(2,1)S(1)}) custom-call(f32[16,16]{1,0:T(8,128)S(1)} %get-tuple-element.37.lent_ref, bf16[512,256]{1,0:T(8,128)(2,1)S(1)} %get-tuple-element.38.hot_ref, f32[2,512,128]{2,1,0:T(8,128)S(1)} %get-tuple-element.39.radial_ref, ...), custom_call_target="tpu_custom_call" | custom-call | tf_op jit(solution)/shard_map/layer/pallas_call | solution.py:481
  20.8 0.1 collective-permute-start.8
  20.9 3.0 %collective-permute-start.9 = (bf16[16,2816]{1,0:T(8,128)(2,1)S(1)}, bf16[16,2816]{1,0:T(8,128)(2,1)S(1)}, u32[]{:S(2)}, u32[]{:S(2)}) collective-permute-start(bf16[16,2816]{1,0:T(8,128)(2,1)S(1)} %get-tuple-element.58), channel_id=1, source_target_pairs={{0,28},{4,8},{8,4},{12,16},{16,12},{20,24},{24,20},{28,0},{1,29},{... | collective-permute-start | bytes 270344 | tf_op jit(solution)/shard_map/ppermute | solution.py:366
  23.9 0.2 collective-permute-start.10
  24.1 1.8 %collective-permute-done.8.refs_1_ = bf16[16,2816]{1,0:T(8,128)(2,1)S(1)} collective-permute-done((bf16[16,2816]{1,0:T(8,128)(2,1)S(1)}, bf16[16,2816]{1,0:T(8,128)(2,1)S(1)}, u32[]{:S(2)}, u32[]{:S(2)}) %collective-permute-start.8) | collective-permute-done | bytes 90144 | tf_op jit(solution)/shard_map/ppermute | solution.py:366
  25.9 0.0 collective-permute-start.11
  25.9 2.8 %collective-permute-done.9.refs_2_ = bf16[16,2816]{1,0:T(8,128)(2,1)S(1)} collective-permute-done((bf16[16,2816]{1,0:T(8,128)(2,1)S(1)}, bf16[16,2816]{1,0:T(8,128)(2,1)S(1)}, u32[]{:S(2)}, u32[]{:S(2)}) %collective-permute-start.9) | collective-permute-done | bytes 90144 | tf_op jit(solution)/shard_map/ppermute | solution.py:366
  28.7 0.0 collective-permute-start.12
  28.7 0.0 collective-permute-done.11.refs_4_
  28.7 1.3 %collective-permute-done.12.refs_5_ = bf16[16,2816]{1,0:T(8,128)(2,1)S(1)} collective-permute-done((bf16[16,2816]{1,0:T(8,128)(2,1)S(1)}, bf16[16,2816]{1,0:T(8,128)(2,1)S(1)}, u32[]{:S(2)}, u32[]{:S(2)}) %collective-permute-start.12) | collective-permute-done | bytes 90144 | tf_op jit(solution)/shard_map/ppermute | solution.py:358
  30.0 0.0 collective-permute-done.10.refs_3_
  30.0 2.5 %last_layer.1 = (bf16[25,16,128]{2,1,0:T(8,128)(2,1)}, f32[3,16]{1,0:T(4,128)}) custom-call(bf16[6,16,128]{2,1,0:T(8,128)(2,1)S(1)} %get-tuple-element.34.rest_ref, f32[16,16]{1,0:T(8,128)S(1)} %get-tuple-element.37.lent_ref, bf16[512,256]{1,0:T(8,128)(2,1)S(1)} %get-tuple-element.38.hot_ref, f32[2,512,128]{2,1,0:T(8,128)S(1)} %get-tuple-element.39.radial_ref, ...), custom_call_target="tpu_custom_call" | custom-call | tf_op jit(solution)/shard_map/last_layer/pallas_call | solution.py:498
  (1 shorter events, 0.0 us)
Async XLA Ops:
  1.9 10.2 %collective-permute-start.1 = (bf16[8,2432]{1,0:T(8,128)(2,1)S(1)}, bf16[8,2432]{1,0:T(8,128)(2,1)S(1)}, u32[]{:S(2)}, u32[]{:S(2)}) collective-permute-start(bf16[8,2432]{1,0:T(8,128)(2,1)S(1)} %get-tuple-element.42), channel_id=1, source_target_pairs={{0,4},{4,0},{8,12},{12,8},{16,20},{20,16},{24,28},{28,24},{1,5},{5... | collective-permute-start | bytes 116744 | tf_op jit(solution)/shard_map/ppermute | solution.py:366
  4.9 7.2 %collective-permute-start.2 = (bf16[8,2432]{1,0:T(8,128)(2,1)S(1)}, bf16[8,2432]{1,0:T(8,128)(2,1)S(1)}, u32[]{:S(2)}, u32[]{:S(2)}) collective-permute-start(bf16[8,2432]{1,0:T(8,128)(2,1)S(1)} %get-tuple-element.50), channel_id=1, source_target_pairs={{0,28},{4,8},{8,4},{12,16},{16,12},{20,24},{24,20},{28,0},{1,29},{... | collective-permute-start | bytes 116744 | tf_op jit(solution)/shard_map/ppermute | solution.py:366
  8.5 4.6 %collective-permute-start = (bf16[16,2944]{1,0:T(8,128)(2,1)S(1)}, bf16[16,2944]{1,0:T(8,128)(2,1)S(1)}, u32[]{:S(2)}, u32[]{:S(2)}) collective-permute-start(bf16[16,2944]{1,0:T(8,128)(2,1)S(1)} %get-tuple-element.35.facts_ref.refs_0_), channel_id=1, source_target_pairs={{0,2},{1,3},{2,0},{3,1},{4,6},{5,7},{6,4},{7,5},{8,10},{9,11},{10,... | collective-permute-start | bytes 282632 | tf_op jit(solution)/shard_map/ppermute | solution.py:358
  12.2 4.5 %collective-permute-start.3 = (bf16[16,2432]{1,0:T(8,128)(2,1)S(1)}, bf16[16,2432]{1,0:T(8,128)(2,1)S(1)}, u32[]{:S(2)}, u32[]{:S(2)}) collective-permute-start(bf16[16,2432]{1,0:T(8,128)(2,1)S(1)} %join.1.refs_2_), channel_id=1, source_target_pairs={{0,2},{1,3},{2,0},{3,1},{4,6},{5,7},{6,4},{7,5},{8,10},{9,11},{10,... | collective-permute-start | bytes 233480 | tf_op jit(solution)/shard_map/ppermute | solution.py:358
  13.1 5.2 %collective-permute-start.4 = (bf16[16,2944]{1,0:T(8,128)(2,1)S(1)}, bf16[16,2944]{1,0:T(8,128)(2,1)S(1)}, u32[]{:S(2)}, u32[]{:S(2)}) collective-permute-start(bf16[16,2944]{1,0:T(8,128)(2,1)S(1)} %get-tuple-element.35.facts_ref.refs_0_), channel_id=1, source_target_pairs={{0,1},{1,0},{2,3},{3,2},{4,5},{5,4},{6,7},{7,6},{8,9},{9,8},{10,11... | collective-permute-start | bytes 282632 | tf_op jit(solution)/shard_map/ppermute | solution.py:358
  13.1 5.2 %collective-permute-start.5 = (bf16[16,2944]{1,0:T(8,128)(2,1)S(1)}, bf16[16,2944]{1,0:T(8,128)(2,1)S(1)}, u32[]{:S(2)}, u32[]{:S(2)}) collective-permute-start(bf16[16,2944]{1,0:T(8,128)(2,1)S(1)} %collective-permute-done.facts_ref.refs_1_), channel_id=1, source_target_pairs={{0,1},{1,0},{2,3},{3,2},{4,5},{5,4},{6,7},{7,6},{8,9},{9,8},{10,11... | collective-permute-start | bytes 282632 | tf_op jit(solution)/shard_map/ppermute | solution.py:358
  13.6 4.7 %collective-permute-start.6 = (bf16[16,2432]{1,0:T(8,128)(2,1)S(1)}, bf16[16,2432]{1,0:T(8,128)(2,1)S(1)}, u32[]{:S(2)}, u32[]{:S(2)}) collective-permute-start(bf16[16,2432]{1,0:T(8,128)(2,1)S(1)} %join.1.refs_2_), channel_id=1, source_target_pairs={{0,1},{1,0},{2,3},{3,2},{4,5},{5,4},{6,7},{7,6},{8,9},{9,8},{10,11... | collective-permute-start | bytes 233480 | tf_op jit(solution)/shard_map/ppermute | solution.py:358
  16.6 1.7 %collective-permute-start.7 = (bf16[16,2432]{1,0:T(8,128)(2,1)S(1)}, bf16[16,2432]{1,0:T(8,128)(2,1)S(1)}, u32[]{:S(2)}, u32[]{:S(2)}) collective-permute-start(bf16[16,2432]{1,0:T(8,128)(2,1)S(1)} %collective-permute-done.3.refs_3_), channel_id=1, source_target_pairs={{0,1},{1,0},{2,3},{3,2},{4,5},{5,4},{6,7},{7,6},{8,9},{9,8},{10,11... | collective-permute-start | bytes 233480 | tf_op jit(solution)/shard_map/ppermute | solution.py:358
  20.8 5.1 %collective-permute-start.8 = (bf16[16,2816]{1,0:T(8,128)(2,1)S(1)}, bf16[16,2816]{1,0:T(8,128)(2,1)S(1)}, u32[]{:S(2)}, u32[]{:S(2)}) collective-permute-start(bf16[16,2816]{1,0:T(8,128)(2,1)S(1)} %get-tuple-element.57), channel_id=1, source_target_pairs={{0,4},{4,0},{8,12},{12,8},{16,20},{20,16},{24,28},{28,24},{1,5},{5... | collective-permute-start | bytes 270344 | tf_op jit(solution)/shard_map/ppermute | solution.py:366
  20.9 7.8 %collective-permute-start.9 = (bf16[16,2816]{1,0:T(8,128)(2,1)S(1)}, bf16[16,2816]{1,0:T(8,128)(2,1)S(1)}, u32[]{:S(2)}, u32[]{:S(2)}) collective-permute-start(bf16[16,2816]{1,0:T(8,128)(2,1)S(1)} %get-tuple-element.58), channel_id=1, source_target_pairs={{0,28},{4,8},{8,4},{12,16},{16,12},{20,24},{24,20},{28,0},{1,29},{... | collective-permute-start | bytes 270344 | tf_op jit(solution)/shard_map/ppermute | solution.py:366
  23.9 6.1 %collective-permute-start.10 = (bf16[32,2816]{1,0:T(8,128)(2,1)S(1)}, bf16[32,2816]{1,0:T(8,128)(2,1)S(1)}, u32[]{:S(2)}, u32[]{:S(2)}) collective-permute-start(bf16[32,2816]{1,0:T(8,128)(2,1)S(1)} %get-tuple-element.56.refs_0_), channel_id=1, source_target_pairs={{0,1},{1,0},{2,3},{3,2},{4,5},{5,4},{6,7},{7,6},{8,9},{9,8},{10,11... | collective-permute-start | bytes 540680 | tf_op jit(solution)/shard_map/ppermute | solution.py:358
  25.9 2.8 %collective-permute-start.11 = (bf16[16,2816]{1,0:T(8,128)(2,1)S(1)}, bf16[16,2816]{1,0:T(8,128)(2,1)S(1)}, u32[]{:S(2)}, u32[]{:S(2)}) collective-permute-start(bf16[16,2816]{1,0:T(8,128)(2,1)S(1)} %collective-permute-done.8.refs_1_), channel_id=1, source_target_pairs={{0,1},{1,0},{2,3},{3,2},{4,5},{5,4},{6,7},{7,6},{8,9},{9,8},{10,11... | collective-permute-start | bytes 270344 | tf_op jit(solution)/shard_map/ppermute | solution.py:358
  28.7 1.3 %collective-permute-start.12 = (bf16[16,2816]{1,0:T(8,128)(2,1)S(1)}, bf16[16,2816]{1,0:T(8,128)(2,1)S(1)}, u32[]{:S(2)}, u32[]{:S(2)}) collective-permute-start(bf16[16,2816]{1,0:T(8,128)(2,1)S(1)} %collective-permute-done.9.refs_2_), channel_id=1, source_target_pairs={{0,1},{1,0},{2,3},{3,2},{4,5},{5,4},{6,7},{7,6},{8,9},{9,8},{10,11... | collective-permute-start | bytes 270344 | tf_op jit(solution)/shard_map/ppermute | solution.py:358

commit v8 on v7

--- a/solution.py
+++ b/solution.py
@@ -139,7 +139,7 @@
     odd = odd_slab()
     edges = hot_ref.shape[0]
     count = hot_ref.shape[1] // 2
-    nbr, valid, picks, distance, azimuth, polar = edge_facts(facts_ref, edges)
+    nbr, valid, picks, distance, _, _ = edge_facts(facts_ref, edges)
     is_own = nbr < own_count
     ghost = nbr - own_count
     below = ghost < ghost_count
@@ -164,9 +164,14 @@
         radial = scale / (1.0 + jnp.exp(-scale))
         radial_ref[layer] = radial
     lent_ref[...] = lent_hot(picks[:, : 2 * ghosts], atoms)
+    return hot, radial
+
+
+def pull_sums(facts_ref, hot, radial):
+    _, _, _, _, azimuth, polar = edge_facts(facts_ref, hot.shape[1])
     sin_polar = jnp.sin(polar)
     dirs = [sin_polar * jnp.cos(azimuth), sin_polar * jnp.sin(azimuth), jnp.cos(polar)]
-    channels = radial.shape[1]
+    count, channels = hot.shape[0], radial.shape[1]
     high = radial.astype(BF16)
     both = jnp.concatenate([high, (radial - high.astype(F32)).astype(BF16)], axis=1)
     pulls = []
@@ -176,37 +181,40 @@
         low = (along - high.astype(F32)).astype(BF16)
         got = dot(jnp.concatenate([high, low], axis=0), both)
         pulls.append(got[:count, :channels] + got[:count, channels:] + got[count:, :channels])
-    return dirs, pulls
-
-
-def own_scale_kernel(atoms, ghosts, slab_devices, count, plan, facts_ref, rw_ref, *refs):
-    far, (hot_ref, radial_ref, lent_ref, dirs_ref, part_ref), refs = (
+    return dirs, jnp.concatenate(pulls, axis=1)
+
+
+def own_scale_kernel(
+    atoms, ghosts, slab_devices, facts_ref, rw_ref, hot_ref, radial_ref, lent_ref, flags_ref
+):
+    flags_ref[...], _ = edge_scales(
+        atoms, ghosts, slab_devices, facts_ref, rw_ref, hot_ref, radial_ref, lent_ref
+    )
+
+
+def partner_scale_kernel(
+    atoms, ghosts, slab_devices, count, plan,
+    facts_ref, rw_ref, own_ref, own_radial_ref, flags_ref, *refs,
+):
+    far, (hot_ref, radial_ref, lent_ref, dirs_ref, pulls_ref), refs = (
         refs[:count], refs[count : count + 5], refs[count + 5 :]
     )
     copies = start_fetch(far, refs[:-1], refs[-1], plan)
-    dirs, pulls = edge_scales(
+    hot, radial = edge_scales(
         atoms, ghosts, slab_devices, facts_ref, rw_ref, hot_ref, radial_ref, lent_ref
     )
+    _, pulls = pull_sums(facts_ref, hot, radial)
+    dirs, own_pulls = pull_sums(own_ref, flags_ref[...], own_radial_ref[own_radial_ref.shape[0] - 1])
+    pulls_ref[...] = (pulls + own_pulls).astype(BF16)
     columns = jnp.transpose(jnp.concatenate([*dirs, *dirs, *dirs[:2]], axis=0))
     for axis in range(3):
         dirs_ref[axis] = jnp.broadcast_to(columns[:, axis : axis + 1], dirs_ref.shape[1:])
-    part_ref[...] = jnp.concatenate(pulls, axis=1)
     for copy in copies:
         copy.wait()
 
 
-def partner_scale_kernel(
-    atoms, ghosts, slab_devices, count, plan, facts_ref, rw_ref, part_ref, *refs
-):
-    far, (hot_ref, radial_ref, lent_ref, pulls_ref), refs = (
-        refs[:count], refs[count : count + 4], refs[count + 4 :]
-    )
-    copies = start_fetch(far, refs[:-1], refs[-1], plan)
-    _, pulls = edge_scales(
-        atoms, ghosts, slab_devices, facts_ref, rw_ref, hot_ref, radial_ref, lent_ref
-    )
-    pulls_ref[...] = (part_ref[...] + jnp.concatenate(pulls, axis=1)).astype(BF16)
-    for copy in copies:
+def fetch_kernel(count, plan, *refs):
+    for copy in start_fetch(refs[:count], refs[count:-1], refs[-1], plan):
         copy.wait()
 
 
@@ -431,27 +439,17 @@
         held((edges, 2 * rows), BF16), held((layers, edges, channels), F32),
         held((atoms, 2 * ghosts), F32),
     ]
-    later = [(layer, which) for layer in range(1, layers) for which in range(count)]
-    plans = (
-        [(0, which) for which in range(count)] + [entry for entry in later if entry[1] < 2],
-        [entry for entry in later if entry[1] >= 2],
-    )
-
-    def scales(kernel, plan, more, *arrays):
-        return pl.pallas_call(
-            functools.partial(kernel, atoms, ghosts, slab_devices, count, plan),
-            out_shape=[*side_shapes, *more, *(near_weights[which] for _, which in plan)],
-            in_specs=[VMEM] * len(arrays) + [far] * count,
-            out_specs=[VMEM] * (3 + len(more) + len(plan)),
-            scratch_shapes=[pltpu.SemaphoreType.DMA((len(plan),))],
-            compiler_params=params,
-        )(*near(*arrays), *away(*weights))
-
-    hot, radial, lent, dirs, part, *first_weights = scales(
-        own_scale_kernel, plans[0],
-        [held((3, edges, channels), F32), held((rows, 3 * channels), F32)], own, radial_weight,
-    )
-    got_pair, part = lax.optimization_barrier((got_pair, part))
+    plans = [[(layer, which) for which in range(count)] for layer in range(layers)]
+
+    hot, radial, lent, flags = pl.pallas_call(
+        functools.partial(own_scale_kernel, atoms, ghosts, slab_devices),
+        out_shape=[*side_shapes, held((rows, edges), F32)],
+        in_specs=[VMEM] * 2,
+        out_specs=[VMEM] * 4,
+        compiler_params=params,
+        name="scales",
+    )(*near(own, radial_weight))
+    got_pair, flags = lax.optimization_barrier((got_pair, flags))
     joined = pl.pallas_call(
         join_kernel,
         out_shape=held((2 * ghosts, width), BF16),
@@ -461,10 +459,18 @@
         name="join",
     )(*near(got_pair, got_other))
     joined_y = across(joined, half, slab_devices)
-    hot_y, radial_y, lent_y, pulls, *later_weights = scales(
-        partner_scale_kernel, plans[1], [held((rows, 3 * channels), BF16)],
-        got_own, radial_weight, part,
-    )
+    hot_y, radial_y, lent_y, dirs, pulls, *now = pl.pallas_call(
+        functools.partial(partner_scale_kernel, atoms, ghosts, slab_devices, count, plans[0]),
+        out_shape=[
+            *side_shapes, held((3, edges, channels), F32), held((rows, 3 * channels), BF16),
+            *near_weights,
+        ],
+        in_specs=[VMEM] * 5 + [far] * count,
+        out_specs=[VMEM] * (5 + count),
+        scratch_shapes=[pltpu.SemaphoreType.DMA((count,))],
+        compiler_params=params,
+        name="scales_y",
+    )(*near(got_own, radial_weight, own, radial, flags), *away(*weights))
     blocks = spread({0: (own, joined), half: (got_own, joined_y)}, bits[1:], slab_devices)
     tables = [
         blocks[slot + upper][kind]
@@ -472,9 +478,7 @@
     ]
     scratch = [pltpu.VMEM((rows, width), F32), pltpu.VMEM((2 * rows, width), BF16)]
     per_atom = edges // atoms
-    fetched = dict(zip(plans[0] + plans[1], [*first_weights, *later_weights]))
     for layer in range(layers):
-        now = [fetched[layer, which] for which in range(count)]
         if layer < layers - 1:
             last = layer == layers - 2
             wide = width + ((half + 1) // 2 * 3 * channels if last else 0)
@@ -492,6 +496,15 @@
             )(*near(lent, hot, radial, lent_y, hot_y, radial_y, pulls, *tables, *now))
             got_other = toward(other, -1, slabs)
             got_pair = toward(pair, 1, slabs)
+            now = pl.pallas_call(
+                functools.partial(fetch_kernel, count, plans[layer + 1]),
+                out_shape=near_weights,
+                in_specs=[far] * count,
+                out_specs=[VMEM] * count,
+                scratch_shapes=[pltpu.SemaphoreType.DMA((count,))],
+                compiler_params=params,
+                name="fetch",
+            )(*away(*weights))
             blocks = spread({0: (own, got_pair, got_other)}, bits[1:], slab_devices)
             tables = [block for slot in range(half) for block in blocks[slot]]
         else:

time: 32.6 us -> 33.4 us (1.025)
  waiting for transfers between devices: 8.85 us -> 6.95 us
  starting transfers between devices: 12.9 us -> 14.4 us
  Pallas kernels: 9.95 us -> 11.1 us
    ppermute x9, waiting for transfers between devices: 4.29 us -> 2.38 us  [across(): lax.ppermute(block, 'yz', [(q, q ^ bit) for q in range(slab_devices)])]
    pallas_call x2 -> x3, Pallas kernels: 3.74 us -> 5.08 us  [the longest x1 2.7 us: body(): pl.pallas_call(functools.partial(partner_scale_kernel, atoms, ghosts, sla...]
    ppermute x9, starting transfers between devices: 3.23 us -> 4.14 us  [across(): lax.ppermute(block, 'yz', [(q, q ^ bit) for q in range(slab_devices)])]
    ppermute x4, starting transfers between devices: 9.67 us -> 10.2 us  [toward(): return lax.ppermute(block, 'slab', route)]
  transfers between devices with their start and end apart: 13 -> 13, of which waited for: 4 -> 5; matrix products, arithmetic and copies ran while one was open for 0% -> 0% of each run, Pallas kernels for 12% -> 15%
where the time goes in v8:
time: 33.4 us; the launch traced here: 33.2 us
  starting transfers between devices  14.4 us (43%)
  Pallas kernels  11.1 us (33%)
  waiting for transfers between devices  6.95 us (21%)
  between operations  0.75 us (2%)
    ppermute x4, starting transfers between devices, toward(): return lax.ppermute(block, 'slab', route)  10.2 us
    ppermute x4, waiting for transfers between devices, toward(): return lax.ppermute(block, 'slab', route)  4.56 us
    ppermute x9, starting transfers between devices, across(): lax.ppermute(block, 'yz', [(q, q ^ bit) for q in range(slab_devices)])  4.14 us
    pallas_call x1, Pallas kernels, body(): pl.pallas_call(functools.partial(partner_scale_kernel, atoms, ghosts, sla...  2.7 us
    pallas_call x1, Pallas kernels, body(): pl.pallas_call(functools.partial(last_kernel, layer, degrees, channels, a...  2.39 us
    ppermute x9, waiting for transfers between devices, across(): lax.ppermute(block, 'yz', [(q, q ^ bit) for q in range(slab_devices)])  2.38 us
    pallas_call x1, Pallas kernels, body(): pl.pallas_call(functools.partial(first_kernel, layer, last, degrees, chan...  2.38 us
    pallas_call x1, Pallas kernels, body(): pl.pallas_call(functools.partial(fetch_kernel, count, plans[layer + 1]),...  1.66 us
  transfers between devices with their start and end apart: 13, of which 5 were waited for; matrix products, arithmetic and copies ran while one was open for 0% of the time, Pallas kernels for 15%

profile of v8, /device:TPU:0, one launch (start us, length us, event | category | flops | bytes accessed | tf_op | source)
XLA Modules:
  0.0 33.2 jit_solution(9107162941443342612)
XLA Ops:
  0.6 1.3 %pack.1 = (bf16[16,2944]{1,0:T(8,128)(2,1)S(1)}, bf16[8,2432]{1,0:T(8,128)(2,1)S(1)}, bf16[8,2432]{1,0:T(8,128)(2,1)S(1)}, bf16[6,16,128]{2,1,0:T(8,128)(2,1)S(1...) custom-call(bf16[25,16,128]{2,1,0:T(8,128)(2,1)} %bitcast.10, s32[1,8]{1,0:T(1,128)} %bitcast.16, s32[1,8]{1,0:T(1,128)} %bitcast.17, ...), custom_call_target="tpu_custom_call" | custom-call | tf_op jit(solution)/shard_map/pack/pallas_call | solution.py:416
  1.9 3.0 %collective-permute-start.1 = (bf16[8,2432]{1,0:T(8,128)(2,1)S(1)}, bf16[8,2432]{1,0:T(8,128)(2,1)S(1)}, u32[]{:S(2)}, u32[]{:S(2)}) collective-permute-start(bf16[8,2432]{1,0:T(8,128)(2,1)S(1)} %get-tuple-element.40), channel_id=1, source_target_pairs={{0,4},{4,0},{8,12},{12,8},{16,20},{20,16},{24,28},{28,24},{1,5},{5... | collective-permute-start | bytes 116744 | tf_op jit(solution)/shard_map/ppermute | solution.py:374
  4.9 3.6 %collective-permute-start.2 = (bf16[8,2432]{1,0:T(8,128)(2,1)S(1)}, bf16[8,2432]{1,0:T(8,128)(2,1)S(1)}, u32[]{:S(2)}, u32[]{:S(2)}) collective-permute-start(bf16[8,2432]{1,0:T(8,128)(2,1)S(1)} %get-tuple-element.50), channel_id=1, source_target_pairs={{0,28},{4,8},{8,4},{12,16},{16,12},{20,24},{24,20},{28,0},{1,29},{... | collective-permute-start | bytes 116744 | tf_op jit(solution)/shard_map/ppermute | solution.py:374
  8.5 1.5 %collective-permute-start = (bf16[16,2944]{1,0:T(8,128)(2,1)S(1)}, bf16[16,2944]{1,0:T(8,128)(2,1)S(1)}, u32[]{:S(2)}, u32[]{:S(2)}) collective-permute-start(bf16[16,2944]{1,0:T(8,128)(2,1)S(1)} %get-tuple-element.35.facts_ref.own_ref.refs_0_), channel_id=1, source_target_pairs={{0,2},{1,3},{2,0},{3,1},{4,6},{5,7},{6,4},{7,5},{8,10},{9,11},{10,... | collective-permute-start | bytes 282632 | tf_op jit(solution)/shard_map/ppermute | solution.py:366
  10.0 0.7 %scales.1 = (bf16[512,256]{1,0:T(8,128)(2,1)S(1)}, f32[2,512,128]{2,1,0:T(8,128)S(1)}, f32[16,16]{1,0:T(8,128)S(1)}, f32[128,512]{1,0:T(8,128)S(1)}) custom-call(bf16[16,2944]{1,0:T(8,128)(2,1)S(1)} %get-tuple-element.35.facts_ref.own_ref.refs_0_, f32[2,8,128]{2,1,0:T(8,128)S(1)} %get-tuple-element.36.rw_ref), custom_call_target="tpu_custom_call" | custom-call | tf_op jit(solution)/shard_map/scales/pallas_call | solution.py:444
  10.8 0.0 collective-permute-done.1.pair_ref
  10.8 0.8 %collective-permute-done.2.other_ref = bf16[8,2432]{1,0:T(8,128)(2,1)S(1)} collective-permute-done((bf16[8,2432]{1,0:T(8,128)(2,1)S(1)}, bf16[8,2432]{1,0:T(8,128)(2,1)S(1)}, u32[]{:S(2)}, u32[]{:S(2)}) %collective-permute-start.2) | collective-permute-done | bytes 38944 | tf_op jit(solution)/shard_map/ppermute | solution.py:374
  11.6 1.5 %collective-permute-start.3 = (bf16[16,2432]{1,0:T(8,128)(2,1)S(1)}, bf16[16,2432]{1,0:T(8,128)(2,1)S(1)}, u32[]{:S(2)}, u32[]{:S(2)}) collective-permute-start(bf16[16,2432]{1,0:T(8,128)(2,1)S(1)} %join.1.refs_2_), channel_id=1, source_target_pairs={{0,2},{1,3},{2,0},{3,1},{4,6},{5,7},{6,4},{7,5},{8,10},{9,11},{10,... | collective-permute-start | bytes 233480 | tf_op jit(solution)/shard_map/ppermute | solution.py:366
  13.1 0.0 collective-permute-start.4
  13.1 0.4 %collective-permute-done.facts_ref.refs_1_ = bf16[16,2944]{1,0:T(8,128)(2,1)S(1)} collective-permute-done((bf16[16,2944]{1,0:T(8,128)(2,1)S(1)}, bf16[16,2944]{1,0:T(8,128)(2,1)S(1)}, u32[]{:S(2)}, u32[]{:S(2)}) %collective-permute-start) | collective-permute-done | bytes 94240 | tf_op jit(solution)/shard_map/ppermute | solution.py:366
  13.5 0.1 collective-permute-start.5
  13.6 0.4 %collective-permute-start.6 = (bf16[16,2432]{1,0:T(8,128)(2,1)S(1)}, bf16[16,2432]{1,0:T(8,128)(2,1)S(1)}, u32[]{:S(2)}, u32[]{:S(2)}) collective-permute-start(bf16[16,2432]{1,0:T(8,128)(2,1)S(1)} %join.1.refs_2_), channel_id=1, source_target_pairs={{0,1},{1,0},{2,3},{3,2},{4,5},{5,4},{6,7},{7,6},{8,9},{9,8},{10,11... | collective-permute-start | bytes 233480 | tf_op jit(solution)/shard_map/ppermute | solution.py:366
  14.0 2.0 %collective-permute-done.3.refs_3_ = bf16[16,2432]{1,0:T(8,128)(2,1)S(1)} collective-permute-done((bf16[16,2432]{1,0:T(8,128)(2,1)S(1)}, bf16[16,2432]{1,0:T(8,128)(2,1)S(1)}, u32[]{:S(2)}, u32[]{:S(2)}) %collective-permute-start.3) | collective-permute-done | bytes 77856 | tf_op jit(solution)/shard_map/ppermute | solution.py:366
  16.0 0.0 collective-permute-start.7
  16.0 2.7 %scales_y.1 = (bf16[512,256]{1,0:T(8,128)(2,1)S(1)}, f32[2,512,128]{2,1,0:T(8,128)S(1)}, f32[16,16]{1,0:T(8,128)S(1)}, f32[3,512,128]{2,1,0:T(8,128)S(1)}, bf16[...) custom-call(bf16[16,2944]{1,0:T(8,128)(2,1)S(1)} %collective-permute, ...), custom_call_target="tpu_custom_call" | custom-call | tf_op jit(solution)/shard_map/scales_y/pallas_call | solution.py:462
  18.7 0.0 collective-permute-done.4.refs_4_
  18.7 0.0 collective-permute-done.6.refs_6_
  18.7 0.0 collective-permute-done.5.refs_5_
  18.7 0.0 collective-permute-done.7.refs_7_
  18.8 2.4 %layer.1 = (bf16[32,2816]{1,0:T(8,128)(2,1)S(1)}, bf16[16,2816]{1,0:T(8,128)(2,1)S(1)}, bf16[16,2816]{1,0:T(8,128)(2,1)S(1)}) custom-call(f32[16,16]{1,0:T(8,128)S(1)} %get-tuple-element.37.lent_ref, bf16[512,256]{1,0:T(8,128)(2,1)S(1)} %get-tuple-element.38.hot_ref, f32[2,512,128]{2,1,0:T(8,128)S(1)} %get-tuple-element.39.own_radial_ref.radial_ref, ...), custom_call_target="tpu_custom_call" | custom-call | tf_op jit(solution)/shard_map/layer/pallas_call | solution.py:485
  21.1 0.1 collective-permute-start.8
  21.2 0.6 %collective-permute-start.10 = (bf16[32,2816]{1,0:T(8,128)(2,1)S(1)}, bf16[32,2816]{1,0:T(8,128)(2,1)S(1)}, u32[]{:S(2)}, u32[]{:S(2)}) collective-permute-start(bf16[32,2816]{1,0:T(8,128)(2,1)S(1)} %get-tuple-element.56.refs_0_), channel_id=1, source_target_pairs={{0,1},{1,0},{2,3},{3,2},{4,5},{5,4},{6,7},{7,6},{8,9},{9,8},{10,11... | collective-permute-start | bytes 540680 | tf_op jit(solution)/shard_map/ppermute | solution.py:366
  21.8 3.6 %collective-permute-start.9 = (bf16[16,2816]{1,0:T(8,128)(2,1)S(1)}, bf16[16,2816]{1,0:T(8,128)(2,1)S(1)}, u32[]{:S(2)}, u32[]{:S(2)}) collective-permute-start(bf16[16,2816]{1,0:T(8,128)(2,1)S(1)} %get-tuple-element.58), channel_id=1, source_target_pairs={{0,28},{4,8},{8,4},{12,16},{16,12},{20,24},{24,20},{28,0},{1,29},{... | collective-permute-start | bytes 270344 | tf_op jit(solution)/shard_map/ppermute | solution.py:374
  25.3 0.9 %collective-permute-done.8.refs_1_ = bf16[16,2816]{1,0:T(8,128)(2,1)S(1)} collective-permute-done((bf16[16,2816]{1,0:T(8,128)(2,1)S(1)}, bf16[16,2816]{1,0:T(8,128)(2,1)S(1)}, u32[]{:S(2)}, u32[]{:S(2)}) %collective-permute-start.8) | collective-permute-done | bytes 90144 | tf_op jit(solution)/shard_map/ppermute | solution.py:374
  26.2 0.0 collective-permute-start.11
  26.2 2.9 %collective-permute-done.9.refs_2_ = bf16[16,2816]{1,0:T(8,128)(2,1)S(1)} collective-permute-done((bf16[16,2816]{1,0:T(8,128)(2,1)S(1)}, bf16[16,2816]{1,0:T(8,128)(2,1)S(1)}, u32[]{:S(2)}, u32[]{:S(2)}) %collective-permute-start.9) | collective-permute-done | bytes 90144 | tf_op jit(solution)/shard_map/ppermute | solution.py:374
  29.1 0.0 collective-permute-start.12
  29.1 1.7 %fetch.1 = (bf16[640,640]{1,0:T(8,128)(2,1)S(1)}, bf16[512,512]{1,0:T(8,128)(2,1)S(1)}, bf16[512,512]{1,0:T(8,128)(2,1)S(1)}, bf16[384,384]{1,0:T(8,128)(2,1)S(1)}, bf16[384,384]{1,0:T(8,128)(2,1)S(1)}) custom-call(bf16[2,640,640]{2,1,0:T(8,128)(2,1)} %refs_0_.3, bf16[2,512,512]{2,1,0:T(8,128)(2,1)} %refs_1_.3, bf16[2,512,512]{2,1,0:T(8,128)(2,1)} %refs_2_.3, ...), custom_call_target="tpu_custom_call" | custom-call | tf_op jit(solution)/shard_map/fetch/pallas_call | solution.py:499
  30.7 0.0 collective-permute-done.10.refs_3_
  30.8 0.0 collective-permute-done.11.refs_4_
  30.8 0.0 collective-permute-done.12.refs_5_
  30.8 2.4 %last_layer.1 = (bf16[25,16,128]{2,1,0:T(8,128)(2,1)}, f32[3,16]{1,0:T(4,128)}) custom-call(bf16[6,16,128]{2,1,0:T(8,128)(2,1)S(1)} %get-tuple-element.34.rest_ref, f32[16,16]{1,0:T(8,128)S(1)} %get-tuple-element.37.lent_ref, bf16[512,256]{1,0:T(8,128)(2,1)S(1)} %get-tuple-element.38.hot_ref, f32[2,512,128]{2,1,0:T(8,128)S(1)} %get-tuple-element.39.own_radial_ref.radial_ref, ...), custom_call_target="tpu_custom_call" | custom-call | tf_op jit(solution)/shard_map/last_layer/pallas_call | solution.py:511
  (1 shorter events, 0.0 us)
Async XLA Ops:
  1.9 8.9 %collective-permute-start.1 = (bf16[8,2432]{1,0:T(8,128)(2,1)S(1)}, bf16[8,2432]{1,0:T(8,128)(2,1)S(1)}, u32[]{:S(2)}, u32[]{:S(2)}) collective-permute-start(bf16[8,2432]{1,0:T(8,128)(2,1)S(1)} %get-tuple-element.40), channel_id=1, source_target_pairs={{0,4},{4,0},{8,12},{12,8},{16,20},{20,16},{24,28},{28,24},{1,5},{5... | collective-permute-start | bytes 116744 | tf_op jit(solution)/shard_map/ppermute | solution.py:374
  4.9 6.7 %collective-permute-start.2 = (bf16[8,2432]{1,0:T(8,128)(2,1)S(1)}, bf16[8,2432]{1,0:T(8,128)(2,1)S(1)}, u32[]{:S(2)}, u32[]{:S(2)}) collective-permute-start(bf16[8,2432]{1,0:T(8,128)(2,1)S(1)} %get-tuple-element.50), channel_id=1, source_target_pairs={{0,28},{4,8},{8,4},{12,16},{16,12},{20,24},{24,20},{28,0},{1,29},{... | collective-permute-start | bytes 116744 | tf_op jit(solution)/shard_map/ppermute | solution.py:374
  8.5 5.0 %collective-permute-start = (bf16[16,2944]{1,0:T(8,128)(2,1)S(1)}, bf16[16,2944]{1,0:T(8,128)(2,1)S(1)}, u32[]{:S(2)}, u32[]{:S(2)}) collective-permute-start(bf16[16,2944]{1,0:T(8,128)(2,1)S(1)} %get-tuple-element.35.facts_ref.own_ref.refs_0_), channel_id=1, source_target_pairs={{0,2},{1,3},{2,0},{3,1},{4,6},{5,7},{6,4},{7,5},{8,10},{9,11},{10,... | collective-permute-start | bytes 282632 | tf_op jit(solution)/shard_map/ppermute | solution.py:366
  11.6 4.4 %collective-permute-start.3 = (bf16[16,2432]{1,0:T(8,128)(2,1)S(1)}, bf16[16,2432]{1,0:T(8,128)(2,1)S(1)}, u32[]{:S(2)}, u32[]{:S(2)}) collective-permute-start(bf16[16,2432]{1,0:T(8,128)(2,1)S(1)} %join.1.refs_2_), channel_id=1, source_target_pairs={{0,2},{1,3},{2,0},{3,1},{4,6},{5,7},{6,4},{7,5},{8,10},{9,11},{10,... | collective-permute-start | bytes 233480 | tf_op jit(solution)/shard_map/ppermute | solution.py:366
  13.1 5.6 %collective-permute-start.4 = (bf16[16,2944]{1,0:T(8,128)(2,1)S(1)}, bf16[16,2944]{1,0:T(8,128)(2,1)S(1)}, u32[]{:S(2)}, u32[]{:S(2)}) collective-permute-start(bf16[16,2944]{1,0:T(8,128)(2,1)S(1)} %get-tuple-element.35.facts_ref.own_ref.refs_0_), channel_id=1, source_target_pairs={{0,1},{1,0},{2,3},{3,2},{4,5},{5,4},{6,7},{7,6},{8,9},{9,8},{10,11... | collective-permute-start | bytes 282632 | tf_op jit(solution)/shard_map/ppermute | solution.py:366
  13.5 5.2 %collective-permute-start.5 = (bf16[16,2944]{1,0:T(8,128)(2,1)S(1)}, bf16[16,2944]{1,0:T(8,128)(2,1)S(1)}, u32[]{:S(2)}, u32[]{:S(2)}) collective-permute-start(bf16[16,2944]{1,0:T(8,128)(2,1)S(1)} %collective-permute-done.facts_ref.refs_1_), channel_id=1, source_target_pairs={{0,1},{1,0},{2,3},{3,2},{4,5},{5,4},{6,7},{7,6},{8,9},{9,8},{10,11... | collective-permute-start | bytes 282632 | tf_op jit(solution)/shard_map/ppermute | solution.py:366
  13.6 5.1 %collective-permute-start.6 = (bf16[16,2432]{1,0:T(8,128)(2,1)S(1)}, bf16[16,2432]{1,0:T(8,128)(2,1)S(1)}, u32[]{:S(2)}, u32[]{:S(2)}) collective-permute-start(bf16[16,2432]{1,0:T(8,128)(2,1)S(1)} %join.1.refs_2_), channel_id=1, source_target_pairs={{0,1},{1,0},{2,3},{3,2},{4,5},{5,4},{6,7},{7,6},{8,9},{9,8},{10,11... | collective-permute-start | bytes 233480 | tf_op jit(solution)/shard_map/ppermute | solution.py:366
  16.0 2.7 %collective-permute-start.7 = (bf16[16,2432]{1,0:T(8,128)(2,1)S(1)}, bf16[16,2432]{1,0:T(8,128)(2,1)S(1)}, u32[]{:S(2)}, u32[]{:S(2)}) collective-permute-start(bf16[16,2432]{1,0:T(8,128)(2,1)S(1)} %collective-permute-done.3.refs_3_), channel_id=1, source_target_pairs={{0,1},{1,0},{2,3},{3,2},{4,5},{5,4},{6,7},{7,6},{8,9},{9,8},{10,11... | collective-permute-start | bytes 233480 | tf_op jit(solution)/shard_map/ppermute | solution.py:366
  21.1 5.1 %collective-permute-start.8 = (bf16[16,2816]{1,0:T(8,128)(2,1)S(1)}, bf16[16,2816]{1,0:T(8,128)(2,1)S(1)}, u32[]{:S(2)}, u32[]{:S(2)}) collective-permute-start(bf16[16,2816]{1,0:T(8,128)(2,1)S(1)} %get-tuple-element.57), channel_id=1, source_target_pairs={{0,4},{4,0},{8,12},{12,8},{16,20},{20,16},{24,28},{28,24},{1,5},{5... | collective-permute-start | bytes 270344 | tf_op jit(solution)/shard_map/ppermute | solution.py:374
  21.2 9.5 %collective-permute-start.10 = (bf16[32,2816]{1,0:T(8,128)(2,1)S(1)}, bf16[32,2816]{1,0:T(8,128)(2,1)S(1)}, u32[]{:S(2)}, u32[]{:S(2)}) collective-permute-start(bf16[32,2816]{1,0:T(8,128)(2,1)S(1)} %get-tuple-element.56.refs_0_), channel_id=1, source_target_pairs={{0,1},{1,0},{2,3},{3,2},{4,5},{5,4},{6,7},{7,6},{8,9},{9,8},{10,11... | collective-permute-start | bytes 540680 | tf_op jit(solution)/shard_map/ppermute | solution.py:366
  21.8 7.3 %collective-permute-start.9 = (bf16[16,2816]{1,0:T(8,128)(2,1)S(1)}, bf16[16,2816]{1,0:T(8,128)(2,1)S(1)}, u32[]{:S(2)}, u32[]{:S(2)}) collective-permute-start(bf16[16,2816]{1,0:T(8,128)(2,1)S(1)} %get-tuple-element.58), channel_id=1, source_target_pairs={{0,28},{4,8},{8,4},{12,16},{16,12},{20,24},{24,20},{28,0},{1,29},{... | collective-permute-start | bytes 270344 | tf_op jit(solution)/shard_map/ppermute | solution.py:374
  26.2 4.5 %collective-permute-start.11 = (bf16[16,2816]{1,0:T(8,128)(2,1)S(1)}, bf16[16,2816]{1,0:T(8,128)(2,1)S(1)}, u32[]{:S(2)}, u32[]{:S(2)}) collective-permute-start(bf16[16,2816]{1,0:T(8,128)(2,1)S(1)} %collective-permute-done.8.refs_1_), channel_id=1, source_target_pairs={{0,1},{1,0},{2,3},{3,2},{4,5},{5,4},{6,7},{7,6},{8,9},{9,8},{10,11... | collective-permute-start | bytes 270344 | tf_op jit(solution)/shard_map/ppermute | solution.py:366
  29.1 1.7 %collective-permute-start.12 = (bf16[16,2816]{1,0:T(8,128)(2,1)S(1)}, bf16[16,2816]{1,0:T(8,128)(2,1)S(1)}, u32[]{:S(2)}, u32[]{:S(2)}) collective-permute-start(bf16[16,2816]{1,0:T(8,128)(2,1)S(1)} %collective-permute-done.9.refs_2_), channel_id=1, source_target_pairs={{0,1},{1,0},{2,3},{3,2},{4,5},{5,4},{6,7},{7,6},{8,9},{9,8},{10,11... | collective-permute-start | bytes 270344 | tf_op jit(solution)/shard_map/ppermute | solution.py:366

commit v9 on v8

--- a/solution.py
+++ b/solution.py
@@ -185,30 +185,30 @@
 
 
 def own_scale_kernel(
-    atoms, ghosts, slab_devices, facts_ref, rw_ref, hot_ref, radial_ref, lent_ref, flags_ref
-):
-    flags_ref[...], _ = edge_scales(
+    atoms, ghosts, slab_devices,
+    facts_ref, rw_ref, hot_ref, radial_ref, lent_ref, dirs_ref, part_ref,
+):
+    hot, radial = edge_scales(
         atoms, ghosts, slab_devices, facts_ref, rw_ref, hot_ref, radial_ref, lent_ref
     )
+    dirs, part_ref[...] = pull_sums(facts_ref, hot, radial)
+    columns = jnp.transpose(jnp.concatenate([*dirs, *dirs, *dirs[:2]], axis=0))
+    for axis in range(3):
+        dirs_ref[axis] = jnp.broadcast_to(columns[:, axis : axis + 1], dirs_ref.shape[1:])
 
 
 def partner_scale_kernel(
-    atoms, ghosts, slab_devices, count, plan,
-    facts_ref, rw_ref, own_ref, own_radial_ref, flags_ref, *refs,
-):
-    far, (hot_ref, radial_ref, lent_ref, dirs_ref, pulls_ref), refs = (
-        refs[:count], refs[count : count + 5], refs[count + 5 :]
+    atoms, ghosts, slab_devices, count, plan, facts_ref, rw_ref, part_ref, *refs
+):
+    far, (hot_ref, radial_ref, lent_ref, pulls_ref), refs = (
+        refs[:count], refs[count : count + 4], refs[count + 4 :]
     )
     copies = start_fetch(far, refs[:-1], refs[-1], plan)
     hot, radial = edge_scales(
         atoms, ghosts, slab_devices, facts_ref, rw_ref, hot_ref, radial_ref, lent_ref
     )
     _, pulls = pull_sums(facts_ref, hot, radial)
-    dirs, own_pulls = pull_sums(own_ref, flags_ref[...], own_radial_ref[own_radial_ref.shape[0] - 1])
-    pulls_ref[...] = (pulls + own_pulls).astype(BF16)
-    columns = jnp.transpose(jnp.concatenate([*dirs, *dirs, *dirs[:2]], axis=0))
-    for axis in range(3):
-        dirs_ref[axis] = jnp.broadcast_to(columns[:, axis : axis + 1], dirs_ref.shape[1:])
+    pulls_ref[...] = (part_ref[...] + pulls).astype(BF16)
     for copy in copies:
         copy.wait()
 
@@ -441,15 +441,15 @@
     ]
     plans = [[(layer, which) for which in range(count)] for layer in range(layers)]
 
-    hot, radial, lent, flags = pl.pallas_call(
+    hot, radial, lent, dirs, part = pl.pallas_call(
         functools.partial(own_scale_kernel, atoms, ghosts, slab_devices),
-        out_shape=[*side_shapes, held((rows, edges), F32)],
+        out_shape=[*side_shapes, held((3, edges, channels), F32), held((rows, 3 * channels), F32)],
         in_specs=[VMEM] * 2,
-        out_specs=[VMEM] * 4,
+        out_specs=[VMEM] * 5,
         compiler_params=params,
         name="scales",
     )(*near(own, radial_weight))
-    got_pair, flags = lax.optimization_barrier((got_pair, flags))
+    got_pair, part = lax.optimization_barrier((got_pair, part))
     joined = pl.pallas_call(
         join_kernel,
         out_shape=held((2 * ghosts, width), BF16),
@@ -459,18 +459,15 @@
         name="join",
     )(*near(got_pair, got_other))
     joined_y = across(joined, half, slab_devices)
-    hot_y, radial_y, lent_y, dirs, pulls, *now = pl.pallas_call(
+    hot_y, radial_y, lent_y, pulls, *now = pl.pallas_call(
         functools.partial(partner_scale_kernel, atoms, ghosts, slab_devices, count, plans[0]),
-        out_shape=[
-            *side_shapes, held((3, edges, channels), F32), held((rows, 3 * channels), BF16),
-            *near_weights,
-        ],
-        in_specs=[VMEM] * 5 + [far] * count,
-        out_specs=[VMEM] * (5 + count),
+        out_shape=[*side_shapes, held((rows, 3 * channels), BF16), *near_weights],
+        in_specs=[VMEM] * 3 + [far] * count,
+        out_specs=[VMEM] * (4 + count),
         scratch_shapes=[pltpu.SemaphoreType.DMA((count,))],
         compiler_params=params,
         name="scales_y",
-    )(*near(got_own, radial_weight, own, radial, flags), *away(*weights))
+    )(*near(got_own, radial_weight, part), *away(*weights))
     blocks = spread({0: (own, joined), half: (got_own, joined_y)}, bits[1:], slab_devices)
     tables = [
         blocks[slot + upper][kind]

time: 33.4 us -> 32.6 us (0.976)
  waiting for transfers between devices: 6.95 us -> 6.46 us
    pallas_call x1, Pallas kernels: 2.7 us -> 1.88 us  [body(): pl.pallas_call(functools.partial(partner_scale_kernel, atoms, ghosts, sla...]
    pallas_call x1, Pallas kernels: 0.73 us -> 1.22 us  [body(): pl.pallas_call(functools.partial(own_scale_kernel, atoms, ghosts, slab_de...]
    ppermute x4, waiting for transfers between devices: 4.56 us -> 4.07 us  [toward(): return lax.ppermute(block, 'slab', route)]
where the time goes in v9:
time: 32.6 us; the launch traced here: 32.4 us
  starting transfers between devices  14.4 us (44%)
  Pallas kernels  10.8 us (33%)
  waiting for transfers between devices  6.46 us (20%)
  between operations  0.75 us (2%)
    ppermute x4, starting transfers between devices, toward(): return lax.ppermute(block, 'slab', route)  10.2 us
    ppermute x9, starting transfers between devices, across(): lax.ppermute(block, 'yz', [(q, q ^ bit) for q in range(slab_devices)])  4.14 us
    ppermute x4, waiting for transfers between devices, toward(): return lax.ppermute(block, 'slab', route)  4.07 us
    pallas_call x1, Pallas kernels, body(): pl.pallas_call(functools.partial(first_kernel, layer, last, degrees, chan...  2.44 us
    pallas_call x1, Pallas kernels, body(): pl.pallas_call(functools.partial(last_kernel, layer, degrees, channels, a...  2.38 us
    ppermute x9, waiting for transfers between devices, across(): lax.ppermute(block, 'yz', [(q, q ^ bit) for q in range(slab_devices)])  2.38 us
    pallas_call x1, Pallas kernels, body(): pl.pallas_call(functools.partial(partner_scale_kernel, atoms, ghosts, sla...  1.88 us
    pallas_call x1, Pallas kernels, body(): pl.pallas_call(functools.partial(fetch_kernel, count, plans[layer + 1]),...  1.66 us
  transfers between devices with their start and end apart: 13, of which 5 were waited for; matrix products, arithmetic and copies ran while one was open for 0% of the time, Pallas kernels for 15%

profile of v9, /device:TPU:0, one launch (start us, length us, event | category | flops | bytes accessed | tf_op | source)
XLA Modules:
  0.0 32.4 jit_solution(4890067762960682897)
XLA Ops:
  0.6 1.3 %pack.1 = (bf16[16,2944]{1,0:T(8,128)(2,1)S(1)}, bf16[8,2432]{1,0:T(8,128)(2,1)S(1)}, bf16[8,2432]{1,0:T(8,128)(2,1)S(1)}, bf16[6,16,128]{2,1,0:T(8,128)(2,1)S(1...) custom-call(bf16[25,16,128]{2,1,0:T(8,128)(2,1)} %bitcast.10, s32[1,8]{1,0:T(1,128)} %bitcast.16, s32[1,8]{1,0:T(1,128)} %bitcast.17, ...), custom_call_target="tpu_custom_call" | custom-call | tf_op jit(solution)/shard_map/pack/pallas_call | solution.py:416
  1.9 3.0 %collective-permute-start.1 = (bf16[8,2432]{1,0:T(8,128)(2,1)S(1)}, bf16[8,2432]{1,0:T(8,128)(2,1)S(1)}, u32[]{:S(2)}, u32[]{:S(2)}) collective-permute-start(bf16[8,2432]{1,0:T(8,128)(2,1)S(1)} %get-tuple-element.42), channel_id=1, source_target_pairs={{0,4},{4,0},{8,12},{12,8},{16,20},{20,16},{24,28},{28,24},{1,5},{5... | collective-permute-start | bytes 116744 | tf_op jit(solution)/shard_map/ppermute | solution.py:374
  4.9 3.6 %collective-permute-start.2 = (bf16[8,2432]{1,0:T(8,128)(2,1)S(1)}, bf16[8,2432]{1,0:T(8,128)(2,1)S(1)}, u32[]{:S(2)}, u32[]{:S(2)}) collective-permute-start(bf16[8,2432]{1,0:T(8,128)(2,1)S(1)} %get-tuple-element.50), channel_id=1, source_target_pairs={{0,28},{4,8},{8,4},{12,16},{16,12},{20,24},{24,20},{28,0},{1,29},{... | collective-permute-start | bytes 116744 | tf_op jit(solution)/shard_map/ppermute | solution.py:374
  8.5 1.5 %collective-permute-start = (bf16[16,2944]{1,0:T(8,128)(2,1)S(1)}, bf16[16,2944]{1,0:T(8,128)(2,1)S(1)}, u32[]{:S(2)}, u32[]{:S(2)}) collective-permute-start(bf16[16,2944]{1,0:T(8,128)(2,1)S(1)} %get-tuple-element.35.facts_ref.refs_0_), channel_id=1, source_target_pairs={{0,2},{1,3},{2,0},{3,1},{4,6},{5,7},{6,4},{7,5},{8,10},{9,11},{10,... | collective-permute-start | bytes 282632 | tf_op jit(solution)/shard_map/ppermute | solution.py:366
  10.0 1.2 %scales.1 = (bf16[512,256]{1,0:T(8,128)(2,1)S(1)}, f32[2,512,128]{2,1,0:T(8,128)S(1)}, f32[16,16]{1,0:T(8,128)S(1)}, f32[3,512,128]{2,1,0:T(8,128)S(1)}, f32[128,384]{1,0:T(8,128)S(1)}) custom-call(bf16[16,2944]{1,0:T(8,128)(2,1)S(1)} %get-tuple-element.35.facts_ref.refs_0_, f32[2,8,128]{2,1,0:T(8,128)S(1)} %get-tuple-element.36.rw_ref), custom_call_target="tpu_custom_call" | custom-call | tf_op jit(solution)/shard_map/scales/pallas_call | solution.py:444
  11.2 0.0 collective-permute-done.1.pair_ref
  11.3 0.3 %collective-permute-done.2.other_ref = bf16[8,2432]{1,0:T(8,128)(2,1)S(1)} collective-permute-done((bf16[8,2432]{1,0:T(8,128)(2,1)S(1)}, bf16[8,2432]{1,0:T(8,128)(2,1)S(1)}, u32[]{:S(2)}, u32[]{:S(2)}) %collective-permute-start.2) | collective-permute-done | bytes 38944 | tf_op jit(solution)/shard_map/ppermute | solution.py:374
  11.6 1.5 %collective-permute-start.3 = (bf16[16,2432]{1,0:T(8,128)(2,1)S(1)}, bf16[16,2432]{1,0:T(8,128)(2,1)S(1)}, u32[]{:S(2)}, u32[]{:S(2)}) collective-permute-start(bf16[16,2432]{1,0:T(8,128)(2,1)S(1)} %join.1.refs_2_), channel_id=1, source_target_pairs={{0,2},{1,3},{2,0},{3,1},{4,6},{5,7},{6,4},{7,5},{8,10},{9,11},{10,... | collective-permute-start | bytes 233480 | tf_op jit(solution)/shard_map/ppermute | solution.py:366
  13.1 0.0 collective-permute-start.4
  13.1 0.1 collective-permute-done.facts_ref.refs_1_
  13.2 0.4 %collective-permute-start.5 = (bf16[16,2944]{1,0:T(8,128)(2,1)S(1)}, bf16[16,2944]{1,0:T(8,128)(2,1)S(1)}, u32[]{:S(2)}, u32[]{:S(2)}) collective-permute-start(bf16[16,2944]{1,0:T(8,128)(2,1)S(1)} %collective-permute-done.facts_ref.refs_1_), channel_id=1, source_target_pairs={{0,1},{1,0},{2,3},{3,2},{4,5},{5,4},{6,7},{7,6},{8,9},{9,8},{10,11... | collective-permute-start | bytes 282632 | tf_op jit(solution)/shard_map/ppermute | solution.py:366
  13.6 0.1 collective-permute-start.6
  13.7 2.3 %collective-permute-done.3.refs_3_ = bf16[16,2432]{1,0:T(8,128)(2,1)S(1)} collective-permute-done((bf16[16,2432]{1,0:T(8,128)(2,1)S(1)}, bf16[16,2432]{1,0:T(8,128)(2,1)S(1)}, u32[]{:S(2)}, u32[]{:S(2)}) %collective-permute-start.3) | collective-permute-done | bytes 77856 | tf_op jit(solution)/shard_map/ppermute | solution.py:366
  16.0 0.0 collective-permute-start.7
  16.0 1.9 %scales_y.1 = (bf16[512,256]{1,0:T(8,128)(2,1)S(1)}, f32[2,512,128]{2,1,0:T(8,128)S(1)}, f32[16,16]{1,0:T(8,128)S(1)}, bf16[128,384]{1,0:T(8,128)(2,1)S(1)}, bf1...) custom-call(bf16[16,2944]{1,0:T(8,128)(2,1)S(1)} %collective-permute, ...), custom_call_target="tpu_custom_call" | custom-call | tf_op jit(solution)/shard_map/scales_y/pallas_call | solution.py:462
  17.9 0.0 collective-permute-done.4.refs_4_
  17.9 0.0 collective-permute-done.6.refs_6_
  17.9 0.0 collective-permute-done.5.refs_5_
  17.9 0.0 collective-permute-done.7.refs_7_
  17.9 2.4 %layer.1 = (bf16[32,2816]{1,0:T(8,128)(2,1)S(1)}, bf16[16,2816]{1,0:T(8,128)(2,1)S(1)}, bf16[16,2816]{1,0:T(8,128)(2,1)S(1)}) custom-call(f32[16,16]{1,0:T(8,128)S(1)} %get-tuple-element.37.lent_ref, bf16[512,256]{1,0:T(8,128)(2,1)S(1)} %get-tuple-element.38.hot_ref, f32[2,512,128]{2,1,0:T(8,128)S(1)} %get-tuple-element.39.radial_ref, ...), custom_call_target="tpu_custom_call" | custom-call | tf_op jit(solution)/shard_map/layer/pallas_call | solution.py:482
  20.4 0.1 collective-permute-start.8
  20.4 0.6 %collective-permute-start.10 = (bf16[32,2816]{1,0:T(8,128)(2,1)S(1)}, bf16[32,2816]{1,0:T(8,128)(2,1)S(1)}, u32[]{:S(2)}, u32[]{:S(2)}) collective-permute-start(bf16[32,2816]{1,0:T(8,128)(2,1)S(1)} %get-tuple-element.56.refs_0_), channel_id=1, source_target_pairs={{0,1},{1,0},{2,3},{3,2},{4,5},{5,4},{6,7},{7,6},{8,9},{9,8},{10,11... | collective-permute-start | bytes 540680 | tf_op jit(solution)/shard_map/ppermute | solution.py:366
  21.0 3.6 %collective-permute-start.9 = (bf16[16,2816]{1,0:T(8,128)(2,1)S(1)}, bf16[16,2816]{1,0:T(8,128)(2,1)S(1)}, u32[]{:S(2)}, u32[]{:S(2)}) collective-permute-start(bf16[16,2816]{1,0:T(8,128)(2,1)S(1)} %get-tuple-element.58), channel_id=1, source_target_pairs={{0,28},{4,8},{8,4},{12,16},{16,12},{20,24},{24,20},{28,0},{1,29},{... | collective-permute-start | bytes 270344 | tf_op jit(solution)/shard_map/ppermute | solution.py:374
  24.6 0.9 %collective-permute-done.8.refs_1_ = bf16[16,2816]{1,0:T(8,128)(2,1)S(1)} collective-permute-done((bf16[16,2816]{1,0:T(8,128)(2,1)S(1)}, bf16[16,2816]{1,0:T(8,128)(2,1)S(1)}, u32[]{:S(2)}, u32[]{:S(2)}) %collective-permute-start.8) | collective-permute-done | bytes 90144 | tf_op jit(solution)/shard_map/ppermute | solution.py:374
  25.4 0.0 collective-permute-start.11
  25.5 2.9 %collective-permute-done.9.refs_2_ = bf16[16,2816]{1,0:T(8,128)(2,1)S(1)} collective-permute-done((bf16[16,2816]{1,0:T(8,128)(2,1)S(1)}, bf16[16,2816]{1,0:T(8,128)(2,1)S(1)}, u32[]{:S(2)}, u32[]{:S(2)}) %collective-permute-start.9) | collective-permute-done | bytes 90144 | tf_op jit(solution)/shard_map/ppermute | solution.py:374
  28.3 0.0 collective-permute-start.12
  28.3 1.7 %fetch.1 = (bf16[640,640]{1,0:T(8,128)(2,1)S(1)}, bf16[512,512]{1,0:T(8,128)(2,1)S(1)}, bf16[512,512]{1,0:T(8,128)(2,1)S(1)}, bf16[384,384]{1,0:T(8,128)(2,1)S(1)}, bf16[384,384]{1,0:T(8,128)(2,1)S(1)}) custom-call(bf16[2,640,640]{2,1,0:T(8,128)(2,1)} %refs_0_.3, bf16[2,512,512]{2,1,0:T(8,128)(2,1)} %refs_1_.3, bf16[2,512,512]{2,1,0:T(8,128)(2,1)} %refs_2_.3, ...), custom_call_target="tpu_custom_call" | custom-call | tf_op jit(solution)/shard_map/fetch/pallas_call | solution.py:496
  30.0 0.0 collective-permute-done.10.refs_3_
  30.0 0.0 collective-permute-done.11.refs_4_
  30.0 0.0 collective-permute-done.12.refs_5_
  30.0 2.4 %last_layer.1 = (bf16[25,16,128]{2,1,0:T(8,128)(2,1)}, f32[3,16]{1,0:T(4,128)}) custom-call(bf16[6,16,128]{2,1,0:T(8,128)(2,1)S(1)} %get-tuple-element.34.rest_ref, f32[16,16]{1,0:T(8,128)S(1)} %get-tuple-element.37.lent_ref, bf16[512,256]{1,0:T(8,128)(2,1)S(1)} %get-tuple-element.38.hot_ref, f32[2,512,128]{2,1,0:T(8,128)S(1)} %get-tuple-element.39.radial_ref, ...), custom_call_target="tpu_custom_call" | custom-call | tf_op jit(solution)/shard_map/last_layer/pallas_call | solution.py:508
  (1 shorter events, 0.0 us)
Async XLA Ops:
  1.9 9.4 %collective-permute-start.1 = (bf16[8,2432]{1,0:T(8,128)(2,1)S(1)}, bf16[8,2432]{1,0:T(8,128)(2,1)S(1)}, u32[]{:S(2)}, u32[]{:S(2)}) collective-permute-start(bf16[8,2432]{1,0:T(8,128)(2,1)S(1)} %get-tuple-element.42), channel_id=1, source_target_pairs={{0,4},{4,0},{8,12},{12,8},{16,20},{20,16},{24,28},{28,24},{1,5},{5... | collective-permute-start | bytes 116744 | tf_op jit(solution)/shard_map/ppermute | solution.py:374
  4.9 6.7 %collective-permute-start.2 = (bf16[8,2432]{1,0:T(8,128)(2,1)S(1)}, bf16[8,2432]{1,0:T(8,128)(2,1)S(1)}, u32[]{:S(2)}, u32[]{:S(2)}) collective-permute-start(bf16[8,2432]{1,0:T(8,128)(2,1)S(1)} %get-tuple-element.50), channel_id=1, source_target_pairs={{0,28},{4,8},{8,4},{12,16},{16,12},{20,24},{24,20},{28,0},{1,29},{... | collective-permute-start | bytes 116744 | tf_op jit(solution)/shard_map/ppermute | solution.py:374
  8.5 4.7 %collective-permute-start = (bf16[16,2944]{1,0:T(8,128)(2,1)S(1)}, bf16[16,2944]{1,0:T(8,128)(2,1)S(1)}, u32[]{:S(2)}, u32[]{:S(2)}) collective-permute-start(bf16[16,2944]{1,0:T(8,128)(2,1)S(1)} %get-tuple-element.35.facts_ref.refs_0_), channel_id=1, source_target_pairs={{0,2},{1,3},{2,0},{3,1},{4,6},{5,7},{6,4},{7,5},{8,10},{9,11},{10,... | collective-permute-start | bytes 282632 | tf_op jit(solution)/shard_map/ppermute | solution.py:366
  11.6 4.4 %collective-permute-start.3 = (bf16[16,2432]{1,0:T(8,128)(2,1)S(1)}, bf16[16,2432]{1,0:T(8,128)(2,1)S(1)}, u32[]{:S(2)}, u32[]{:S(2)}) collective-permute-start(bf16[16,2432]{1,0:T(8,128)(2,1)S(1)} %join.1.refs_2_), channel_id=1, source_target_pairs={{0,2},{1,3},{2,0},{3,1},{4,6},{5,7},{6,4},{7,5},{8,10},{9,11},{10,... | collective-permute-start | bytes 233480 | tf_op jit(solution)/shard_map/ppermute | solution.py:366
  13.1 4.8 %collective-permute-start.4 = (bf16[16,2944]{1,0:T(8,128)(2,1)S(1)}, bf16[16,2944]{1,0:T(8,128)(2,1)S(1)}, u32[]{:S(2)}, u32[]{:S(2)}) collective-permute-start(bf16[16,2944]{1,0:T(8,128)(2,1)S(1)} %get-tuple-element.35.facts_ref.refs_0_), channel_id=1, source_target_pairs={{0,1},{1,0},{2,3},{3,2},{4,5},{5,4},{6,7},{7,6},{8,9},{9,8},{10,11... | collective-permute-start | bytes 282632 | tf_op jit(solution)/shard_map/ppermute | solution.py:366
  13.2 4.7 %collective-permute-start.5 = (bf16[16,2944]{1,0:T(8,128)(2,1)S(1)}, bf16[16,2944]{1,0:T(8,128)(2,1)S(1)}, u32[]{:S(2)}, u32[]{:S(2)}) collective-permute-start(bf16[16,2944]{1,0:T(8,128)(2,1)S(1)} %collective-permute-done.facts_ref.refs_1_), channel_id=1, source_target_pairs={{0,1},{1,0},{2,3},{3,2},{4,5},{5,4},{6,7},{7,6},{8,9},{9,8},{10,11... | collective-permute-start | bytes 282632 | tf_op jit(solution)/shard_map/ppermute | solution.py:366
  13.6 4.3 %collective-permute-start.6 = (bf16[16,2432]{1,0:T(8,128)(2,1)S(1)}, bf16[16,2432]{1,0:T(8,128)(2,1)S(1)}, u32[]{:S(2)}, u32[]{:S(2)}) collective-permute-start(bf16[16,2432]{1,0:T(8,128)(2,1)S(1)} %join.1.refs_2_), channel_id=1, source_target_pairs={{0,1},{1,0},{2,3},{3,2},{4,5},{5,4},{6,7},{7,6},{8,9},{9,8},{10,11... | collective-permute-start | bytes 233480 | tf_op jit(solution)/shard_map/ppermute | solution.py:366
  16.0 1.9 %collective-permute-start.7 = (bf16[16,2432]{1,0:T(8,128)(2,1)S(1)}, bf16[16,2432]{1,0:T(8,128)(2,1)S(1)}, u32[]{:S(2)}, u32[]{:S(2)}) collective-permute-start(bf16[16,2432]{1,0:T(8,128)(2,1)S(1)} %collective-permute-done.3.refs_3_), channel_id=1, source_target_pairs={{0,1},{1,0},{2,3},{3,2},{4,5},{5,4},{6,7},{7,6},{8,9},{9,8},{10,11... | collective-permute-start | bytes 233480 | tf_op jit(solution)/shard_map/ppermute | solution.py:366
  20.4 5.1 %collective-permute-start.8 = (bf16[16,2816]{1,0:T(8,128)(2,1)S(1)}, bf16[16,2816]{1,0:T(8,128)(2,1)S(1)}, u32[]{:S(2)}, u32[]{:S(2)}) collective-permute-start(bf16[16,2816]{1,0:T(8,128)(2,1)S(1)} %get-tuple-element.57), channel_id=1, source_target_pairs={{0,4},{4,0},{8,12},{12,8},{16,20},{20,16},{24,28},{28,24},{1,5},{5... | collective-permute-start | bytes 270344 | tf_op jit(solution)/shard_map/ppermute | solution.py:374
  20.4 9.5 %collective-permute-start.10 = (bf16[32,2816]{1,0:T(8,128)(2,1)S(1)}, bf16[32,2816]{1,0:T(8,128)(2,1)S(1)}, u32[]{:S(2)}, u32[]{:S(2)}) collective-permute-start(bf16[32,2816]{1,0:T(8,128)(2,1)S(1)} %get-tuple-element.56.refs_0_), channel_id=1, source_target_pairs={{0,1},{1,0},{2,3},{3,2},{4,5},{5,4},{6,7},{7,6},{8,9},{9,8},{10,11... | collective-permute-start | bytes 540680 | tf_op jit(solution)/shard_map/ppermute | solution.py:366
  21.0 7.3 %collective-permute-start.9 = (bf16[16,2816]{1,0:T(8,128)(2,1)S(1)}, bf16[16,2816]{1,0:T(8,128)(2,1)S(1)}, u32[]{:S(2)}, u32[]{:S(2)}) collective-permute-start(bf16[16,2816]{1,0:T(8,128)(2,1)S(1)} %get-tuple-element.58), channel_id=1, source_target_pairs={{0,28},{4,8},{8,4},{12,16},{16,12},{20,24},{24,20},{28,0},{1,29},{... | collective-permute-start | bytes 270344 | tf_op jit(solution)/shard_map/ppermute | solution.py:374
  25.4 4.5 %collective-permute-start.11 = (bf16[16,2816]{1,0:T(8,128)(2,1)S(1)}, bf16[16,2816]{1,0:T(8,128)(2,1)S(1)}, u32[]{:S(2)}, u32[]{:S(2)}) collective-permute-start(bf16[16,2816]{1,0:T(8,128)(2,1)S(1)} %collective-permute-done.8.refs_1_), channel_id=1, source_target_pairs={{0,1},{1,0},{2,3},{3,2},{4,5},{5,4},{6,7},{7,6},{8,9},{9,8},{10,11... | collective-permute-start | bytes 270344 | tf_op jit(solution)/shard_map/ppermute | solution.py:366
  28.3 1.7 %collective-permute-start.12 = (bf16[16,2816]{1,0:T(8,128)(2,1)S(1)}, bf16[16,2816]{1,0:T(8,128)(2,1)S(1)}, u32[]{:S(2)}, u32[]{:S(2)}) collective-permute-start(bf16[16,2816]{1,0:T(8,128)(2,1)S(1)} %collective-permute-done.9.refs_2_), channel_id=1, source_target_pairs={{0,1},{1,0},{2,3},{3,2},{4,5},{5,4},{6,7},{7,6},{8,9},{9,8},{10,11... | collective-permute-start | bytes 270344 | tf_op jit(solution)/shard_map/ppermute | solution.py:366
